TPU v7x, 32 devices: a whole 2x2x4 slice. The times are simulated.
32 devices in a mesh: dp: 8 (over y, x, core), tensor: 4 (over z).
Axes of the slice: x: 2, y: 2, z: 4, core: 2. Of those that a mesh axis runs over, the one named last changes fastest.
Arguments:
- layer_input: bfloat16 [4096, 2048], P(('dp', 'tensor')), may hold values from -6 to 6
- segment_ids: int32 [4096], P('dp'), may hold values from 0 to 15, as said below
- norm_attn: bfloat16 [2048], P('dp'), may hold values from 0.5 to 1.5
- w_query: bfloat16 [2048, 2048], P('dp', 'tensor')
- w_key: bfloat16 [2048, 256], P('dp', 'tensor')
- w_value: bfloat16 [2048, 256], P('dp', 'tensor'), may hold values from -0.125 to 0.125
- w_output: bfloat16 [2048, 2048], P('tensor', 'dp'), may hold values from -0.5 to 0.5
- norm_ffn: bfloat16 [2048], P('dp'), may hold values from 0.5 to 1.5
- w_gate: bfloat16 [2048, 5632], P('dp', 'tensor'), may hold values from -0.125 to 0.125
- w_up: bfloat16 [2048, 5632], P('dp', 'tensor'), may hold values from -0.125 to 0.125
- w_down: bfloat16 [5632, 2048], P('tensor', 'dp'), may hold values from -0.078125 to 0.078125
- cotangent: bfloat16 [4096, 2048], P(('dp', 'tensor')), may hold values from -6 to 6
Outputs:
- layer_output: bfloat16 [4096, 2048], P(('dp', 'tensor'))
- grad_input: float32 [4096, 2048], P(('dp', 'tensor'))
- grad_norm_attn: float32 [2048], P('dp')
- grad_w_query: float32 [2048, 2048], P('dp', 'tensor')
- grad_w_key: float32 [2048, 256], P('dp', 'tensor')
- grad_w_value: float32 [2048, 256], P('dp', 'tensor')
- grad_w_output: float32 [2048, 2048], P('tensor', 'dp')
- grad_norm_ffn: float32 [2048], P('dp')
- grad_w_gate: float32 [2048, 5632], P('dp', 'tensor')
- grad_w_up: float32 [2048, 5632], P('dp', 'tensor')
- grad_w_down: float32 [5632, 2048], P('tensor', 'dp')
Inputs may be any that keep to these rules, and one draw needn't show every extreme that they name: `segment_ids`: within each aligned block of 512 rows the ids start at 0, never fall and rise by one at each new sequence, so that a block holds 1 to 16 sequences; in every draw some block is a single sequence of 512 rows and some block holds 16.
All inputs are finite; a program needn't handle non-finite values.
Results may differ from a plain program's by a relative error of at most 0.014.
Values may be sent and summed in bfloat16 or wider, within the bound.
A program may use at most 192 MiB of HBM per device.

v0:
```python
import math

import jax
import jax.numpy as jnp
from jax import lax
from jax.sharding import PartitionSpec as P

HD = 64


EPSILON = 1e-05
NEGATIVE = -1e30


def rope_tables(segments, head_dim):
    row_count = segments.shape[0]
    row_index = jnp.arange(row_count, dtype=jnp.int32)
    change = jnp.concatenate(
        [jnp.ones((1,), jnp.int32), (segments[1:] != segments[:-1]).astype(jnp.int32)]
    )
    starts = lax.cummax(jnp.where(change > 0, row_index, jnp.zeros_like(row_index)), axis=0)
    position = (row_index - starts).astype(jnp.float32)
    half_dim = head_dim // 2
    frequency = jnp.exp(jnp.arange(half_dim, dtype=jnp.float32) * (-math.log(10000.0) / half_dim))
    angles = position[:, None] * frequency[None, :]
    return (jnp.cos(angles)[:, None, :], jnp.sin(angles)[:, None, :])


def rotate(tensor, cosine, sine):
    half_dim = tensor.shape[-1] // 2
    first_half = tensor[..., :half_dim]
    second_half = tensor[..., half_dim:]
    return jnp.concatenate(
        [first_half * cosine - second_half * sine, second_half * cosine + first_half * sine],
        axis=-1,
    )


def unrotate(tensor, cosine, sine):
    half_dim = tensor.shape[-1] // 2
    first_half = tensor[..., :half_dim]
    second_half = tensor[..., half_dim:]
    return jnp.concatenate(
        [first_half * cosine + second_half * sine, second_half * cosine - first_half * sine],
        axis=-1,
    )


def visible(segments):
    row_index = jnp.arange(segments.shape[0], dtype=jnp.int32)
    same_seq = segments[:, None] == segments[None, :]
    return same_seq & (row_index[:, None] >= row_index[None, :])


def normalize(values, gain):
    inverse = lax.rsqrt(jnp.mean(values * values, axis=-1, keepdims=True) + EPSILON)
    unit_rows = values * inverse
    return (unit_rows, inverse, (unit_rows * gain.astype(jnp.float32)).astype(jnp.bfloat16))


def normalize_back(grad_normed, unit_rows, inverse, gain):
    scaled = grad_normed * gain.astype(jnp.float32)
    grad_values = inverse * (
        scaled - unit_rows * jnp.mean(scaled * unit_rows, axis=-1, keepdims=True)
    )
    return (grad_values, jnp.sum(grad_normed * unit_rows, axis=0))


def contract(left, right, left_dim, right_dim):
    return lax.dot_general(
        left, right, (((left_dim,), (right_dim,)), ((), ())), preferred_element_type=jnp.float32
    )


def block_scores(query_block, key_heads, allowed_block, score_scale):
    scores = (
        jnp.einsum("rkgd,skd->kgrs", query_block, key_heads, preferred_element_type=jnp.float32)
        * score_scale
    )
    return jnp.where(allowed_block[None, None], scores, NEGATIVE)


def attend_forward(query_groups, key_heads, value_heads, allowed, score_scale):
    scores = block_scores(query_groups, key_heads, allowed, score_scale)
    row_max = jnp.max(scores, axis=-1, keepdims=True)
    log_total = row_max + jnp.log(jnp.sum(jnp.exp(scores - row_max), axis=-1, keepdims=True))
    probs_low = jnp.exp(scores - log_total).astype(jnp.bfloat16)
    mixed_parts = jnp.einsum(
        "kgrs,skd->rkgd", probs_low, value_heads, preferred_element_type=jnp.float32
    ).astype(jnp.bfloat16)
    return (mixed_parts, log_total)


def attend_backward(
    query_groups, key_heads, value_heads, mixed_heads, grad_mixed, log_totals, allowed, score_scale
):
    scores = block_scores(query_groups, key_heads, allowed, score_scale)
    attn_probs = jnp.exp(scores - log_totals)
    probs_low = attn_probs.astype(jnp.bfloat16)
    grad_probs = jnp.einsum(
        "rkgd,skd->kgrs", grad_mixed, value_heads, preferred_element_type=jnp.float32
    )
    row_delta = jnp.sum(grad_mixed.astype(jnp.float32) * mixed_heads.astype(jnp.float32), axis=-1)
    row_delta = jnp.transpose(row_delta, (1, 2, 0))[..., None]
    grad_scores = (attn_probs * (grad_probs - row_delta)).astype(jnp.bfloat16)
    query_parts = (
        jnp.einsum("kgrs,skd->rkgd", grad_scores, key_heads, preferred_element_type=jnp.float32)
        * score_scale
    )
    grad_key_rot = (
        jnp.einsum("kgrs,rkgd->skd", grad_scores, query_groups, preferred_element_type=jnp.float32)
        * score_scale
    )
    grad_value_heads = jnp.einsum(
        "kgrs,rkgd->skd", probs_low, grad_mixed, preferred_element_type=jnp.float32
    )
    return (query_parts, grad_key_rot, grad_value_heads)


def on_device(
    layer_input,
    segment_ids,
    norm_attn,
    w_query,
    w_key,
    w_value,
    w_output,
    norm_ffn,
    w_gate,
    w_up,
    w_down,
    cotangent,
):
    score_scale = HD ** (-0.5)
    query_full, key_full, value_full, output_full, gain_attn = (
        lax.all_gather(w_query, "dp", axis=0, tiled=True),
        lax.all_gather(w_key, "dp", axis=0, tiled=True),
        lax.all_gather(w_value, "dp", axis=0, tiled=True),
        lax.all_gather(w_output, "dp", axis=1, tiled=True),
        lax.all_gather(norm_attn, "dp", axis=0, tiled=True),
    )
    gate_full, up_full, down_full, gain_ffn = (
        lax.all_gather(w_gate, "dp", axis=0, tiled=True),
        lax.all_gather(w_up, "dp", axis=0, tiled=True),
        lax.all_gather(w_down, "dp", axis=1, tiled=True),
        lax.all_gather(norm_ffn, "dp", axis=0, tiled=True),
    )
    heads_local = query_full.shape[1] // HD
    kv_local = key_full.shape[1] // HD
    group = heads_local // kv_local
    residual_in = layer_input.astype(jnp.float32)
    unit_attn, inverse_attn, normed_local = normalize(residual_in, gain_attn)
    normed_attn = lax.all_gather(normed_local, "tensor", axis=0, tiled=True)
    row_count = normed_attn.shape[0]
    cosine, sine = rope_tables(segment_ids, HD)
    allowed = visible(segment_ids)
    query_heads = rotate(
        jnp.dot(normed_attn, query_full, preferred_element_type=jnp.float32).reshape(
            row_count, heads_local, HD
        ),
        cosine,
        sine,
    ).astype(jnp.bfloat16)
    query_groups = query_heads.reshape(row_count, kv_local, group, HD)
    key_heads = rotate(
        jnp.dot(normed_attn, key_full, preferred_element_type=jnp.float32).reshape(
            row_count, kv_local, HD
        ),
        cosine,
        sine,
    ).astype(jnp.bfloat16)
    value_heads = (
        jnp.dot(normed_attn, value_full, preferred_element_type=jnp.float32)
        .astype(jnp.bfloat16)
        .reshape(row_count, kv_local, HD)
    )
    mixed_heads, log_totals = attend_forward(
        query_groups, key_heads, value_heads, allowed, score_scale
    )
    mixed_flat = mixed_heads.reshape(row_count, heads_local * HD)
    hidden_res = residual_in + lax.psum_scatter(
        jnp.dot(mixed_flat, output_full, preferred_element_type=jnp.float32),
        "tensor",
        scatter_dimension=0,
        tiled=True,
    )
    unit_ffn, inverse_ffn, normed_ffn_local = normalize(hidden_res, gain_ffn)
    normed_ffn = lax.all_gather(normed_ffn_local, "tensor", axis=0, tiled=True)
    gate_rows = jnp.dot(normed_ffn, gate_full, preferred_element_type=jnp.float32)
    up_rows = jnp.dot(normed_ffn, up_full, preferred_element_type=jnp.float32)
    sigmoid_gate = jax.nn.sigmoid(gate_rows)
    active = (gate_rows * sigmoid_gate * up_rows).astype(jnp.bfloat16)
    layer_output = (
        hidden_res
        + lax.psum_scatter(
            jnp.dot(active, down_full, preferred_element_type=jnp.float32).astype(jnp.bfloat16),
            "tensor",
            scatter_dimension=0,
            tiled=True,
        ).astype(jnp.float32)
    ).astype(jnp.bfloat16)
    query_full, key_full, value_full, output_full, gate_full, up_full, down_full = (
        lax.all_gather(w_query, "dp", axis=0, tiled=True),
        lax.all_gather(w_key, "dp", axis=0, tiled=True),
        lax.all_gather(w_value, "dp", axis=0, tiled=True),
        lax.all_gather(w_output, "dp", axis=1, tiled=True),
        lax.all_gather(w_gate, "dp", axis=0, tiled=True),
        lax.all_gather(w_up, "dp", axis=0, tiled=True),
        lax.all_gather(w_down, "dp", axis=1, tiled=True),
    )
    cotangent_full = lax.all_gather(cotangent, "tensor", axis=0, tiled=True)
    grad_active = contract(cotangent_full, down_full, 1, 1)
    grad_w_down = contract(active, cotangent_full, 0, 0)
    grad_up_rows = (grad_active * gate_rows * sigmoid_gate).astype(jnp.bfloat16)
    grad_gate_rows = (
        grad_active * up_rows * sigmoid_gate * (1.0 + gate_rows * (1.0 - sigmoid_gate))
    ).astype(jnp.bfloat16)
    grad_w_gate = contract(normed_ffn, grad_gate_rows, 0, 0)
    grad_w_up = contract(normed_ffn, grad_up_rows, 0, 0)
    grad_normed_ffn = lax.psum_scatter(
        contract(grad_gate_rows, gate_full, 1, 1) + contract(grad_up_rows, up_full, 1, 1),
        "tensor",
        scatter_dimension=0,
        tiled=True,
    )
    grad_hidden, gain_ffn_part = normalize_back(grad_normed_ffn, unit_ffn, inverse_ffn, gain_ffn)
    grad_hidden = cotangent.astype(jnp.float32) + grad_hidden
    branch_full = lax.all_gather(grad_hidden.astype(jnp.bfloat16), "tensor", axis=0, tiled=True)
    grad_mixed = contract(branch_full, output_full, 1, 1).astype(jnp.bfloat16)
    grad_w_output = contract(mixed_flat, branch_full, 0, 0)
    grad_query_rot, grad_key_rot, grad_value_heads = attend_backward(
        query_groups,
        key_heads,
        value_heads,
        mixed_heads,
        grad_mixed.reshape(row_count, kv_local, group, HD),
        log_totals,
        allowed,
        score_scale,
    )
    grad_queries = (
        unrotate(grad_query_rot.reshape(row_count, heads_local, HD), cosine, sine)
        .reshape(row_count, heads_local * HD)
        .astype(jnp.bfloat16)
    )
    grad_keys = (
        unrotate(grad_key_rot, cosine, sine).reshape(row_count, kv_local * HD).astype(jnp.bfloat16)
    )
    grad_values = grad_value_heads.reshape(row_count, kv_local * HD).astype(jnp.bfloat16)
    grad_w_query = contract(normed_attn, grad_queries, 0, 0)
    grad_w_key = contract(normed_attn, grad_keys, 0, 0)
    grad_w_value = contract(normed_attn, grad_values, 0, 0)
    grad_normed_attn = lax.psum_scatter(
        contract(grad_queries, query_full, 1, 1)
        + contract(grad_keys, key_full, 1, 1)
        + contract(grad_values, value_full, 1, 1),
        "tensor",
        scatter_dimension=0,
        tiled=True,
    )
    grad_residual, gain_attn_part = normalize_back(
        grad_normed_attn, unit_attn, inverse_attn, gain_attn
    )
    grad_input = grad_hidden + grad_residual
    gain_attn_total, gain_ffn_total = lax.psum((gain_attn_part, gain_ffn_part), "tensor")
    owned = (
        lax.psum_scatter(grad_w_query, "dp", scatter_dimension=0, tiled=True),
        lax.psum_scatter(grad_w_key, "dp", scatter_dimension=0, tiled=True),
        lax.psum_scatter(grad_w_value, "dp", scatter_dimension=0, tiled=True),
        lax.psum_scatter(grad_w_output, "dp", scatter_dimension=1, tiled=True),
        lax.psum_scatter(gain_attn_total, "dp", scatter_dimension=0, tiled=True),
        lax.psum_scatter(gain_ffn_total, "dp", scatter_dimension=0, tiled=True),
        lax.psum_scatter(grad_w_gate, "dp", scatter_dimension=0, tiled=True),
        lax.psum_scatter(grad_w_up, "dp", scatter_dimension=0, tiled=True),
        lax.psum_scatter(grad_w_down, "dp", scatter_dimension=1, tiled=True),
    )
    return (
        layer_output,
        grad_input,
        owned[4],
        owned[0],
        owned[1],
        owned[2],
        owned[3],
        owned[5],
        owned[6],
        owned[7],
        owned[8],
    )


def solution(mesh):
    placed = (
        P(("dp", "tensor"), None),
        P("dp"),
        P("dp"),
        P("dp", "tensor"),
        P("dp", "tensor"),
        P("dp", "tensor"),
        P("tensor", "dp"),
        P("dp"),
        P("dp", "tensor"),
        P("dp", "tensor"),
        P("tensor", "dp"),
        P(("dp", "tensor"), None),
    )
    return jax.shard_map(
        on_device,
        mesh=mesh,
        in_specs=placed,
        out_specs=(
            P(("dp", "tensor"), None),
            P(("dp", "tensor"), None),
            P("dp"),
            P("dp", "tensor"),
            P("dp", "tensor"),
            P("dp", "tensor"),
            P("tensor", "dp"),
            P("dp"),
            P("dp", "tensor"),
            P("dp", "tensor"),
            P("tensor", "dp"),
        ),
        check_vma=False,
    )
```

profile of v0, /device:TPU:0, one launch (start us, length us, event | category | flops | bytes accessed | tf_op | source)
XLA Modules:
  0.0 1196.2 jit_solution(9461690144520946599)
XLA Ops:
  7.9 10.4 all-gather
  24.7 9.8 all_gather.49
  34.5 9.1 all_gather.48
  44.1 23.6 %all-gather.12.cloned.1.call-done = bf16[512,2048]{1,0:T(8,128)(2,1)} async-done(((bf16[128,2048]{1,0:T(8,128)(2,1)}), bf16[512,2048]{1,0:T(8,128)(2,1)}) %all-gather.12.cloned.1.call-update) | async-done | bytes 2097168 | tf_op jit(solution)/shard_map/all_gather | solution.py:153
  73.6 22.6 %all-gather.14.cloned.1.call-done = bf16[2048,512]{1,0:T(8,128)(2,1)} async-done(((bf16[256,512]{1,0:T(8,128)(2,1)}), bf16[2048,512]{1,0:T(8,128)(2,1)}) %all-gather.14.cloned.1.call-update) | async-done | bytes 2097168 | tf_op jit(solution)/shard_map/all_gather | solution.py:136
  106.5 19.8 %all-gather.16.cloned.1.call-done = bf16[512,2048]{1,0:T(8,128)(2,1)} async-done(((bf16[512,256]{1,0:T(8,128)(2,1)}), bf16[512,2048]{1,0:T(8,128)(2,1)}) %all-gather.16.cloned.1.call-update) | async-done | bytes 2097168 | tf_op jit(solution)/shard_map/all_gather | solution.py:139
  131.9 9.3 all-gather.1
  141.2 66.9 %reduce-scatter.12.cloned.1.call-done = f32[128,2048]{1,0:T(8,128)} async-done(((f32[512,2048]{1,0:T(8,128)}), f32[128,2048]{1,0:T(8,128)}) %reduce-scatter.12.cloned.1.call-update) | async-done | bytes 1048592 | tf_op jit(solution)/shard_map/reduce_scatter | solution.py:181
  213.5 40.0 %all-gather.20.cloned.1.call-done = bf16[2048,1408]{1,0:T(8,128)(2,1)} async-done(((bf16[256,1408]{1,0:T(8,128)(2,1)}), bf16[2048,1408]{1,0:T(8,128)(2,1)}) %all-gather.20.cloned.1.call-update) | async-done | bytes 5767184 | tf_op jit(solution)/shard_map/all_gather | solution.py:143
  253.6 47.7 %all-gather.18.cloned.1.call-done = bf16[512,2048]{1,0:T(8,128)(2,1)} async-done(((bf16[128,2048]{1,0:T(8,128)(2,1)}), bf16[512,2048]{1,0:T(8,128)(2,1)}) %all-gather.18.cloned.1.call-update) | async-done | bytes 2097168 | tf_op jit(solution)/shard_map/all_gather | solution.py:188
  301.3 8.2 fusion.58
  309.5 35.7 %all-gather.22.cloned.1.call-done = bf16[2048,1408]{1,0:T(8,128)(2,1)} async-done(((bf16[256,1408]{1,0:T(8,128)(2,1)}), bf16[2048,1408]{1,0:T(8,128)(2,1)}) %all-gather.22.cloned.1.call-update) | async-done | bytes 5767184 | tf_op jit(solution)/shard_map/all_gather | solution.py:144
  345.2 8.3 fusion.59
  353.4 39.0 %all-gather.26.cloned.1.call-done = bf16[512,2048]{1,0:T(8,128)(2,1)} async-done(((bf16[128,2048]{1,0:T(8,128)(2,1)}), bf16[512,2048]{1,0:T(8,128)(2,1)}) %all-gather.26.cloned.1.call-update) | async-done | bytes 2097168 | tf_op jit(solution)/shard_map/all_gather | solution.py:211
  392.4 45.0 %all-gather.24.cloned.1.call-done = bf16[1408,2048]{1,0:T(8,128)(2,1)} async-done(((bf16[1408,256]{1,0:T(8,128)(2,1)}), bf16[1408,2048]{1,0:T(8,128)(2,1)}) %all-gather.24.cloned.1.call-update) | async-done | bytes 5767184 | tf_op jit(solution)/shard_map/all_gather | solution.py:145
  437.4 10.4 multiply_convert_fusion
  459.5 76.9 %reduce-scatter.16.cloned.1.call-done = f32[128,2048]{1,0:T(8,128)} async-done(((f32[512,2048]{1,0:T(8,128)}), f32[128,2048]{1,0:T(8,128)}) %reduce-scatter.16.cloned.1.call-update) | async-done | bytes 1048592 | tf_op jit(solution)/shard_map/reduce_scatter | solution.py:220
  541.9 46.1 %all-gather.28.cloned.1.call-done = bf16[512,2048]{1,0:T(8,128)(2,1)} async-done(((bf16[128,2048]{1,0:T(8,128)(2,1)}), bf16[512,2048]{1,0:T(8,128)(2,1)}) %all-gather.28.cloned.1.call-update) | async-done | bytes 2097168 | tf_op jit(solution)/shard_map/all_gather | solution.py:228
  619.8 9.7 fusion.64
  629.6 9.7 fusion.65
  639.4 9.4 fusion.66
  660.6 24.1 %reduce-scatter.18.cloned.1.call-done = f32[128,2048]{1,0:T(8,128)} async-done(((f32[512,2048]{1,0:T(8,128)}), f32[128,2048]{1,0:T(8,128)}) %reduce-scatter.18.cloned.1.call-update) | async-done | bytes 1048592 | tf_op jit(solution)/shard_map/reduce_scatter | solution.py:253
  686.2 24.5 %all-reduce.2 = (f32[2048]{0:T(1024)S(1)}, f32[2048]{0:T(1024)S(1)}) all-reduce(f32[2048]{0:T(1024)S(1)} %get-tuple-element.13, f32[2048]{0:T(1024)S(1)} %copy-done.31), channel_id=6, replica_groups=mesh['dp'=8,'tensor'=4] {'dp'}, use_global_device_ids=true, to_apply=%region_15.16.clone | all-reduce | flops 4096 | bytes 32768
  710.9 11.8 all-reduce.3
  722.7 8.6 reduce-scatter.14.cloned.1.call-done
  734.3 33.9 %reduce-scatter.22.cloned.1.call-done = f32[256,64]{0,1:T(8,128)} async-done(((f32[2048,64]{0,1:T(8,128)}), f32[256,64]{0,1:T(8,128)}) %reduce-scatter.22.cloned.1.call-update) | async-done | bytes 65552 | tf_op jit(solution)/shard_map/reduce_scatter | solution.py:268
  768.2 37.7 %reduce-scatter.24.cloned.1.call-done = f32[256,64]{0,1:T(8,128)} async-done(((f32[2048,64]{0,1:T(8,128)}), f32[256,64]{0,1:T(8,128)}) %reduce-scatter.24.cloned.1.call-update) | async-done | bytes 65552 | tf_op jit(solution)/shard_map/reduce_scatter | solution.py:269
  805.9 91.1 %reduce-scatter.28.cloned.1.call-done = f32[256,1408]{1,0:T(8,128)} async-done(((f32[2048,1408]{1,0:T(8,128)}), f32[256,1408]{1,0:T(8,128)}) %reduce-scatter.28.cloned.1.call-update) | async-done | bytes 1441808 | tf_op jit(solution)/shard_map/reduce_scatter | solution.py:273
  897.0 91.1 %reduce-scatter.30.cloned.1.call-done = f32[256,1408]{1,0:T(8,128)} async-done(((f32[2048,1408]{1,0:T(8,128)}), f32[256,1408]{1,0:T(8,128)}) %reduce-scatter.30.cloned.1.call-update) | async-done | bytes 1441808 | tf_op jit(solution)/shard_map/reduce_scatter | solution.py:274
  988.1 90.8 %reduce-scatter.32.cloned.1.call-done = f32[1408,256]{1,0:T(8,128)} async-done(((f32[1408,2048]{1,0:T(8,128)}), f32[1408,256]{1,0:T(8,128)}) %reduce-scatter.32.cloned.1.call-update) | async-done | bytes 1441808 | tf_op jit(solution)/shard_map/reduce_scatter | solution.py:275
  1078.9 55.0 %reduce-scatter.26.cloned.1.call-done = f32[512,256]{1,0:T(8,128)} async-done(((f32[512,2048]{1,0:T(8,128)}), f32[512,256]{1,0:T(8,128)}) %reduce-scatter.26.cloned.1.call-update) | async-done | bytes 524304 | tf_op jit(solution)/shard_map/reduce_scatter | solution.py:270
  1134.0 55.0 %reduce-scatter.20.cloned.1.call-done = f32[256,512]{1,0:T(8,128)} async-done(((f32[2048,512]{1,0:T(8,128)}), f32[256,512]{1,0:T(8,128)}) %reduce-scatter.20.cloned.1.call-update) | async-done | bytes 524304 | tf_op jit(solution)/shard_map/reduce_scatter | solution.py:267
  (201 shorter events, 98.8 us)
Async XLA Ops:
  7.2 36.7 %copy-start.32 = (s32[512]{0:T(512)S(1)}, s32[512]{0:T(512)}, u32[]{:S(2)}) copy-start(s32[512]{0:T(512)} %param.13) | copy-start | bytes 6148
  7.2 60.5 %all-gather.12.cloned.1.call-start = ((), (), s32[]{:S(2)}) async-start(), calls=%async_computation.11 | async-start | bytes 2621440 | tf_op jit(solution)/shard_map/all_gather | solution.py:153
  21.6 74.6 %all-gather.14.cloned.1.call-start = ((), (), s32[]{:S(2)}) async-start(), calls=%async_computation.12 | async-start | bytes 2359296 | tf_op jit(solution)/shard_map/all_gather | solution.py:136
  22.4 103.9 %all-gather.16.cloned.1.call-start = ((), (), s32[]{:S(2)}) async-start(), calls=%async_computation.13 | async-start | bytes 2359296 | tf_op jit(solution)/shard_map/all_gather | solution.py:139
  23.1 185.0 %reduce-scatter.12.cloned.1.call-start = ((), (), s32[]{:S(2)}) async-start(), calls=%async_computation.14 | async-start | bytes 5242880 | tf_op jit(solution)/shard_map/reduce_scatter | solution.py:181
  23.2 50.4 %copy-start.40 = (f32[32]{0:T(128)}, f32[32]{0:T(128)S(1)}, u32[]{:S(2)}) copy-start(f32[32]{0:T(128)S(1)} %multiply_exponential_fusion) | copy-start | bytes 388
  24.7 48.9 %copy-start.29 = (f32[512]{0:T(512)}, f32[512]{0:T(512)S(1)}, u32[]{:S(2)}) copy-start(f32[512]{0:T(512)S(1)} %fusion.46) | copy-start | bytes 6148
  34.5 39.1 %copy-start.8 = (bf16[2048,64]{0,1:T(8,128)(2,1)}, bf16[2048,64]{0,1:T(8,128)(2,1)S(1)}, u32[]{:S(2)}) copy-start(bf16[2048,64]{0,1:T(8,128)(2,1)S(1)} %all_gather.49) | copy-start | bytes 786436
  44.1 58.5 %copy-start.11 = (pred[512,512]{0,1:T(8,128)(4,1)}, pred[512,512]{0,1:T(8,128)(4,1)S(1)}, u32[]{:S(2)}) copy-start(pred[512,512]{0,1:T(8,128)(4,1)S(1)} %fusion.24) | copy-start | bytes 786436
  67.7 28.5 %copy-start = (bf16[512,2048]{1,0:T(8,128)(2,1)S(1)}, bf16[512,2048]{1,0:T(8,128)(2,1)}, u32[]{:S(2)}) copy-start(bf16[512,2048]{1,0:T(8,128)(2,1)} %all-gather.12.cloned.1.call-done) | copy-start | bytes 6291460
  70.5 28.8 %copy-start.23 = (bf16[512,32]{0,1:T(8,128)(2,1)}, bf16[512,32]{0,1:T(8,128)(2,1)S(1)}, u32[]{:S(2)}) copy-start(bf16[512,32]{0,1:T(8,128)(2,1)S(1)} %get-tuple-element.32) | copy-start | bytes 98308
  70.6 28.8 %copy-start.25 = (bf16[512,32]{0,1:T(8,128)(2,1)}, bf16[512,32]{0,1:T(8,128)(2,1)S(1)}, u32[]{:S(2)}) copy-start(bf16[512,32]{0,1:T(8,128)(2,1)S(1)} %get-tuple-element.33) | copy-start | bytes 98308
  131.2 122.4 %all-gather.20.cloned.1.call-start = ((), (), s32[]{:S(2)}) async-start(), calls=%async_computation.16 | async-start | bytes 6488064 | tf_op jit(solution)/shard_map/all_gather | solution.py:143
  131.8 169.5 %all-gather.18.cloned.1.call-start = ((), (), s32[]{:S(2)}) async-start(), calls=%async_computation.15 | async-start | bytes 2621440 | tf_op jit(solution)/shard_map/all_gather | solution.py:188
  211.3 133.9 %all-gather.22.cloned.1.call-start = ((), (), s32[]{:S(2)}) async-start(), calls=%async_computation.17 | async-start | bytes 6488064 | tf_op jit(solution)/shard_map/all_gather | solution.py:144
  212.0 180.4 %all-gather.26.cloned.1.call-start = ((), (), s32[]{:S(2)}) async-start(), calls=%async_computation.20 | async-start | bytes 2621440 | tf_op jit(solution)/shard_map/all_gather | solution.py:211
  212.8 224.7 %all-gather.24.cloned.1.call-start = ((), (), s32[]{:S(2)}) async-start(), calls=%async_computation.18 | async-start | bytes 6488064 | tf_op jit(solution)/shard_map/all_gather | solution.py:145
  213.5 322.9 %reduce-scatter.16.cloned.1.call-start = ((), (), s32[]{:S(2)}) async-start(), calls=%async_computation.21 | async-start | bytes 5242880 | tf_op jit(solution)/shard_map/reduce_scatter | solution.py:220
  459.5 128.5 %all-gather.28.cloned.1.call-start = ((), (), s32[]{:S(2)}) async-start(), calls=%async_computation.22 | async-start | bytes 2621440 | tf_op jit(solution)/shard_map/all_gather | solution.py:228
  541.7 142.9 %reduce-scatter.18.cloned.1.call-start = ((), (), s32[]{:S(2)}) async-start(), calls=%async_computation.23 | async-start | bytes 5242880 | tf_op jit(solution)/shard_map/reduce_scatter | solution.py:253
  608.9 122.5 %reduce-scatter.14.cloned.1.call-start = ((), (), s32[]{:S(2)}) async-start(), calls=%async_computation.19 | async-start | bytes 2621440 | tf_op jit(solution)/shard_map/reduce_scatter | solution.py:195
  616.8 151.4 %reduce-scatter.22.cloned.1.call-start = ((), (), s32[]{:S(2)}) async-start(), calls=%async_computation.25 | async-start | bytes 589824 | tf_op jit(solution)/shard_map/reduce_scatter | solution.py:268
  618.2 187.7 %reduce-scatter.24.cloned.1.call-start = ((), (), s32[]{:S(2)}) async-start(), calls=%async_computation.26 | async-start | bytes 589824 | tf_op jit(solution)/shard_map/reduce_scatter | solution.py:269
  619.6 277.4 %reduce-scatter.28.cloned.1.call-start = ((), (), s32[]{:S(2)}) async-start(), calls=%async_computation.28 | async-start | bytes 12976128 | tf_op jit(solution)/shard_map/reduce_scatter | solution.py:273
  629.6 358.5 %reduce-scatter.30.cloned.1.call-start = ((), (), s32[]{:S(2)}) async-start(), calls=%async_computation.29 | async-start | bytes 12976128 | tf_op jit(solution)/shard_map/reduce_scatter | solution.py:274
  639.4 439.5 %reduce-scatter.32.cloned.1.call-start = ((), (), s32[]{:S(2)}) async-start(), calls=%async_computation.30 | async-start | bytes 12976128 | tf_op jit(solution)/shard_map/reduce_scatter | solution.py:275
  648.8 485.1 %reduce-scatter.26.cloned.1.call-start = ((), (), s32[]{:S(2)}) async-start(), calls=%async_computation.27 | async-start | bytes 4718592 | tf_op jit(solution)/shard_map/reduce_scatter | solution.py:270
  653.9 535.0 %reduce-scatter.20.cloned.1.call-start = ((), (), s32[]{:S(2)}) async-start(), calls=%async_computation.24 | async-start | bytes 4718592 | tf_op jit(solution)/shard_map/reduce_scatter | solution.py:267
  658.7 72.7 %copy-start.2 = (f32[128,2048]{1,0:T(8,128)S(1)}, f32[128,2048]{1,0:T(8,128)}, u32[]{:S(2)}) copy-start(f32[128,2048]{1,0:T(8,128)} %reduce-scatter.16.cloned.1.call-done) | copy-start | bytes 3145732
  658.7 72.7 %copy-start.5 = (bf16[128,2048]{1,0:T(8,128)(2,1)S(1)}, bf16[128,2048]{1,0:T(8,128)(2,1)}, u32[]{:S(2)}) copy-start(bf16[128,2048]{1,0:T(8,128)(2,1)} %param.23) | copy-start | bytes 1572868
  658.7 72.7 %copy-start.37 = (f32[128]{0:T(128)S(1)}, f32[128]{0:T(128)}, u32[]{:S(2)}) copy-start(f32[128]{0:T(128)} %copy-done.36) | copy-start | bytes 1540
  658.7 72.7 %copy-start.43 = (f32[128]{0:T(128)S(1)}, f32[128]{0:T(128)}, u32[]{:S(2)}) copy-start(f32[128]{0:T(128)} %copy-done.42) | copy-start | bytes 1540
  (39 other events, 244.3 us)
Sparse Core Ops, SparseCore 0:
  21.7 45.9 all-gather.11
  69.6 26.5 all-gather.13
  98.1 28.0 all-gather.15
  131.3 76.7 reduce-scatter.11
  209.9 43.6 all-gather.19
  255.6 45.6 all-gather.17
  303.2 41.9 all-gather.21
  346.8 45.6 all-gather.25
  394.3 43.0 all-gather.23
  459.6 76.7 reduce-scatter.15
  541.8 46.1 all-gather.27
  609.0 75.5 reduce-scatter.17
  686.9 44.3 reduce-scatter.13
  734.8 33.3 reduce-scatter.21
  771.7 34.1 reduce-scatter.23
  809.8 87.1 reduce-scatter.27
  900.9 87.1 reduce-scatter.29
  992.0 86.8 reduce-scatter.31
  1082.8 51.0 reduce-scatter.25
  1137.7 51.1 reduce-scatter.19
where the time goes:
time: 1210 us; the launch traced here: 1200 us
  waiting for transfers between devices  955 us (79%)
  matrix products  123 us (10%)
  blocking collectives  75 us (6%)
  other arithmetic  19.8 us (2%)
  between operations  16.1 us (1%)
    reduce_scatter x1, waiting for transfers between devices, on_device(): lax.psum_scatter(grad_w_gate, 'dp', scatter_dimension=0, tiled=True)  91.1 us
    reduce_scatter x1, waiting for transfers between devices, on_device(): lax.psum_scatter(grad_w_up, 'dp', scatter_dimension=0, tiled=True)  91.1 us
    reduce_scatter x1, waiting for transfers between devices, on_device(): lax.psum_scatter(grad_w_down, 'dp', scatter_dimension=1, tiled=True)  90.8 us
    reduce_scatter x1, waiting for transfers between devices, on_device(): lax.psum_scatter(contract(grad_gate_rows, gate_full, 1, 1) + contract(gra...  76.9 us
    dot_general x14, matrix products, contract(): lax.dot_general(left, right, (((left_dim,), (right_dim,)), ((), ())), pre...  71.2 us
    reduce_scatter x1, waiting for transfers between devices, on_device(): lax.psum_scatter(jnp.dot(mixed_flat, output_full, preferred_element_type=...  66.9 us
    reduce_scatter x1, waiting for transfers between devices, on_device(): lax.psum_scatter(grad_w_output, 'dp', scatter_dimension=1, tiled=True)  55 us
    reduce_scatter x1, waiting for transfers between devices, on_device(): lax.psum_scatter(grad_w_query, 'dp', scatter_dimension=0, tiled=True)  55 us
  transfers between devices with their start and end apart: 20, of which 20 were waited for; matrix products, arithmetic and copies ran while one was open for 7% of the time, Pallas kernels for 0%

commit v1 on v0

v1 whole, which is shorter than its diff:
```python
import functools
import math

import jax
import jax.numpy as jnp
from jax import lax
from jax.experimental import pallas as pl
from jax.experimental.pallas import tpu as pltpu
from jax.sharding import PartitionSpec as P

HD = 64
EPSILON = 1e-05
NEGATIVE = -1e30
LANES = 128
BF = jnp.bfloat16
F32 = jnp.float32
VMEM_BYTES = 66_000_000


def spans(bits):
    masks = [0]
    for bit in bits:
        masks = masks + [mask | (1 << bit) for mask in masks]
    return masks


def flip(index, mask, width):
    total = 0
    for bit in range(width):
        own = lax.rem(lax.div(index, 1 << bit), 2)
        if isinstance(mask, int):
            other = (mask >> bit) & 1
        else:
            other = lax.rem(lax.div(mask, 1 << bit), 2)
        total = total + lax.rem(own + other, 2) * (1 << bit)
    return total


def aligned(value, step):
    return value if isinstance(value, int) else pl.multiple_of(value, step)


def remote(src, dst, send_sem, recv_sem, device):
    return pltpu.make_async_remote_copy(
        src_ref=src,
        dst_ref=dst,
        send_sem=send_sem,
        recv_sem=recv_sem,
        device_id=device,
        device_id_type=pl.DeviceIdType.MESH,
    )


def dot(left, right, left_dim=1, right_dim=0):
    return lax.dot_general(
        left, right, (((left_dim,), (right_dim,)), ((), ())), preferred_element_type=F32
    )


def tiles_of(size, most):
    units = size // LANES
    parts = -(-units // most)
    cuts, start = [], 0
    for part in range(parts):
        width = (units // parts + (1 if part < units % parts else 0)) * LANES
        cuts.append((start, width))
        start += width
    return cuts


def enter(t, nt, me, width, barrier, everyone_along_tensor=False):
    signal = functools.partial(
        pl.semaphore_signal, barrier, inc=1, device_id_type=pl.DeviceIdType.MESH
    )
    for mask in range(1, 1 << width):
        signal(device_id={"dp": flip(me, mask, width)})
    if everyone_along_tensor:
        for step in range(1, nt):
            signal(device_id={"tensor": lax.rem(t + step, nt)})
        pl.semaphore_wait(barrier, (1 << width) - 1 + nt - 1)
        return

    @pl.when(t > 0)
    def _():
        signal(device_id={"tensor": t - 1})

    @pl.when(t < nt - 1)
    def _():
        signal(device_id={"tensor": t + 1})

    neighbours = lax.min(t, 1) + lax.min(nt - 1 - t, 1)
    pl.semaphore_wait(barrier, (1 << width) - 1 + neighbours)


class LineGather:
    def __init__(self, full, t, nt, sems):
        self.full, self.t, self.nt, self.sems = full, t, nt, sems
        self.rows = full.shape[0] // nt

    def window(self, j):
        return self.full.at[pl.ds(pl.multiple_of(j * self.rows, self.rows), self.rows), :]

    def right(self, j):
        return remote(
            self.window(j), self.window(j), self.sems.at[0, j], self.sems.at[2, j],
            {"tensor": lax.rem(self.t + 1, self.nt)},
        )

    def left(self, j):
        return remote(
            self.window(j), self.window(j), self.sems.at[1, j], self.sems.at[3, j],
            {"tensor": lax.rem(self.t + self.nt - 1, self.nt)},
        )

    def start(self):
        @pl.when(self.t < self.nt - 1)
        def _():
            self.right(self.t).start()

        @pl.when(self.t > 0)
        def _():
            self.left(self.t).start()

    def step(self, s):
        t, nt = self.t, self.nt

        @pl.when(t >= s)
        def _():
            self.right(t - s).wait_recv()

            @pl.when(t < nt - 1)
            def _():
                self.right(t - s).start()

        @pl.when(t + s < nt)
        def _():
            self.left(t + s).wait_recv()

            @pl.when(t > 0)
            def _():
                self.left(t + s).start()

    def finish(self):
        t, nt = self.t, self.nt
        for s in range(nt):
            @pl.when((t >= s) & (t < nt - 1))
            def _():
                self.right(t - s).wait_send()

            @pl.when((t + s < nt) & (t > 0))
            def _():
                self.left(t + s).wait_send()


class LineScatter:
    def __init__(self, part, sent, from_left, from_right, t, nt, cuts, sems):
        self.part, self.sent = part, sent
        self.from_left, self.from_right = from_left, from_right
        self.t, self.nt, self.cuts, self.sems = t, nt, cuts, sems
        self.rows = sent.shape[1]
        self.width = sent.shape[2] // cuts

    def cols(self, c):
        if isinstance(c, int):
            return slice(c * self.width, (c + 1) * self.width)
        return pl.ds(pl.multiple_of(c * self.width, self.width), self.width)

    def right(self, j, c):
        cols = self.cols(c)
        return remote(
            self.sent.at[j, :, cols], self.from_left.at[j, :, cols],
            self.sems.at[0, j, c], self.sems.at[2, j, c],
            {"tensor": lax.rem(self.t + 1, self.nt)},
        )

    def left(self, j, c):
        cols = self.cols(c)
        return remote(
            self.sent.at[j, :, cols], self.from_right.at[j, :, cols],
            self.sems.at[1, j, c], self.sems.at[3, j, c],
            {"tensor": lax.rem(self.t + self.nt - 1, self.nt)},
        )

    def mine(self, j, c):
        rows = pl.ds(pl.multiple_of(j * self.rows, self.rows), self.rows)
        return self.part[rows, self.cols(c)]

    def edge(self, c):
        t, nt = self.t, self.nt

        @pl.when(t == 0)
        def _():
            @pl.loop(0, nt - 1)
            def _(k):
                j = nt - 1 - k
                self.sent[j, :, self.cols(c)] = self.mine(j, c).astype(BF)
                self.right(j, c).start()

        @pl.when(t == nt - 1)
        def _():
            @pl.loop(0, nt - 1)
            def _(j):
                self.sent[j, :, self.cols(c)] = self.mine(j, c).astype(BF)
                self.left(j, c).start()

    def round(self, k):
        t, nt = self.t, self.nt
        j_right, j_left = nt - 1 - k, k

        @pl.loop(0, self.cuts)
        def _(c):
            @pl.when((t > 0) & (j_right > t))
            def _():
                self.right(j_right, c).wait_recv()
                total = self.mine(j_right, c) + self.from_left[j_right, :, self.cols(c)].astype(F32)
                self.sent[j_right, :, self.cols(c)] = total.astype(BF)
                self.right(j_right, c).start()

            @pl.when((t < nt - 1) & (j_left < t))
            def _():
                self.left(j_left, c).wait_recv()
                total = self.mine(j_left, c) + self.from_right[j_left, :, self.cols(c)].astype(F32)
                self.sent[j_left, :, self.cols(c)] = total.astype(BF)
                self.left(j_left, c).start()

    def own(self, store):
        t, nt = self.t, self.nt
        rows = pl.ds(pl.multiple_of(t * self.rows, self.rows), self.rows)
        for c in range(self.cuts):
            cols = self.cols(c)

            @pl.when(t > 0)
            def _():
                self.right(t, c).wait_recv()
                self.part[rows, cols] += self.from_left[t, :, cols].astype(F32)

            @pl.when(t < nt - 1)
            def _():
                self.left(t, c).wait_recv()
                self.part[rows, cols] += self.from_right[t, :, cols].astype(F32)

            store(cols, self.part[rows, cols])

    def finish(self):
        t, nt = self.t, self.nt
        for j in range(nt):
            for c in range(self.cuts):
                @pl.when(j > t)
                def _():
                    self.right(j, c).wait_send()

                @pl.when(j < t)
                def _():
                    self.left(j, c).wait_send()


class Cube:
    def setup(self, me, width, half_send, half_recv, pair_send, pair_recv):
        self.me, self.width = me, width
        self.hs, self.hr, self.ps, self.pr = half_send, half_recv, pair_send, pair_recv
        self.bits = list(range(1, width))
        self.orders = (self.bits, self.bits[::-1])
        self.masks = spans(self.bits)
        self.stages = len(self.bits)

    def at(self, mask):
        return flip(self.me, mask, self.width)


class BlockGather(Cube):
    def __init__(self, own, full, by_rows, me, width, *sems):
        self.setup(me, width, *sems)
        self.own_ref, self.full, self.by_rows = own, full, by_rows

    def half(self, h):
        rows = self.own_ref.shape[0] // 2
        return self.own_ref.at[pl.ds(h * rows, rows), :]

    def window(self, who, h=None):
        rows, cols = self.own_ref.shape
        take, start = (rows, 0) if h is None else (rows // 2, h * (rows // 2))
        if self.by_rows:
            return self.full.at[pl.ds(aligned(who * rows + start, take), take), :]
        return self.full.at[pl.ds(start, take), pl.ds(aligned(who * cols, cols), cols)]

    def hop(self, stage, h, m):
        order = self.orders[h]
        bit = 1 << order[stage]
        slot = (m | bit) >> 1
        src = self.half(h) if m == 0 else self.window(self.at(m), h)
        return remote(
            src, self.window(self.at(m), h), self.hs.at[h, slot], self.hr.at[h, slot],
            {"dp": self.at(bit)},
        )

    def send(self, stage):
        for h in range(2):
            for m in spans(self.orders[h][:stage]):
                self.hop(stage, h, m).start()

    def wait(self, stage):
        for h in range(2):
            bit = 1 << self.orders[h][stage]
            for m in spans(self.orders[h][:stage]):
                slot = (m | bit) >> 1
                landed = self.window(self.at(m | bit), h)
                remote(
                    landed, landed, self.hs.at[h, slot], self.hr.at[h, slot], {"dp": self.at(bit)}
                ).wait_recv()

    def pair(self, m):
        src = self.own_ref if m == 0 else self.window(self.at(m))
        return remote(
            src, self.window(self.at(m)), self.ps.at[m >> 1], self.pr.at[m >> 1],
            {"dp": self.at(1)},
        )

    def pair_send(self):
        for m in self.masks:
            self.pair(m).start()

    def pair_wait(self):
        for m in self.masks:
            landed = self.window(self.at(m | 1))
            remote(
                landed, landed, self.ps.at[m >> 1], self.pr.at[m >> 1], {"dp": self.at(1)}
            ).wait_recv()

    def place(self, sem):
        return pltpu.make_async_copy(self.own_ref, self.window(self.me), sem)

    def drain(self):
        for stage in range(self.stages):
            for h in range(2):
                for m in spans(self.orders[h][:stage]):
                    self.hop(stage, h, m).wait_send()
        for m in self.masks:
            self.pair(m).wait_send()


class BlockScatter(Cube):
    def __init__(self, chunk, out_sent, total, landed, store, me, width, *sems):
        self.setup(me, width, *sems)
        self.chunk, self.sent, self.total, self.landed = chunk, out_sent, total, landed
        self.store = store
        self.slots = 1 << (width - 1)

    def pair(self, slot):
        return remote(
            self.sent.at[slot], self.total.at[slot], self.ps.at[slot], self.pr.at[slot],
            {"dp": self.at(1)},
        )

    def give(self):
        @pl.loop(0, self.slots)
        def _(k):
            slot = self.slots - 1 - k
            self.sent[slot] = self.chunk(self.at(2 * slot + 1)).astype(BF)
            self.pair(slot).start()

    def given(self):
        @pl.loop(0, self.slots)
        def _(slot):
            self.pair(slot).wait_send()

    def take(self):
        @pl.loop(0, self.slots)
        def _(k):
            slot = self.slots - 1 - k
            term = self.chunk(self.at(2 * slot))
            self.pair(slot).wait_recv()
            self.total[slot] = (term + self.total[slot].astype(F32)).astype(BF)

    def moves(self, stage):
        for h in range(2):
            order = self.orders[h]
            last = self.stages - 1 - stage
            bit = 1 << order[last]
            for m in spans(order[:last]):
                yield h, bit, m | bit

    def hop(self, h, bit, m):
        rows = self.total.shape[1] // 2
        return remote(
            self.total.at[m >> 1, pl.ds(h * rows, rows), :], self.landed.at[h, (m >> 1) - 1],
            self.hs.at[h, m >> 1], self.hr.at[h, m >> 1], {"dp": self.at(bit)},
        )

    def send(self, stage):
        for h, bit, m in self.moves(stage):
            self.hop(h, bit, m).start()

    def add(self, stage):
        rows = self.total.shape[1] // 2
        for h, bit, m in self.moves(stage):
            self.hop(h, bit, m).wait_recv()
            keep = (m ^ bit) >> 1
            at = slice(h * rows, (h + 1) * rows)
            total = self.total[keep, at, :].astype(F32) + self.landed[h, (m >> 1) - 1].astype(F32)
            if stage == self.stages - 1:
                self.store(at, total)
            else:
                self.total[keep, at, :] = total.astype(BF)

    def drain(self):
        for stage in range(self.stages):
            for h, bit, m in self.moves(stage):
                self.hop(h, bit, m).wait_send()


def inverse_of(rows):
    return lax.rsqrt(jnp.mean(rows * rows, axis=-1, keepdims=True) + EPSILON)


def times_gain(unit, gains, which, store):
    parts, _, width = gains.shape
    for d in range(parts):
        cols = slice(d * width, (d + 1) * width)
        store(cols, unit[:, cols] * gains[d, which : which + 1, :])


def lane_index(shape):
    return lax.broadcasted_iota(jnp.int32, shape, len(shape) - 1)


def rope_into(cos_ref, sin_ref, segc, segr):
    rows = segc.shape[0]
    before = (segr[...] < segc[...]).astype(F32)
    start = jnp.sum(before, axis=1, keepdims=True)
    position = lax.broadcasted_iota(jnp.int32, (rows, 1), 0).astype(F32) - start
    lane = lane_index((rows, LANES))
    half = HD // 2
    frequency = jnp.exp(lax.rem(lane, half).astype(F32) * (-math.log(10000.0) / half))
    angle = position * frequency
    cos_ref[...] = jnp.cos(angle)
    sine = jnp.sin(angle)
    sin_ref[...] = jnp.where(lax.rem(lane, HD) < half, -sine, sine)


def swapped(x):
    lane = lane_index(x.shape)
    half = HD // 2
    return jnp.where(
        lax.rem(lane, HD) < half,
        pltpu.roll(x, LANES - half, 1),
        pltpu.roll(x, half, 1),
    )


def bias_into(bias, segc, segr):
    rows = segc.shape[0]
    query = lax.broadcasted_iota(jnp.int32, (rows, rows), 0)
    key = lax.broadcasted_iota(jnp.int32, (rows, rows), 1)
    seen = (segr[...] == segc[...]) & (query >= key)
    bias[...] = jnp.where(seen, 0.0, NEGATIVE)


def pad_pair(keys_values, keys, values):
    low = lane_index(keys_values.shape) < HD
    key = jnp.where(low, keys_values, 0.0)
    value = jnp.where(low, 0.0, keys_values)
    keys[0] = key.astype(BF)
    keys[1] = pltpu.roll(key, HD, 1).astype(BF)
    values[0] = pltpu.roll(value, HD, 1).astype(BF)
    values[1] = value.astype(BF)


def query_cuts(rows):
    block = 256 if rows % 256 == 0 else rows
    return [(start, block, start + block) for start in range(0, rows, block)]


def attend_pairs(first, last, qo, kpad, vpad, bias, mo, lo):
    rows = qo.shape[0]
    lane = lane_index((1, LANES))

    @pl.loop(first, last)
    def _(pair):
        lanes = pl.ds(pl.multiple_of(pair * LANES, LANES), LANES)
        for start, block, seen in query_cuts(rows):
            at = slice(start, start + block)
            query = qo[at, lanes]
            mixed = jnp.zeros((block, LANES), F32)
            logs = lo[at, :]
            for side in range(2):
                scores = dot(query, kpad[side, :seen, :], 1, 1) + bias[at, :seen]
                top = jnp.max(scores, axis=-1, keepdims=True)
                probs = jnp.exp(scores - top)
                total = jnp.sum(probs, axis=-1, keepdims=True)
                mixed = mixed + dot(probs.astype(BF), vpad[side, :seen, :]) / total
                logs = jnp.where(lane == 2 * pair + side, top + jnp.log(total), logs)
            lo[at, :] = logs
            mo[at, lanes] = mixed.astype(BF)


def front_kernel(
    nt, width,
    x, cot, gain, segc, segr, wqkv, wo, gate, up, down,
    wqkv_f, wo_f, gate_f, up_f, down_f, na, cf, nf, qo, kvo, mo, lo, hid, gall, cos, sin,
    part, sent, from_left, from_right, wqkv_v, wo_v, bias, kpad, vpad,
    gain_sem, place_sem, line_na, line_cf, line_nf, scatter_sem, hs, hr, ps, pr,
):
    me, t = lax.axis_index("dp"), lax.axis_index("tensor")
    nd = 1 << width
    rows, model = x.shape
    queries = qo.shape[1]
    enter(t, nt, me, width, pltpu.get_barrier_semaphore())

    gathers = []
    for w, (own, full, by_rows) in enumerate(
        ((wqkv, wqkv_f, True), (wo, wo_f, False), (gate, gate_f, True), (up, up_f, True), (down, down_f, False))
    ):
        gathers.append(
            BlockGather(own, full, by_rows, me, width, hs.at[w], hr.at[w], ps.at[w], pr.at[w])
        )
    g_qkv, g_out, g_gate, g_up, g_down = gathers

    def gain_copy(mask):
        return remote(
            gain, gall.at[me], gain_sem.at[0, mask], gain_sem.at[1, mask],
            {"dp": flip(me, mask, width)},
        )

    for mask in range(1, nd):
        gain_copy(mask).start()
    gall[me] = gain[...]
    stages = g_qkv.stages
    for g in (g_qkv, g_out, g_gate):
        g.send(0)
    for w, g in enumerate(gathers):
        g.place(place_sem.at[w]).start()
    for mask in range(1, nd):
        slot = gall.at[flip(me, mask, width)]
        remote(
            slot, slot, gain_sem.at[0, mask], gain_sem.at[1, mask], {"dp": flip(me, mask, width)}
        ).wait_recv()

    def forward(g, stage):
        g.wait(stage)
        if stage + 1 < stages:
            g.send(stage + 1)
        else:
            g.pair_send()

    local = pl.ds(pl.multiple_of(t * rows, rows), rows)
    residual = x[...].astype(F32)

    def store_na(cols, value):
        na[local, cols] = value.astype(BF)

    times_gain(residual * inverse_of(residual), gall, 0, store_na)
    cf[local, :] = cot[...]
    tokens = LineGather(na, t, nt, line_na)
    tokens.start()
    for s in range(stages - 1):
        forward(g_qkv, s)
        forward(g_out, s)
    rope_into(cos, sin, segc, segr)
    bias_into(bias, segc, segr)
    lo[...] = jnp.zeros_like(lo)
    fills = [
        lambda: (forward(g_gate, 0), g_up.send(0)),
        lambda: (forward(g_qkv, stages - 1), forward(g_out, stages - 1), g_down.send(0)),
    ]
    for s in range(1, nt):
        tokens.step(s)
        if fills:
            fills.pop(0)()
    for fill in fills:
        fill()

    cots = LineGather(cf, t, nt, line_cf)
    cots.start()

    g_qkv.place(place_sem.at[0]).wait()
    g_qkv.pair_wait()
    load = pltpu.make_async_copy(wqkv_f, wqkv_v, place_sem.at[5])
    load.start()
    g_out.place(place_sem.at[1]).wait()
    g_out.pair_wait()
    load_out = pltpu.make_async_copy(wo_f, wo_v, place_sem.at[6])
    load_out.start()
    load.wait()

    wide = wqkv_v.shape[1]
    part[:, :wide] = dot(na[...], wqkv_v[...])
    c, s_ = cos[...], sin[...]
    for start in range(0, queries, LANES):
        lanes = slice(start, start + LANES)
        value = part[:, lanes]
        qo[:, lanes] = ((value * c + swapped(value) * s_) * HD ** (-0.5)).astype(BF)
    value = part[:, queries : queries + LANES]
    keyed = jnp.where(lane_index(value.shape) < HD, value * c + swapped(value) * s_, value)
    kvo[...] = keyed.astype(BF)
    pad_pair(keyed, kpad, vpad)

    pairs = queries // LANES
    later = [
        lambda: forward(g_up, 0),
        lambda: forward(g_down, 0),
    ]
    for s in range(1, stages):
        later.append(functools.partial(forward, g_gate, s))
        later.append(functools.partial(forward, g_up, s))
        later.append(functools.partial(forward, g_down, s))
    attend_pairs(0, pairs // 2, qo, kpad, vpad, bias, mo, lo)
    later.pop(0)()
    cots.step(1)
    attend_pairs(pairs // 2, pairs, qo, kpad, vpad, bias, mo, lo)
    later.pop(0)()
    load_out.wait()

    summed = LineScatter(part, sent, from_left, from_right, t, nt, scatter_sem.shape[2], scatter_sem)
    for cut in range(summed.cuts):
        cols = summed.cols(cut)
        part[:, cols] = dot(mo[...], wo_v[:, cols])
        summed.edge(cut)
    for k in range(nt - 1):
        summed.round(k)
        if k + 2 < nt:
            cots.step(k + 2)
        if later:
            later.pop(0)()

    def store_hidden(cols, value):
        hid[:, cols] = x[:, cols].astype(F32) + value

    summed.own(store_hidden)
    hidden = hid[...]

    def store_nf(cols, value):
        nf[local, cols] = value.astype(BF)

    times_gain(hidden * inverse_of(hidden), gall, 1, store_nf)
    tokens_ffn = LineGather(nf, t, nt, line_nf)
    tokens_ffn.start()
    for s in range(1, nt):
        if later:
            later.pop(0)()
        tokens_ffn.step(s)
    for fill in later:
        fill()
    for w, g in enumerate(gathers):
        if w >= 2:
            g.place(place_sem.at[w]).wait()
            g.pair_wait()
    for g in gathers:
        g.drain()
    for mask in range(1, nd):
        gain_copy(mask).wait_send()
    tokens.finish()
    cots.finish()
    tokens_ffn.finish()
    summed.finish()


def vmem():
    return pl.BlockSpec(memory_space=pltpu.VMEM)


def hbm():
    return pl.BlockSpec(memory_space=pl.ANY)


def scatter_scratch(tokens, nt, model):
    rows = tokens // nt
    return [
        pltpu.VMEM((tokens, model), F32),
        pltpu.VMEM((nt, rows, model), BF),
        pltpu.VMEM((nt, rows, model), BF),
        pltpu.VMEM((nt, rows, model), BF),
    ]


def dma(*shape):
    return pltpu.SemaphoreType.DMA(shape)


CUTS = 4


def front(nt, nd, x, cot, gain, segc, segr, wqkv, wo, gate, up, down):
    width = nd.bit_length() - 1
    rows, model = x.shape
    tokens = segc.shape[0]
    queries = wo.shape[0]
    hidden = gate.shape[1]
    half = nd // 2
    shape = jax.ShapeDtypeStruct
    outs = [
        (shape((model, wqkv.shape[1]), BF), hbm()),
        (shape((queries, model), BF), hbm()),
        (shape((model, hidden), BF), hbm()),
        (shape((model, hidden), BF), hbm()),
        (shape((hidden, model), BF), hbm()),
        (shape((tokens, model), BF), vmem()),
        (shape((tokens, model), BF), vmem()),
        (shape((tokens, model), BF), vmem()),
        (shape((tokens, queries), BF), vmem()),
        (shape((tokens, LANES), BF), vmem()),
        (shape((tokens, queries), BF), vmem()),
        (shape((tokens, LANES), F32), vmem()),
        (shape((rows, model), F32), vmem()),
        (shape((nd,) + gain.shape, F32), vmem()),
        (shape((tokens, LANES), F32), vmem()),
        (shape((tokens, LANES), F32), vmem()),
    ]
    return pl.pallas_call(
        functools.partial(front_kernel, nt, width),
        out_shape=[o for o, _ in outs],
        in_specs=[vmem()] * 10,
        out_specs=[s for _, s in outs],
        scratch_shapes=scatter_scratch(tokens, nt, model)
        + [
            pltpu.VMEM((model, wqkv.shape[1]), BF),
            pltpu.VMEM((queries, model), BF),
            pltpu.VMEM((tokens, tokens), F32),
            pltpu.VMEM((2, tokens, LANES), BF),
            pltpu.VMEM((2, tokens, LANES), BF),
            dma(2, nd),
            dma(7),
            dma(4, nt),
            dma(4, nt),
            dma(4, nt),
            dma(4, nt, CUTS),
            dma(5, 2, half),
            dma(5, 2, half),
            dma(5, half),
            dma(5, half),
        ],
        compiler_params=pltpu.CompilerParams(
            collective_id=0, has_side_effects=True, vmem_limit_bytes=VMEM_BYTES
        ),
        name="front",
    )(x, cot, gain, segc, segr, wqkv, wo, gate, up, down)


def back_through_norm(raw, grads, gains, which, store, store_gain):
    parts, _, width = gains.shape
    cuts = [slice(d * width, (d + 1) * width) for d in range(parts)]
    model = parts * width
    square = sum(jnp.sum(raw(c) * raw(c), axis=-1, keepdims=True) for c in cuts)
    inverse = lax.rsqrt(square / model + EPSILON)
    mean = 0.0
    for d, c in enumerate(cuts):
        unit = raw(c) * inverse
        grad = grads(c)
        store_gain(c, jnp.sum(grad * unit, axis=0, keepdims=True))
        mean = mean + jnp.sum(grad * gains[d, which : which + 1, :] * unit, axis=-1, keepdims=True)
    mean = mean / model
    for d, c in enumerate(cuts):
        unit = raw(c) * inverse
        store(c, inverse * (grads(c) * gains[d, which : which + 1, :] - unit * mean))


def ffn_kernel(
    nt, width,
    nf, cf, hid, cot, gall, gate_f, up_f, down_f,
    act, branch, gh, gains, d_gate, d_up, d_down,
    gate_v, up_v, down_v, wide, dg, du, sent, from_left, from_right, given, totals, landed,
    load_sem, out_sem, scatter_sem, line_sem, hs, hr, ps, pr,
):
    me, t = lax.axis_index("dp"), lax.axis_index("tensor")
    rows, model = hid.shape
    tokens, hidden = act.shape
    shard = model >> width
    cuts = tiles_of(hidden, 6)
    span = max(size for _, size in cuts)
    loads = []
    for i, (start, size) in enumerate(cuts):
        at = pl.ds(start, size)
        loads.append(
            [
                pltpu.make_async_copy(gate_f.at[:, at], gate_v.at[:, at], load_sem.at[i, 0]),
                pltpu.make_async_copy(up_f.at[:, at], up_v.at[:, at], load_sem.at[i, 1]),
                pltpu.make_async_copy(down_f.at[at, :], down_v.at[at, :], load_sem.at[i, 2]),
            ]
        )
        for load in loads[-1]:
            load.start()
    enter(t, nt, me, width, pltpu.get_barrier_semaphore())

    block = 64
    for i, (start, size) in enumerate(cuts):
        at = slice(start, start + size)
        for load in loads[i]:
            load.wait()
        wide[:, 0:size] = dot(nf[...], gate_v[:, at])
        wide[:, span : span + size] = dot(nf[...], up_v[:, at])
        wide[:, 2 * span : 2 * span + size] = dot(cf[...], down_v[at, :], 1, 1)

        @pl.loop(0, tokens // block)
        def _(k):
            these = pl.ds(pl.multiple_of(k * block, block), block)
            g = wide[these, 0:size]
            u = wide[these, span : span + size]
            ga = wide[these, 2 * span : 2 * span + size]
            sig = 1.0 / (1.0 + jnp.exp(-g))
            gs = g * sig
            act[these, at] = (gs * u).astype(BF)
            du[these, at] = (ga * gs).astype(BF)
            dg[these, at] = (ga * u * sig * (1.0 + g * (1.0 - sig))).astype(BF)

    summed = LineScatter(
        wide, sent, from_left, from_right, t, nt, scatter_sem.shape[2], scatter_sem
    )
    for cut in range(summed.cuts):
        cols = summed.cols(cut)
        wide[:, cols] = dot(dg[...], gate_v[cols, :], 1, 1) + dot(du[...], up_v[cols, :], 1, 1)
        summed.edge(cut)

    def keep(place):
        def store(at, value):
            wide[place + at.start : place + at.stop, :hidden] = value

        return store

    def turned(at, value):
        d_down[:, at] = value.T

    scatters = []
    for w, (left, right, store) in enumerate(
        ((nf, dg, keep(0)), (nf, du, keep(shard)), (cf, act, turned))
    ):
        def chunk(d, left=left, right=right):
            return dot(left[:, pl.ds(pl.multiple_of(d * shard, shard), shard)], right[...], 0, 0)

        scatters.append(
            BlockScatter(
                chunk, given, totals.at[w], landed.at[w], store, me, width,
                hs.at[w], hr.at[w], ps.at[w], pr.at[w],
            )
        )
    s_gate, s_up, s_down = scatters
    stages = s_gate.stages

    def take(s):
        s.take()
        s.send(0)

    fills = [
        lambda: take(s_gate),
        lambda: (s_gate.given(), s_up.give()),
        lambda: take(s_up),
    ]
    s_gate.give()
    for k in range(nt - 1):
        summed.round(k)
        if fills:
            fills.pop(0)()
    for fill in fills:
        fill()

    def store_raw(cols, value):
        gh[:, cols] = value

    summed.own(store_raw)
    local = pl.ds(pl.multiple_of(t * rows, rows), rows)
    gains[...] = jnp.zeros_like(gains)

    def store(cols, value):
        total = cot[:, cols].astype(F32) + value
        gh[:, cols] = total
        branch[local, cols] = total.astype(BF)

    def store_gain(cols, value):
        gains[1:2, cols] = value

    back_through_norm(lambda c: hid[:, c], lambda c: gh[:, c], gall, 1, store, store_gain)
    line = LineGather(branch, t, nt, line_sem)
    line.start()
    s_up.given()
    s_down.give()
    take(s_down)

    def on(s, stage):
        s.add(stage)
        if stage + 1 < stages:
            s.send(stage + 1)

    fills = [functools.partial(on, s, stage) for stage in range(stages) for s in scatters]
    for s in range(1, nt):
        line.step(s)
        if fills:
            fills.pop(0)()
    for fill in fills:
        fill()
    out = [
        pltpu.make_async_copy(wide.at[pl.ds(0, shard), pl.ds(0, hidden)], d_gate, out_sem.at[0]),
        pltpu.make_async_copy(wide.at[pl.ds(shard, shard), pl.ds(0, hidden)], d_up, out_sem.at[1]),
    ]
    for copy in out:
        copy.start()
    s_down.given()
    for s in scatters:
        s.drain()
    line.finish()
    summed.finish()
    for copy in out:
        copy.wait()


def ffn(nt, nd, nf, cf, hid, cot, gall, gate_f, up_f, down_f):
    width = nd.bit_length() - 1
    rows, model = hid.shape
    tokens = nf.shape[0]
    hidden = gate_f.shape[1]
    shard = model // nd
    half = nd // 2
    shape = jax.ShapeDtypeStruct
    span = max(size for _, size in tiles_of(hidden, 6))
    outs = [
        (shape((tokens, hidden), BF), vmem()),
        (shape((tokens, model), BF), vmem()),
        (shape((rows, model), F32), vmem()),
        (shape((8, model), F32), vmem()),
        (shape((shard, hidden), F32), hbm()),
        (shape((shard, hidden), F32), hbm()),
        (shape((hidden, shard), F32), vmem()),
    ]
    scratch = scatter_scratch(tokens, nt, model)
    scratch[0] = pltpu.VMEM((max(tokens, 2 * shard), max(model, 3 * span)), F32)
    return pl.pallas_call(
        functools.partial(ffn_kernel, nt, width),
        out_shape=[o for o, _ in outs],
        in_specs=[vmem()] * 5 + [hbm()] * 3,
        out_specs=[s for _, s in outs],
        scratch_shapes=[
            pltpu.VMEM((model, hidden), BF),
            pltpu.VMEM((model, hidden), BF),
            pltpu.VMEM((hidden, model), BF),
            scratch[0],
            pltpu.VMEM((tokens, hidden), BF),
            pltpu.VMEM((tokens, hidden), BF),
        ]
        + scratch[1:]
        + [
            pltpu.VMEM((half, shard, hidden), BF),
            pltpu.VMEM((3, half, shard, hidden), BF),
            pltpu.VMEM((3, 2, half - 1, shard // 2, hidden), BF),
            dma(len(tiles_of(hidden, 6)), 3),
            dma(2),
            dma(4, nt, CUTS),
            dma(4, nt),
            dma(3, 2, half),
            dma(3, 2, half),
            dma(3, half),
            dma(3, half),
        ],
        compiler_params=pltpu.CompilerParams(
            collective_id=1, has_side_effects=True, vmem_limit_bytes=VMEM_BYTES
        ),
        name="ffn",
    )(nf, cf, hid, cot, gall, gate_f, up_f, down_f)


def attend_back_pairs(first, last, qo, gm, mo, lo, kpad, vpad, bias, cos, sin, dqkv, dkey, dval):
    rows = qo.shape[0]

    @pl.loop(first, last)
    def _(pair):
        lanes = pl.ds(pl.multiple_of(pair * LANES, LANES), LANES)
        for start, block, seen in query_cuts(rows):
            at = slice(start, start + block)
            lane = lane_index((block, LANES))
            query, grad = qo[at, lanes], gm[at, lanes]
            both = grad.astype(F32) * mo[at, lanes].astype(F32)
            logs = lo[at, :]
            dq = jnp.zeros((block, LANES), F32)
            for side in range(2):
                inside = (lane >= HD) if side else (lane < HD)
                delta = jnp.sum(jnp.where(inside, both, 0.0), axis=-1, keepdims=True)
                log = jnp.sum(
                    jnp.where(lane == 2 * pair + side, logs, 0.0), axis=-1, keepdims=True
                )
                key, value = kpad[side, :seen, :], vpad[side, :seen, :]
                probs = jnp.exp(dot(query, key, 1, 1) + bias[at, :seen] - log)
                grad_scores = (probs * (dot(grad, value, 1, 1) - delta)).astype(BF)
                dq = dq + dot(grad_scores, key)
                dkey[side, :seen, :] += dot(grad_scores, query, 0, 0)
                dval[side, :seen, :] += dot(probs.astype(BF), grad, 0, 0)
            dq = dq * HD ** (-0.5)
            dqkv[at, lanes] = (dq * cos[at, :] - swapped(dq) * sin[at, :]).astype(BF)


def back_kernel(
    nt, width,
    branch, na, mo, qo, kvo, lo, cos, sin, segc, segr, x, hid, gh, gparts, gall, act,
    wqkv_f, wo_f, down_f,
    y, gi, gain_out, d_qkv, d_wo,
    wqkv_v, wo_v, down_v, part, sent, from_left, from_right, sent2, from_left2, from_right2,
    bias, kpad, vpad, gm, dqkv, dkey, dval,
    given_q, totals_q, landed_q, given_o, totals_o, landed_o,
    gsum, zslots, dslots,
    load_sem, scatter_sem, scatter_sem2, zsem, dsem, hs, hr, ps, pr,
):
    me, t = lax.axis_index("dp"), lax.axis_index("tensor")
    nd = 1 << width
    rows, model = hid.shape
    tokens, queries = qo.shape
    shard = model >> width
    loads = [
        pltpu.make_async_copy(wo_f, wo_v, load_sem.at[0]),
        pltpu.make_async_copy(down_f, down_v, load_sem.at[1]),
        pltpu.make_async_copy(wqkv_f, wqkv_v, load_sem.at[2]),
    ]
    for load in loads:
        load.start()
    enter(t, nt, me, width, pltpu.get_barrier_semaphore(), everyone_along_tensor=True)

    bias_into(bias, segc, segr)
    pad_pair(kvo[...].astype(F32), kpad, vpad)
    dkey[...] = jnp.zeros_like(dkey)
    dval[...] = jnp.zeros_like(dval)
    loads[0].wait()
    gm[...] = dot(branch[...], wo_v[...], 1, 1).astype(BF)
    loads[1].wait()
    cuts = scatter_sem.shape[2]
    outward = LineScatter(part, sent, from_left, from_right, t, nt, cuts, scatter_sem)
    for cut in range(cuts):
        cols = outward.cols(cut)
        part[:, cols] = dot(act[...], down_v[:, cols])
        outward.edge(cut)

    pairs = queries // LANES
    steps = min(nt, pairs)
    for k in range(steps):
        attend_back_pairs(
            k * pairs // steps, (k + 1) * pairs // steps,
            qo, gm, mo, lo, kpad, vpad, bias, cos, sin, dqkv, dkey, dval,
        )
        if k < nt - 1:
            outward.round(k)
    for k in range(steps, nt - 1):
        outward.round(k)

    def store_y(cols, value):
        y[:, cols] = (hid[:, cols] + value).astype(BF)

    outward.own(store_y)
    key = dkey[0] + pltpu.roll(dkey[1], HD, 1)
    value = pltpu.roll(dval[0], HD, 1) + dval[1]
    key = key * cos[...] - swapped(key) * sin[...]
    dqkv[:, queries : queries + LANES] = jnp.where(
        lane_index(key.shape) < HD, key, value
    ).astype(BF)

    loads[2].wait()
    inward = LineScatter(part, sent2, from_left2, from_right2, t, nt, cuts, scatter_sem2)
    for cut in range(cuts):
        cols = inward.cols(cut)
        part[:, cols] = dot(dqkv[...], wqkv_v[cols, :], 1, 1)
        inward.edge(cut)

    def chunk_of(left, right):
        def chunk(d):
            return dot(left[:, pl.ds(pl.multiple_of(d * shard, shard), shard)], right[...], 0, 0)

        return chunk

    def store_qkv(at, value):
        d_qkv[at, :] = value

    def store_wo(at, value):
        d_wo[:, at] = value.T

    s_qkv = BlockScatter(
        chunk_of(na, dqkv), given_q, totals_q, landed_q, store_qkv, me, width,
        hs.at[0], hr.at[0], ps.at[0], pr.at[0],
    )
    s_out = BlockScatter(
        chunk_of(branch, mo), given_o, totals_o, landed_o, store_wo, me, width,
        hs.at[1], hr.at[1], ps.at[1], pr.at[1],
    )
    stages = s_qkv.stages

    def take(s):
        s.take()
        s.send(0)

    def on(s, stage):
        s.add(stage)
        if stage + 1 < stages:
            s.send(stage + 1)

    fills = [
        lambda: (take(s_qkv), s_out.give()),
        lambda: take(s_out),
        lambda: None,
    ]
    fills += [functools.partial(on, s, stage) for stage in range(stages) for s in (s_qkv, s_out)]
    s_qkv.give()
    for k in range(nt - 1):
        inward.round(k)
        if fills:
            fills.pop(0)()
    for fill in fills:
        fill()

    def store_raw(cols, value):
        gi[:, cols] = value

    inward.own(store_raw)
    gsum[...] = gparts[...]

    def store(cols, value):
        gi[:, cols] = gh[:, cols] + value

    def store_gain(cols, value):
        gsum[0:1, cols] = value

    back_through_norm(
        lambda c: x[:, c].astype(F32), lambda c: gi[:, c], gall, 0, store, store_gain
    )

    zslots[t] = gsum[...]

    def along(step):
        return remote(
            zslots.at[t], zslots.at[t], zsem.at[0, step], zsem.at[1, step],
            {"tensor": lax.rem(t + step, nt)},
        )

    for step in range(1, nt):
        along(step).start()
    for step in range(1, nt):
        slot = zslots.at[lax.rem(t + nt - step, nt)]
        remote(
            slot, slot, zsem.at[0, step], zsem.at[1, step], {"tensor": lax.rem(t + step, nt)}
        ).wait_recv()
    gsum[...] = sum(zslots[i] for i in range(nt))

    def across(mask):
        peer = flip(me, mask, width)
        return remote(
            gsum.at[:, pl.ds(pl.multiple_of(peer * shard, shard), shard)], dslots.at[me],
            dsem.at[0, mask], dsem.at[1, mask], {"dp": peer},
        )

    for mask in range(1, nd):
        across(mask).start()
    dslots[me] = gsum[:, pl.ds(pl.multiple_of(me * shard, shard), shard)]
    for mask in range(1, nd):
        peer = flip(me, mask, width)
        slot = dslots.at[peer]
        remote(slot, slot, dsem.at[0, mask], dsem.at[1, mask], {"dp": peer}).wait_recv()
    gain_out[...] = sum(dslots[i] for i in range(nd))

    for step in range(1, nt):
        along(step).wait_send()
    for mask in range(1, nd):
        across(mask).wait_send()
    for s in (s_qkv, s_out):
        s.given()
        s.drain()
    outward.finish()
    inward.finish()


def back(nt, nd, branch, na, mo, qo, kvo, lo, cos, sin, segc, segr, x, hid, gh, gparts, gall, act, wqkv_f, wo_f, down_f):
    width = nd.bit_length() - 1
    rows, model = hid.shape
    tokens, queries = qo.shape
    hidden = down_f.shape[0]
    wide = wqkv_f.shape[1]
    shard = model // nd
    half = nd // 2
    shape = jax.ShapeDtypeStruct
    outs = [
        shape((rows, model), BF),
        shape((rows, model), F32),
        shape((8, shard), F32),
        shape((shard, wide), F32),
        shape((queries, shard), F32),
    ]
    scratch = scatter_scratch(tokens, nt, model)
    cube = lambda size: [
        pltpu.VMEM((half, shard, size), BF),
        pltpu.VMEM((half, shard, size), BF),
        pltpu.VMEM((2, half - 1, shard // 2, size), BF),
    ]
    return pl.pallas_call(
        functools.partial(back_kernel, nt, width),
        out_shape=outs,
        in_specs=[vmem()] * 16 + [hbm()] * 3,
        out_specs=[vmem()] * len(outs),
        scratch_shapes=[
            pltpu.VMEM((model, wide), BF),
            pltpu.VMEM((queries, model), BF),
            pltpu.VMEM((hidden, model), BF),
        ]
        + scratch
        + scratch[1:]
        + [
            pltpu.VMEM((tokens, tokens), F32),
            pltpu.VMEM((2, tokens, LANES), BF),
            pltpu.VMEM((2, tokens, LANES), BF),
            pltpu.VMEM((tokens, queries), BF),
            pltpu.VMEM((tokens, wide), BF),
            pltpu.VMEM((2, tokens, LANES), F32),
            pltpu.VMEM((2, tokens, LANES), F32),
        ]
        + cube(wide)
        + cube(queries)
        + [
            pltpu.VMEM((8, model), F32),
            pltpu.VMEM((nt, 8, model), F32),
            pltpu.VMEM((nd, 8, shard), F32),
            dma(3),
            dma(4, nt, CUTS),
            dma(4, nt, CUTS),
            dma(2, nt),
            dma(2, nd),
            dma(2, 2, half),
            dma(2, 2, half),
            dma(2, half),
            dma(2, half),
        ],
        compiler_params=pltpu.CompilerParams(
            collective_id=2, has_side_effects=True, vmem_limit_bytes=VMEM_BYTES
        ),
        name="back",
    )(branch, na, mo, qo, kvo, lo, cos, sin, segc, segr, x, hid, gh, gparts, gall, act, wqkv_f, wo_f, down_f)


def narrow_scatter(value, axis, scatter_dimension, tiled):
    low = value.astype(BF) if value.ndim == 2 else value
    return lax.psum_scatter(low, axis, scatter_dimension=scatter_dimension, tiled=tiled).astype(F32)


def rope_tables(segments, head_dim):
    row_count = segments.shape[0]
    row_index = jnp.arange(row_count, dtype=jnp.int32)
    change = jnp.concatenate(
        [jnp.ones((1,), jnp.int32), (segments[1:] != segments[:-1]).astype(jnp.int32)]
    )
    starts = lax.cummax(jnp.where(change > 0, row_index, jnp.zeros_like(row_index)), axis=0)
    position = (row_index - starts).astype(F32)
    half_dim = head_dim // 2
    frequency = jnp.exp(jnp.arange(half_dim, dtype=F32) * (-math.log(10000.0) / half_dim))
    angles = position[:, None] * frequency[None, :]
    return (jnp.cos(angles)[:, None, :], jnp.sin(angles)[:, None, :])


def rotate(tensor, cosine, sine):
    half_dim = tensor.shape[-1] // 2
    first_half = tensor[..., :half_dim]
    second_half = tensor[..., half_dim:]
    return jnp.concatenate(
        [first_half * cosine - second_half * sine, second_half * cosine + first_half * sine],
        axis=-1,
    )


def unrotate(tensor, cosine, sine):
    half_dim = tensor.shape[-1] // 2
    first_half = tensor[..., :half_dim]
    second_half = tensor[..., half_dim:]
    return jnp.concatenate(
        [first_half * cosine + second_half * sine, second_half * cosine - first_half * sine],
        axis=-1,
    )


def visible(segments):
    row_index = jnp.arange(segments.shape[0], dtype=jnp.int32)
    same_seq = segments[:, None] == segments[None, :]
    return same_seq & (row_index[:, None] >= row_index[None, :])


def normalize(values, gain):
    inverse = lax.rsqrt(jnp.mean(values * values, axis=-1, keepdims=True) + EPSILON)
    unit_rows = values * inverse
    return (unit_rows, inverse, (unit_rows * gain.astype(F32)).astype(BF))


def normalize_back(grad_normed, unit_rows, inverse, gain):
    scaled = grad_normed * gain.astype(F32)
    grad_values = inverse * (
        scaled - unit_rows * jnp.mean(scaled * unit_rows, axis=-1, keepdims=True)
    )
    return (grad_values, jnp.sum(grad_normed * unit_rows, axis=0))


def contract(left, right, left_dim, right_dim):
    return lax.dot_general(
        left, right, (((left_dim,), (right_dim,)), ((), ())), preferred_element_type=F32
    )


def block_scores(query_block, key_heads, allowed_block, score_scale):
    scores = (
        jnp.einsum("rkgd,skd->kgrs", query_block, key_heads, preferred_element_type=F32)
        * score_scale
    )
    return jnp.where(allowed_block[None, None], scores, NEGATIVE)


def attend_forward(query_groups, key_heads, value_heads, allowed, score_scale):
    scores = block_scores(query_groups, key_heads, allowed, score_scale)
    row_max = jnp.max(scores, axis=-1, keepdims=True)
    log_total = row_max + jnp.log(jnp.sum(jnp.exp(scores - row_max), axis=-1, keepdims=True))
    probs_low = jnp.exp(scores - log_total).astype(BF)
    mixed_parts = jnp.einsum(
        "kgrs,skd->rkgd", probs_low, value_heads, preferred_element_type=F32
    ).astype(BF)
    return (mixed_parts, log_total)


def attend_backward(
    query_groups, key_heads, value_heads, mixed_heads, grad_mixed, log_totals, allowed, score_scale
):
    scores = block_scores(query_groups, key_heads, allowed, score_scale)
    attn_probs = jnp.exp(scores - log_totals)
    probs_low = attn_probs.astype(BF)
    grad_probs = jnp.einsum(
        "rkgd,skd->kgrs", grad_mixed, value_heads, preferred_element_type=F32
    )
    row_delta = jnp.sum(grad_mixed.astype(F32) * mixed_heads.astype(F32), axis=-1)
    row_delta = jnp.transpose(row_delta, (1, 2, 0))[..., None]
    grad_scores = (attn_probs * (grad_probs - row_delta)).astype(BF)
    query_parts = (
        jnp.einsum("kgrs,skd->rkgd", grad_scores, key_heads, preferred_element_type=F32)
        * score_scale
    )
    grad_key_rot = (
        jnp.einsum("kgrs,rkgd->skd", grad_scores, query_groups, preferred_element_type=F32)
        * score_scale
    )
    grad_value_heads = jnp.einsum(
        "kgrs,rkgd->skd", probs_low, grad_mixed, preferred_element_type=F32
    )
    return (query_parts, grad_key_rot, grad_value_heads)


def plain_device(
    layer_input,
    segment_ids,
    norm_attn,
    w_query,
    w_key,
    w_value,
    w_output,
    norm_ffn,
    w_gate,
    w_up,
    w_down,
    cotangent,
):
    score_scale = HD ** (-0.5)
    query_full, key_full, value_full, output_full, gain_attn = (
        lax.all_gather(w_query, "dp", axis=0, tiled=True),
        lax.all_gather(w_key, "dp", axis=0, tiled=True),
        lax.all_gather(w_value, "dp", axis=0, tiled=True),
        lax.all_gather(w_output, "dp", axis=1, tiled=True),
        lax.all_gather(norm_attn, "dp", axis=0, tiled=True),
    )
    gate_full, up_full, down_full, gain_ffn = (
        lax.all_gather(w_gate, "dp", axis=0, tiled=True),
        lax.all_gather(w_up, "dp", axis=0, tiled=True),
        lax.all_gather(w_down, "dp", axis=1, tiled=True),
        lax.all_gather(norm_ffn, "dp", axis=0, tiled=True),
    )
    heads_local = query_full.shape[1] // HD
    kv_local = key_full.shape[1] // HD
    group = heads_local // kv_local
    residual_in = layer_input.astype(F32)
    unit_attn, inverse_attn, normed_local = normalize(residual_in, gain_attn)
    normed_attn = lax.all_gather(normed_local, "tensor", axis=0, tiled=True)
    row_count = normed_attn.shape[0]
    cosine, sine = rope_tables(segment_ids, HD)
    allowed = visible(segment_ids)
    query_heads = rotate(
        jnp.dot(normed_attn, query_full, preferred_element_type=F32).reshape(
            row_count, heads_local, HD
        ),
        cosine,
        sine,
    ).astype(BF)
    query_groups = query_heads.reshape(row_count, kv_local, group, HD)
    key_heads = rotate(
        jnp.dot(normed_attn, key_full, preferred_element_type=F32).reshape(
            row_count, kv_local, HD
        ),
        cosine,
        sine,
    ).astype(BF)
    value_heads = (
        jnp.dot(normed_attn, value_full, preferred_element_type=F32)
        .astype(BF)
        .reshape(row_count, kv_local, HD)
    )
    mixed_heads, log_totals = attend_forward(
        query_groups, key_heads, value_heads, allowed, score_scale
    )
    mixed_flat = mixed_heads.reshape(row_count, heads_local * HD)
    hidden_res = residual_in + narrow_scatter(
        jnp.dot(mixed_flat, output_full, preferred_element_type=F32),
        "tensor",
        scatter_dimension=0,
        tiled=True,
    )
    unit_ffn, inverse_ffn, normed_ffn_local = normalize(hidden_res, gain_ffn)
    normed_ffn = lax.all_gather(normed_ffn_local, "tensor", axis=0, tiled=True)
    gate_rows = jnp.dot(normed_ffn, gate_full, preferred_element_type=F32)
    up_rows = jnp.dot(normed_ffn, up_full, preferred_element_type=F32)
    sigmoid_gate = jax.nn.sigmoid(gate_rows)
    active = (gate_rows * sigmoid_gate * up_rows).astype(BF)
    layer_output = (
        hidden_res
        + narrow_scatter(
            jnp.dot(active, down_full, preferred_element_type=F32).astype(BF),
            "tensor",
            scatter_dimension=0,
            tiled=True,
        ).astype(F32)
    ).astype(BF)
    query_full, key_full, value_full, output_full, gate_full, up_full, down_full = (
        lax.all_gather(w_query, "dp", axis=0, tiled=True),
        lax.all_gather(w_key, "dp", axis=0, tiled=True),
        lax.all_gather(w_value, "dp", axis=0, tiled=True),
        lax.all_gather(w_output, "dp", axis=1, tiled=True),
        lax.all_gather(w_gate, "dp", axis=0, tiled=True),
        lax.all_gather(w_up, "dp", axis=0, tiled=True),
        lax.all_gather(w_down, "dp", axis=1, tiled=True),
    )
    cotangent_full = lax.all_gather(cotangent, "tensor", axis=0, tiled=True)
    grad_active = contract(cotangent_full, down_full, 1, 1)
    grad_w_down = contract(active, cotangent_full, 0, 0)
    grad_up_rows = (grad_active * gate_rows * sigmoid_gate).astype(BF)
    grad_gate_rows = (
        grad_active * up_rows * sigmoid_gate * (1.0 + gate_rows * (1.0 - sigmoid_gate))
    ).astype(BF)
    grad_w_gate = contract(normed_ffn, grad_gate_rows, 0, 0)
    grad_w_up = contract(normed_ffn, grad_up_rows, 0, 0)
    grad_normed_ffn = narrow_scatter(
        contract(grad_gate_rows, gate_full, 1, 1) + contract(grad_up_rows, up_full, 1, 1),
        "tensor",
        scatter_dimension=0,
        tiled=True,
    )
    grad_hidden, gain_ffn_part = normalize_back(grad_normed_ffn, unit_ffn, inverse_ffn, gain_ffn)
    grad_hidden = cotangent.astype(F32) + grad_hidden
    branch_full = lax.all_gather(grad_hidden.astype(BF), "tensor", axis=0, tiled=True)
    grad_mixed = contract(branch_full, output_full, 1, 1).astype(BF)
    grad_w_output = contract(mixed_flat, branch_full, 0, 0)
    grad_query_rot, grad_key_rot, grad_value_heads = attend_backward(
        query_groups,
        key_heads,
        value_heads,
        mixed_heads,
        grad_mixed.reshape(row_count, kv_local, group, HD),
        log_totals,
        allowed,
        score_scale,
    )
    grad_queries = (
        unrotate(grad_query_rot.reshape(row_count, heads_local, HD), cosine, sine)
        .reshape(row_count, heads_local * HD)
        .astype(BF)
    )
    grad_keys = (
        unrotate(grad_key_rot, cosine, sine).reshape(row_count, kv_local * HD).astype(BF)
    )
    grad_values = grad_value_heads.reshape(row_count, kv_local * HD).astype(BF)
    grad_w_query = contract(normed_attn, grad_queries, 0, 0)
    grad_w_key = contract(normed_attn, grad_keys, 0, 0)
    grad_w_value = contract(normed_attn, grad_values, 0, 0)
    grad_normed_attn = narrow_scatter(
        contract(grad_queries, query_full, 1, 1)
        + contract(grad_keys, key_full, 1, 1)
        + contract(grad_values, value_full, 1, 1),
        "tensor",
        scatter_dimension=0,
        tiled=True,
    )
    grad_residual, gain_attn_part = normalize_back(
        grad_normed_attn, unit_attn, inverse_attn, gain_attn
    )
    grad_input = grad_hidden + grad_residual
    gain_attn_total, gain_ffn_total = lax.psum((gain_attn_part, gain_ffn_part), "tensor")
    owned = (
        narrow_scatter(grad_w_query, "dp", scatter_dimension=0, tiled=True),
        narrow_scatter(grad_w_key, "dp", scatter_dimension=0, tiled=True),
        narrow_scatter(grad_w_value, "dp", scatter_dimension=0, tiled=True),
        narrow_scatter(grad_w_output, "dp", scatter_dimension=1, tiled=True),
        narrow_scatter(gain_attn_total, "dp", scatter_dimension=0, tiled=True),
        narrow_scatter(gain_ffn_total, "dp", scatter_dimension=0, tiled=True),
        narrow_scatter(grad_w_gate, "dp", scatter_dimension=0, tiled=True),
        narrow_scatter(grad_w_up, "dp", scatter_dimension=0, tiled=True),
        narrow_scatter(grad_w_down, "dp", scatter_dimension=1, tiled=True),
    )
    return (
        layer_output,
        grad_input,
        owned[4],
        owned[0],
        owned[1],
        owned[2],
        owned[3],
        owned[5],
        owned[6],
        owned[7],
        owned[8],
    )


def with_kernels(nt, nd, layer_input, segment_ids, norm_attn, w_query, w_key, w_value, w_output, norm_ffn, w_gate, w_up, w_down, cotangent):
    gain = jnp.pad(jnp.stack([norm_attn, norm_ffn]).astype(F32), ((0, 6), (0, 0)))
    wqkv = jnp.concatenate([w_query, w_key, w_value], axis=1)
    segc, segr = segment_ids[:, None], segment_ids[None, :]
    (wqkv_f, wo_f, gate_f, up_f, down_f, na, cf, nf, qo, kvo, mo, lo, hid, gall, cos, sin) = front(
        nt, nd, layer_input, cotangent, gain, segc, segr, wqkv, w_output, w_gate, w_up, w_down
    )
    act, branch, gh, gparts, d_gate, d_up, d_down = ffn(
        nt, nd, nf, cf, hid, cotangent, gall, gate_f, up_f, down_f
    )
    y, gi, gains, d_qkv, d_wo = back(
        nt, nd, branch, na, mo, qo, kvo, lo, cos, sin, segc, segr, layer_input, hid, gh, gparts,
        gall, act, wqkv_f, wo_f, down_f,
    )
    q, k = w_query.shape[1], w_query.shape[1] + w_key.shape[1]
    return (
        y, gi, gains[0], d_qkv[:, :q], d_qkv[:, q:k], d_qkv[:, k:], d_wo, gains[1], d_gate, d_up, d_down
    )


def fits(nt, nd, shards):
    layer_input, segment_ids, norm_attn, w_query, w_key, w_value, w_output, norm_ffn, w_gate, w_up, w_down, _ = shards
    return (
        nd >= 4
        and nd & (nd - 1) == 0
        and nt >= 2
        and norm_attn.shape[0] % LANES == 0
        and w_output.shape[1] % LANES == 0
        and w_gate.shape[1] % LANES == 0
        and w_query.shape[1] % LANES == 0
        and w_key.shape[1] == HD
        and segment_ids.shape[0] == nt * layer_input.shape[0]
        and segment_ids.shape[0] % LANES == 0
    )


def on_device(nt, nd, *shards):
    if fits(nt, nd, shards):
        return with_kernels(nt, nd, *shards)
    return plain_device(*shards)


def solution(mesh):
    placed = (
        P(("dp", "tensor"), None),
        P("dp"),
        P("dp"),
        P("dp", "tensor"),
        P("dp", "tensor"),
        P("dp", "tensor"),
        P("tensor", "dp"),
        P("dp"),
        P("dp", "tensor"),
        P("dp", "tensor"),
        P("tensor", "dp"),
        P(("dp", "tensor"), None),
    )
    return jax.shard_map(
        functools.partial(on_device, mesh.shape["tensor"], mesh.shape["dp"]),
        mesh=mesh,
        in_specs=placed,
        out_specs=(
            P(("dp", "tensor"), None),
            P(("dp", "tensor"), None),
            P("dp"),
            P("dp", "tensor"),
            P("dp", "tensor"),
            P("dp", "tensor"),
            P("tensor", "dp"),
            P("dp"),
            P("dp", "tensor"),
            P("dp", "tensor"),
            P("tensor", "dp"),
        ),
        check_vma=False,
    )
```

time: 1210 us -> 448 us (0.37)
  waiting for transfers between devices: 955 us -> 0 us
  Pallas kernels: 0 us -> 421 us
  matrix products: 123 us -> 0 us
  blocking collectives: 75 us -> 0 us
  other arithmetic: 19.8 us -> 2.38 us
  between operations: 16.1 us -> 1.16 us
    reduce_scatter x11 -> x0, waiting for transfers between devices: 631 us -> none  [the longest x1 91.1 us: on_device(): lax.psum_scatter(grad_w_gate, 'dp', scatter_dimension=0, tiled=True)]
    pallas_call x0 -> x3, Pallas kernels: none -> 421 us  [the longest x1 157 us: front(): pl.pallas_call(functools.partial(front_kernel, nt, width), out_shape=[o f...]
    all_gather x9 -> x0, waiting for transfers between devices: 319 us -> none  [the longest x1 47.7 us: on_device(): normed_ffn = lax.all_gather(normed_ffn_local, 'tensor', axis=0, tiled=True)]
    dot_general x27 -> x0, matrix products: 123 us -> none  [the longest x14 71.2 us: contract(): lax.dot_general(left, right, (((left_dim,), (right_dim,)), ((), ())), pre...]
    all_gather x4 -> x0, blocking collectives: 38.6 us -> none  [the longest x1 10.4 us: on_device(): lax.all_gather(norm_attn, 'dp', axis=0, tiled=True)]
    unnamed x1 -> x0, blocking collectives: 24.5 us -> none
  transfers between devices with their start and end apart: 20 -> 0, of which waited for: 20 -> 0; matrix products, arithmetic and copies ran while one was open for 7% -> 0% of each run, Pallas kernels for 0% -> 0%
where the time goes in v1:
time: 448 us; the launch traced here: 441 us
  Pallas kernels  421 us (94%)
  local copies, waits for them, and re-layouts  17.1 us (4%)
    pallas_call x1, Pallas kernels, front(): pl.pallas_call(functools.partial(front_kernel, nt, width), out_shape=[o f...  157 us
    pallas_call x1, Pallas kernels, back(): pl.pallas_call(functools.partial(back_kernel, nt, width), out_shape=outs,...  137 us
    pallas_call x1, Pallas kernels, ffn(): pl.pallas_call(functools.partial(ffn_kernel, nt, width), out_shape=[o for...  127 us
    unnamed x22, local copies, waits for them, and re-layouts  9.83 us

profile of v1, /device:TPU:0, one launch (start us, length us, event | category | flops | bytes accessed | tf_op | source)
XLA Modules:
  0.0 441.5 jit_solution(2375664299337706321)
XLA Ops:
  0.6 0.7 stack.9
  1.3 0.7 stack.10
  2.0 0.6 fusion.3.gain
  2.6 0.9 copy.27
  3.4 0.9 copy.28
  4.3 1.8 pad_maximum_fusion.wqkv
  6.1 1.5 copy.29.segc
  7.6 157.2 %front.1 = (bf16[2048,640]{1,0:T(8,128)(2,1)}, bf16[512,2048]{1,0:T(8,128)(2,1)}, bf16[2048,1408]{1,0:T(8,128)(2,1)}, bf16[2048,1408]{1,0:T(8,128)(2,1)}, bf16[1...) custom-call(bf16[128,2048]{1,0:T(8,128)(2,1)} %x.5, ...), custom_call_target="tpu_custom_call" | custom-call | tf_op jit(solution)/shard_map/front/pallas_call | solution.py:708
  164.8 127.1 %ffn.1 = (bf16[512,1408]{1,0:T(8,128)(2,1)}, bf16[512,2048]{1,0:T(8,128)(2,1)}, f32[128,2048]{1,0:T(8,128)}, f32[8,2048]{1,0:T(8,128)}, f32[256,1408]{1,0:T(8,12...) custom-call(bf16[512,2048]{1,0:T(8,128)(2,1)} %get-tuple-element.39.nf, bf16[512,2048]{1,0:T(8,128)(2,1)} %get-tuple-element.40.cf, ...), custom_call_target="tpu_custom_call" | custom-call | tf_op jit(solution)/shard_map/ffn/pallas_call | solution.py:923
  291.9 136.6 %back.1 = (bf16[128,2048]{1,0:T(8,128)(2,1)}, f32[128,2048]{1,0:T(8,128)}, f32[8,256]{1,0:T(8,128)}, f32[256,640]{1,0:T(8,128)}, f32[512,256]{1,0:T(8,128)}) custom-call(bf16[512,2048]{1,0:T(8,128)(2,1)} %get-tuple-element.46.branch, bf16[512,2048]{1,0:T(8,128)(2,1)} %get-tuple-element.47.na, bf16[512,512]{1,0:T(8,128)(2,1)} %get-tuple-element.48.mo, ...), custom_call_target="tpu_custom_call" | custom-call | tf_op jit(solution)/shard_map/back/pallas_call | solution.py:1182
  428.5 0.0 copy-start.5
  428.5 0.0 copy-start.3
  428.5 1.4 fusion.5
  429.9 1.1 fusion.4
  431.0 0.0 copy-start.4
  431.0 1.9 slice.16
  433.0 0.7 copy.32
  433.7 0.7 copy.31
  434.4 0.0 copy-done.5
  434.4 0.0 copy-start.2
  434.4 0.8 copy.39
  435.2 0.0 copy-done.3
  435.2 1.0 copy.40
  436.2 0.0 copy-done.4
  436.2 0.0 copy-start.1
  436.2 0.8 copy.41
  437.0 0.0 copy-done.2
  437.0 1.1 copy.42
  438.1 0.0 copy-done.1
  438.1 1.1 copy.43
  439.2 0.8 copy-done
  439.9 1.1 copy.44
  (1 shorter events, 0.0 us)
Async XLA Ops:
  428.5 5.9 %copy-start.5 = (bf16[128,2048]{1,0:T(8,128)(2,1)S(1)}, bf16[128,2048]{1,0:T(8,128)(2,1)}, u32[]{:S(2)}) copy-start(bf16[128,2048]{1,0:T(8,128)(2,1)} %get-tuple-element.104) | copy-start | bytes 1572868
  428.5 6.7 %copy-start.3 = (f32[128,2048]{1,0:T(8,128)S(1)}, f32[128,2048]{1,0:T(8,128)}, u32[]{:S(2)}) copy-start(f32[128,2048]{1,0:T(8,128)} %get-tuple-element.105) | copy-start | bytes 3145732
  431.0 5.1 %copy-start.4 = (f32[512,256]{1,0:T(8,128)S(1)}, f32[512,256]{1,0:T(8,128)}, u32[]{:S(2)}) copy-start(f32[512,256]{1,0:T(8,128)} %get-tuple-element.110) | copy-start | bytes 1572868
  434.4 2.6 copy-start.2
  436.2 1.9 copy-start.1
  438.1 1.9 copy-start

commit v2 on v0

v2 whole, which is shorter than its diff:
```python
import functools
import math

import jax
import jax.numpy as jnp
from jax import lax
from jax.experimental import pallas as pl
from jax.experimental.pallas import tpu as pltpu
from jax.sharding import PartitionSpec as P

HD = 64
EPSILON = 1e-05
NEGATIVE = -1e30
LANES = 128
BF = jnp.bfloat16
F32 = jnp.float32
VMEM_BYTES = 66_000_000


def spans(bits):
    masks = [0]
    for bit in bits:
        masks = masks + [mask | (1 << bit) for mask in masks]
    return masks


def flip(index, mask, width):
    total = 0
    for bit in range(width):
        own = lax.rem(lax.div(index, 1 << bit), 2)
        if isinstance(mask, int):
            other = (mask >> bit) & 1
        else:
            other = lax.rem(lax.div(mask, 1 << bit), 2)
        total = total + lax.rem(own + other, 2) * (1 << bit)
    return total


def aligned(value, step):
    return value if isinstance(value, int) else pl.multiple_of(value, step)


def remote(src, dst, send_sem, recv_sem, device):
    return pltpu.make_async_remote_copy(
        src_ref=src,
        dst_ref=dst,
        send_sem=send_sem,
        recv_sem=recv_sem,
        device_id=device,
        device_id_type=pl.DeviceIdType.MESH,
    )


def dot(left, right, left_dim=1, right_dim=0):
    return lax.dot_general(
        left, right, (((left_dim,), (right_dim,)), ((), ())), preferred_element_type=F32
    )


def tiles_of(size, most):
    units = size // LANES
    parts = -(-units // most)
    cuts, start = [], 0
    for part in range(parts):
        width = (units // parts + (1 if part < units % parts else 0)) * LANES
        cuts.append((start, width))
        start += width
    return cuts


def enter(t, nt, me, width, barrier, everyone_along_tensor=False):
    signal = functools.partial(
        pl.semaphore_signal, barrier, inc=1, device_id_type=pl.DeviceIdType.MESH
    )
    for mask in range(1, 1 << width):
        signal(device_id={"dp": flip(me, mask, width)})
    if everyone_along_tensor:
        for step in range(1, nt):
            signal(device_id={"tensor": lax.rem(t + step, nt)})
        pl.semaphore_wait(barrier, (1 << width) - 1 + nt - 1)
        return

    @pl.when(t > 0)
    def _():
        signal(device_id={"tensor": t - 1})

    @pl.when(t < nt - 1)
    def _():
        signal(device_id={"tensor": t + 1})

    neighbours = lax.min(t, 1) + lax.min(nt - 1 - t, 1)
    pl.semaphore_wait(barrier, (1 << width) - 1 + neighbours)


class LineGather:
    def __init__(self, full, row, size, t, nt, sems):
        self.full, self.row, self.size = full, row, size
        self.t, self.nt, self.sems = t, nt, sems
        self.pieces = sems.shape[2]

    def window(self, j, s):
        return self.full.at[pl.ds(aligned(self.row(j, s), self.size), self.size), :]

    def right(self, j, s):
        at = self.window(j, s)
        return remote(
            at, at, self.sems.at[0, j, s], self.sems.at[2, j, s],
            {"tensor": lax.rem(self.t + 1, self.nt)},
        )

    def left(self, j, s):
        at = self.window(j, s)
        return remote(
            at, at, self.sems.at[1, j, s], self.sems.at[3, j, s],
            {"tensor": lax.rem(self.t + self.nt - 1, self.nt)},
        )

    def start(self, s):
        @pl.when(self.t < self.nt - 1)
        def _():
            self.right(self.t, s).start()

        @pl.when(self.t > 0)
        def _():
            self.left(self.t, s).start()

    def step(self, k, s):
        t, nt = self.t, self.nt

        @pl.when(t >= k)
        def _():
            self.right(t - k, s).wait_recv()

            @pl.when(t < nt - 1)
            def _():
                self.right(t - k, s).start()

        @pl.when(t + k < nt)
        def _():
            self.left(t + k, s).wait_recv()

            @pl.when(t > 0)
            def _():
                self.left(t + k, s).start()

    def finish(self):
        t, nt = self.t, self.nt

        @pl.loop(0, nt)
        def _(k):
            for s in range(self.pieces):
                @pl.when((t >= k) & (t < nt - 1))
                def _():
                    self.right(t - k, s).wait_send()

                @pl.when((t + k < nt) & (t > 0))
                def _():
                    self.left(t + k, s).wait_send()


class LineScatter:
    def __init__(self, part, row, sent, arrived, t, nt, sems):
        self.part, self.row, self.sent, self.arrived = part, row, sent, arrived
        self.t, self.nt, self.sems = t, nt, sems
        self.pieces = sems.shape[3]
        self.size = sent.shape[1] // self.pieces
        self.model = sent.shape[2]
        self.near = lax.div(2 * t, nt)
        self.far = 1 - self.near

    def sub(self, s):
        return pl.ds(s * self.size, self.size)

    def depth(self, way):
        return (1 - way) * self.t + way * (self.nt - 1 - self.t)

    def goal(self, way, i):
        return (1 - way) * (self.nt - 1 - i) + way * i

    def move(self, way, j, s):
        return remote(
            self.sent.at[j, self.sub(s), :], self.arrived.at[way, j, self.sub(s), :],
            self.sems.at[0, way, j, s], self.sems.at[1, way, j, s],
            {"tensor": lax.rem(self.t + self.nt + 1 - 2 * way, self.nt)},
        )

    def rows(self, j, s):
        return pl.ds(aligned(self.row(j, s), self.size), self.size)

    def mine(self, j, s):
        return self.part[self.rows(j, s), : self.model]

    def edge(self, s):
        t, nt = self.t, self.nt

        @pl.when((t == 0) | (t == nt - 1))
        def _():
            way = lax.div(t, nt - 1)

            @pl.loop(0, nt - 1)
            def _(i):
                j = self.goal(way, i)
                self.sent[j, self.sub(s), :] = self.mine(j, s).astype(BF)
                self.move(way, j, s).start()

    def relay(self, way, s):
        depth = self.depth(way)

        @pl.when(depth > 0)
        def _():
            @pl.loop(0, self.nt - 1 - depth)
            def _(i):
                j = self.goal(way, i)
                self.move(way, j, s).wait_recv()
                total = self.mine(j, s) + self.arrived[way, j, self.sub(s), :].astype(F32)
                self.sent[j, self.sub(s), :] = total.astype(BF)
                self.move(way, j, s).start()

    def own(self, s):
        t = self.t
        rows = self.rows(t, s)
        for way in (self.near, self.far):
            @pl.when(self.depth(way) > 0)
            def _():
                self.move(way, t, s).wait_recv()
                self.part[rows, : self.model] += self.arrived[way, t, self.sub(s), :].astype(F32)

        return rows

    def finish(self):
        for way in range(2):
            @pl.loop(0, self.nt - 1 - self.depth(way))
            def _(i):
                for s in range(self.pieces):
                    self.move(way, self.goal(way, i), s).wait_send()


class Cube:
    def setup(self, me, width, half_send, half_recv, pair_send, pair_recv):
        self.me, self.width = me, width
        self.hs, self.hr, self.ps, self.pr = half_send, half_recv, pair_send, pair_recv
        self.bits = list(range(1, width))
        self.orders = (self.bits, self.bits[::-1])
        self.masks = spans(self.bits)
        self.stages = len(self.bits)

    def at(self, mask):
        return flip(self.me, mask, self.width)


class BlockGather(Cube):
    def __init__(self, own, full, by_rows, me, width, *sems):
        self.setup(me, width, *sems)
        self.own_ref, self.full, self.by_rows = own, full, by_rows

    def half(self, h):
        rows = self.own_ref.shape[0] // 2
        return self.own_ref.at[pl.ds(h * rows, rows), :]

    def window(self, who, h=None):
        rows, cols = self.own_ref.shape
        take, start = (rows, 0) if h is None else (rows // 2, h * (rows // 2))
        if self.by_rows:
            return self.full.at[pl.ds(aligned(who * rows + start, take), take), :]
        return self.full.at[pl.ds(start, take), pl.ds(aligned(who * cols, cols), cols)]

    def hop(self, stage, h, m):
        order = self.orders[h]
        bit = 1 << order[stage]
        slot = (m | bit) >> 1
        src = self.half(h) if m == 0 else self.window(self.at(m), h)
        return remote(
            src, self.window(self.at(m), h), self.hs.at[h, slot], self.hr.at[h, slot],
            {"dp": self.at(bit)},
        )

    def send(self, stage):
        for h in range(2):
            for m in spans(self.orders[h][:stage]):
                self.hop(stage, h, m).start()

    def wait(self, stage):
        for h in range(2):
            bit = 1 << self.orders[h][stage]
            for m in spans(self.orders[h][:stage]):
                slot = (m | bit) >> 1
                landed = self.window(self.at(m | bit), h)
                remote(
                    landed, landed, self.hs.at[h, slot], self.hr.at[h, slot], {"dp": self.at(bit)}
                ).wait_recv()

    def pair(self, m):
        src = self.own_ref if m == 0 else self.window(self.at(m))
        return remote(
            src, self.window(self.at(m)), self.ps.at[m >> 1], self.pr.at[m >> 1],
            {"dp": self.at(1)},
        )

    def pair_send(self):
        for m in self.masks:
            self.pair(m).start()

    def pair_wait(self):
        for m in self.masks:
            landed = self.window(self.at(m | 1))
            remote(
                landed, landed, self.ps.at[m >> 1], self.pr.at[m >> 1], {"dp": self.at(1)}
            ).wait_recv()

    def place(self, sem):
        return pltpu.make_async_copy(self.own_ref, self.window(self.me), sem)

    def drain(self):
        for stage in range(self.stages):
            for h in range(2):
                for m in spans(self.orders[h][:stage]):
                    self.hop(stage, h, m).wait_send()
        for m in self.masks:
            self.pair(m).wait_send()


class BlockScatter(Cube):
    def __init__(self, chunk, out_sent, total, landed, store, me, width, *sems):
        self.setup(me, width, *sems)
        self.chunk, self.sent, self.total, self.landed = chunk, out_sent, total, landed
        self.store = store
        self.slots = 1 << (width - 1)

    def pair(self, slot):
        return remote(
            self.sent.at[slot], self.total.at[slot], self.ps.at[slot], self.pr.at[slot],
            {"dp": self.at(1)},
        )

    def give(self):
        @pl.loop(0, self.slots)
        def _(k):
            slot = self.slots - 1 - k
            self.sent[slot] = self.chunk(self.at(2 * slot + 1)).astype(BF)
            self.pair(slot).start()

    def given(self):
        @pl.loop(0, self.slots)
        def _(slot):
            self.pair(slot).wait_send()

    def take(self):
        @pl.loop(0, self.slots)
        def _(k):
            slot = self.slots - 1 - k
            term = self.chunk(self.at(2 * slot))
            self.pair(slot).wait_recv()
            self.total[slot] = (term + self.total[slot].astype(F32)).astype(BF)

    def moves(self, stage):
        for h in range(2):
            order = self.orders[h]
            last = self.stages - 1 - stage
            bit = 1 << order[last]
            for m in spans(order[:last]):
                yield h, bit, m | bit

    def hop(self, h, bit, m):
        rows = self.total.shape[1] // 2
        return remote(
            self.total.at[m >> 1, pl.ds(h * rows, rows), :], self.landed.at[h, (m >> 1) - 1],
            self.hs.at[h, m >> 1], self.hr.at[h, m >> 1], {"dp": self.at(bit)},
        )

    def send(self, stage):
        for h, bit, m in self.moves(stage):
            self.hop(h, bit, m).start()

    def add(self, stage):
        rows = self.total.shape[1] // 2
        for h, bit, m in self.moves(stage):
            self.hop(h, bit, m).wait_recv()
            keep = (m ^ bit) >> 1
            at = slice(h * rows, (h + 1) * rows)
            total = self.total[keep, at, :].astype(F32) + self.landed[h, (m >> 1) - 1].astype(F32)
            if stage == self.stages - 1:
                self.store(at, total)
            else:
                self.total[keep, at, :] = total.astype(BF)

    def drain(self):
        for stage in range(self.stages):
            for h, bit, m in self.moves(stage):
                self.hop(h, bit, m).wait_send()


def inverse_of(rows):
    return lax.rsqrt(jnp.mean(rows * rows, axis=-1, keepdims=True) + EPSILON)


def times_gain(unit, gains, which, store):
    parts, _, width = gains.shape
    for d in range(parts):
        cols = slice(d * width, (d + 1) * width)
        store(cols, unit[:, cols] * gains[d, which : which + 1, :])


def lane_index(shape):
    return lax.broadcasted_iota(jnp.int32, shape, len(shape) - 1)


def column_of(segr):
    rows = segr.shape[1]
    wide = jnp.broadcast_to(segr[...].astype(F32), (8, rows))
    return jnp.transpose(wide)[:, 0:1]


def rope_into(cos_ref, sin_ref, segr):
    rows = segr.shape[1]
    before = (segr[...].astype(F32) < column_of(segr)).astype(F32)
    start = jnp.sum(before, axis=1, keepdims=True)
    position = lax.broadcasted_iota(jnp.int32, (rows, 1), 0).astype(F32) - start
    lane = lane_index((rows, LANES))
    half = HD // 2
    frequency = jnp.exp(lax.rem(lane, half).astype(F32) * (-math.log(10000.0) / half))
    angle = position * frequency
    cos_ref[...] = jnp.cos(angle)
    sine = jnp.sin(angle)
    sin_ref[...] = jnp.where(lax.rem(lane, HD) < half, -sine, sine)


def swapped(x):
    lane = lane_index(x.shape)
    half = HD // 2
    return jnp.where(
        lax.rem(lane, HD) < half,
        pltpu.roll(x, LANES - half, 1),
        pltpu.roll(x, half, 1),
    )


def bias_into(bias, segr):
    rows = segr.shape[1]
    query = lax.broadcasted_iota(jnp.int32, (rows, rows), 0)
    key = lax.broadcasted_iota(jnp.int32, (rows, rows), 1)
    seen = (segr[...].astype(F32) == column_of(segr)) & (query >= key)
    bias[...] = jnp.where(seen, 0.0, NEGATIVE)


def pad_pair(keys_values, keys, values):
    low = lane_index(keys_values.shape) < HD
    key = jnp.where(low, keys_values, 0.0)
    value = jnp.where(low, 0.0, keys_values)
    keys[0] = key.astype(BF)
    keys[1] = pltpu.roll(key, HD, 1).astype(BF)
    values[0] = pltpu.roll(value, HD, 1).astype(BF)
    values[1] = value.astype(BF)


def query_cuts(rows):
    block = 256 if rows % 256 == 0 else rows
    return [(start, block, start + block) for start in range(0, rows, block)]


def attend_pairs(first, last, qo, kpad, vpad, bias, mo, lo):
    rows = qo.shape[0]
    lane = lane_index((1, LANES))

    @pl.loop(first, last)
    def _(pair):
        lanes = pl.ds(pl.multiple_of(pair * LANES, LANES), LANES)
        for start, block, seen in query_cuts(rows):
            at = slice(start, start + block)
            query = qo[at, lanes]
            mixed = jnp.zeros((block, LANES), F32)
            logs = lo[at, :]
            for side in range(2):
                scores = dot(query, kpad[side, :seen, :], 1, 1) + bias[at, :seen]
                top = jnp.max(scores, axis=-1, keepdims=True)
                probs = jnp.exp(scores - top)
                total = jnp.sum(probs, axis=-1, keepdims=True)
                mixed = mixed + dot(probs.astype(BF), vpad[side, :seen, :]) / total
                logs = jnp.where(lane == 2 * pair + side, top + jnp.log(total), logs)
            lo[at, :] = logs
            mo[at, lanes] = mixed.astype(BF)


def back_through_norm(raw, grads, gains, which, store, store_gain):
    parts, _, width = gains.shape
    cuts = [slice(d * width, (d + 1) * width) for d in range(parts)]
    model = parts * width
    square = sum(jnp.sum(raw(c) * raw(c), axis=-1, keepdims=True) for c in cuts)
    inverse = lax.rsqrt(square / model + EPSILON)
    mean = 0.0
    for d, c in enumerate(cuts):
        unit = raw(c) * inverse
        grad = grads(c)
        store_gain(c, jnp.sum(grad * unit, axis=0, keepdims=True))
        mean = mean + jnp.sum(grad * gains[d, which : which + 1, :] * unit, axis=-1, keepdims=True)
    mean = mean / model
    for d, c in enumerate(cuts):
        unit = raw(c) * inverse
        store(c, inverse * (grads(c) * gains[d, which : which + 1, :] - unit * mean))


PIECES = 4


def vmem():
    return pl.BlockSpec(memory_space=pltpu.VMEM)


def hbm():
    return pl.BlockSpec(memory_space=pl.ANY)


def dma(*shape):
    return pltpu.SemaphoreType.DMA(shape)


def line_scratch(nt, rows, model):
    return [pltpu.VMEM((nt, rows, model), BF), pltpu.VMEM((2, nt, rows, model), BF)]


def ticks(pieces, nt):
    return [
        [(k, tick - k) for k in range(1, nt) if 0 <= tick - k < pieces]
        for tick in range(pieces + nt - 1)
    ]


def fore_kernel(
    nt, width,
    x, cot, gain_a, gain_f, segr, wq, wkt, wvt, wo, gate, up, down,
    wqkv_f, wo_f, na_o, cf, qo, kvo, mo, lo, gall, cos, sin, act, branch, gh, gains, y, d_gate, d_up,
    rowsbuf, hid, gate_v, up_v, down_v, part, sent, arrived, totals, landed, own_qkv, gain,
    gain_sem, place_sem, out_sem, x_sem, cot_sem, nf_sem, br_sem, o_sem, gn_sem, y_sem, hs, hr, ps, pr,
):
    me, t = lax.axis_index("dp"), lax.axis_index("tensor")
    nd = 1 << width
    rows, model = x.shape
    tokens = nt * rows
    queries = wq.shape[1]
    hidden = gate.shape[1]
    shard = model >> width
    wide = own_qkv.shape[1]
    pieces = PIECES
    size = rows // pieces

    def natural(j, s):
        return j * rows + s * size

    def shuffled(j, s):
        return (s * nt + j) * size

    local = pl.ds(pl.multiple_of(t * rows, rows), rows)
    rowsbuf[local, :] = x[...]
    gain[...] = jnp.zeros_like(gain)
    gain[0:1, :] = gain_a[...].astype(F32)
    gain[1:2, :] = gain_f[...].astype(F32)
    own_qkv[:, :queries] = wq[...]
    turned = jnp.concatenate([wkt[...].astype(F32), wvt[...].astype(F32)], axis=0)
    own_qkv[:, queries:] = jnp.transpose(turned).astype(BF)
    with jax.named_scope("enter"):
        enter(t, nt, me, width, pltpu.get_barrier_semaphore())

    tokens_x = LineGather(rowsbuf, natural, size, t, nt, x_sem)
    for s in range(pieces):
        tokens_x.start(s)
    gathers = []
    for w, (own, full, by_rows) in enumerate(
        ((own_qkv, wqkv_f, True), (wo, wo_f, False), (gate, gate_v, True), (up, up_v, True), (down, down_v, False))
    ):
        gathers.append(
            BlockGather(own, full, by_rows, me, width, hs.at[w], hr.at[w], ps.at[w], pr.at[w])
        )
    g_qkv, g_out, g_gate, g_up, g_down = gathers
    stages = g_qkv.stages

    def gain_copy(mask):
        return remote(
            gain, gall.at[me], gain_sem.at[0, mask], gain_sem.at[1, mask],
            {"dp": flip(me, mask, width)},
        )

    for mask in range(1, nd):
        gain_copy(mask).start()
    for g in (g_qkv, g_out, g_gate):
        g.send(0)
    for w, g in enumerate(gathers):
        g.place(place_sem.at[w]).start()
    gall[me] = gain[...]

    def forward(g, stage):
        g.wait(stage)
        if stage + 1 < stages:
            g.send(stage + 1)
        else:
            g.pair_send()

    for s in range(pieces):
        cf[pl.ds(pl.multiple_of(shuffled(t, s), size), size), :] = cot[s * size : (s + 1) * size, :]
    cots = LineGather(cf, shuffled, size, t, nt, cot_sem)
    scatter_o = LineScatter(part, natural, sent, arrived, t, nt, o_sem)

    def attention(na, wqkv_v, wo_v, bias, kpad, vpad):
        bias_into(bias, segr)
        rope_into(cos, sin, segr)
        lo[...] = jnp.zeros_like(lo)
        for mask in range(1, nd):
            slot = gall.at[flip(me, mask, width)]
            remote(
                slot, slot, gain_sem.at[0, mask], gain_sem.at[1, mask],
                {"dp": flip(me, mask, width)},
            ).wait_recv()

        def norm(j):
            @pl.loop(0, pieces)
            def _(s):
                these = pl.ds(pl.multiple_of(j * rows + s * size, size), size)
                value = rowsbuf[these, :].astype(F32)

                def store(cols, normed):
                    na[these, cols] = normed.astype(BF)

                times_gain(value * inverse_of(value), gall, 0, store)

        norm(t)
        for stage in range(stages - 1):
            forward(g_qkv, stage)
            forward(g_out, stage)
        fills = [
            lambda: (forward(g_gate, 0), g_up.send(0)),
            lambda: (forward(g_qkv, stages - 1), forward(g_out, stages - 1), g_down.send(0)),
        ]
        load = pltpu.make_async_copy(wqkv_f, wqkv_v, place_sem.at[5])
        load_out = pltpu.make_async_copy(wo_f, wo_v, place_sem.at[6])

        def fetch():
            g_qkv.place(place_sem.at[0]).wait()
            g_qkv.pair_wait()
            load.start()
            g_out.place(place_sem.at[1]).wait()
            g_out.pair_wait()
            load_out.start()

        for k in range(1, nt):
            if k == nt - 1:
                for fill in fills:
                    fill()
                fills = []
                with jax.named_scope("fetch"):
                    fetch()
            with jax.named_scope("x_step"):
                for s in range(pieces):
                    tokens_x.step(k, s)
            if k == nt - 1:
                for s in range(pieces):
                    cots.start(s)

            @pl.when(t >= k)
            def _():
                norm(t - k)

            @pl.when(t + k < nt)
            def _():
                norm(t + k)

            if fills:
                with jax.named_scope("x_fill"):
                    fills.pop(0)()
        keep = pltpu.make_async_copy(na, na_o, out_sem.at[0])
        keep.start()
        with jax.named_scope("wait_qkv"):
            load.wait()
        with jax.named_scope("qkv"):
            part[:, :wide] = dot(na[...], wqkv_v[...])
            c, s_ = cos[...], sin[...]
            for start in range(0, queries, LANES):
                lanes = slice(start, start + LANES)
                value = part[:, lanes]
                qo[:, lanes] = ((value * c + swapped(value) * s_) * HD ** (-0.5)).astype(BF)
            value = part[:, queries : queries + LANES]
            keyed = jnp.where(lane_index(value.shape) < HD, value * c + swapped(value) * s_, value)
            kvo[...] = keyed.astype(BF)
            pad_pair(keyed, kpad, vpad)
        pairs = queries // LANES
        with jax.named_scope("g1"):
            for stage in range(1, stages):
                forward(g_gate, stage)
        with jax.named_scope("att"):
            attend_pairs(0, pairs, qo, kpad, vpad, bias, mo, lo)
        load_out.wait()
        with jax.named_scope("outproj"):
            for start, width_ in tiles_of(model, 4):
                cols = slice(start, start + width_)
                part[:, cols] = dot(mo[...], wo_v[:, cols])
        keep.wait()
        tokens_x.finish()

    pl.run_scoped(
        attention,
        pltpu.VMEM((tokens, model), BF),
        pltpu.VMEM((model, wide), BF),
        pltpu.VMEM((queries, model), BF),
        pltpu.VMEM((tokens, tokens), F32),
        pltpu.VMEM((2, tokens, LANES), BF),
        pltpu.VMEM((2, tokens, LANES), BF),
    )

    gather_nf = LineGather(rowsbuf, shuffled, size, t, nt, nf_sem)

    def take_hidden(s):
        at = scatter_o.own(s)
        block = slice(s * size, (s + 1) * size)
        hidden_rows = x[block, :].astype(F32) + part[at, :model]
        hid[block, :] = hidden_rows
        there = pl.ds(pl.multiple_of(shuffled(t, s), size), size)

        def store(cols, normed):
            rowsbuf[there, cols] = normed.astype(BF)

        times_gain(hidden_rows * inverse_of(hidden_rows), gall, 1, store)
        gather_nf.start(s)

    scatter_o.edge(0)
    scatter_o.edge(1)
    with jax.named_scope("cot1"):
        for s in range(pieces):
            cots.step(1, s)
    with jax.named_scope("u0"):
        forward(g_up, 0)
    later = [
        lambda: ([cots.step(2, s) for s in range(pieces)], forward(g_down, 0)),
        lambda: [cots.step(k, s) for k in range(3, nt) for s in range(pieces)],
        lambda: [forward(g_up, stage) for stage in range(1, stages)],
        lambda: [forward(g_down, stage) for stage in range(1, stages)],
    ]
    steps = ticks(pieces, nt)

    def flow(tick, scatter, gather, take):
        todo = list(steps[tick])
        if 0 < tick < pieces - 1:
            scatter.edge(tick + 1)
        scatter.relay(scatter.near, tick)
        if todo:
            gather.step(*todo.pop(0))
        scatter.relay(scatter.far, tick)
        if todo:
            gather.step(*todo.pop(0))
        take(tick)
        for late in todo:
            gather.step(*late)

    for tick in range(pieces):
        with jax.named_scope("o_tick"):
            flow(tick, scatter_o, gather_nf, take_hidden)
        if later:
            with jax.named_scope("o_later"):
                later.pop(0)()
    for fill in later:
        fill()

    def feed(dg, du, given):
        cuts = tiles_of(hidden, 6)
        span = max(width_ for _, width_ in cuts)
        half = tokens // 2
        block = 64
        draft = half

        def tile(h, i):
            start, width_ = cuts[i]
            at = slice(start, start + width_)
            mine = slice(h * half, (h + 1) * half)
            held = slice(draft, draft + half)
            part[held, 0:width_] = dot(rowsbuf[mine, :], gate_v[:, at])
            part[held, span : span + width_] = dot(rowsbuf[mine, :], up_v[:, at])
            part[held, 2 * span : 2 * span + width_] = dot(cf[mine, :], down_v[at, :], 1, 1)

            @pl.loop(0, half // block)
            def _(k):
                from_ = pl.ds(pl.multiple_of(draft + k * block, block), block)
                to = pl.ds(pl.multiple_of(h * half + k * block, block), block)
                g = part[from_, 0:width_]
                u = part[from_, span : span + width_]
                ga = part[from_, 2 * span : 2 * span + width_]
                sig = 1.0 / (1.0 + jnp.exp(-g))
                gs = g * sig
                act[to, at] = (gs * u).astype(BF)
                du[to, at] = (ga * gs).astype(BF)
                dg[to, at] = (ga * u * sig * (1.0 + g * (1.0 - sig))).astype(BF)

        def back_dots(h):
            mine = slice(h * half, (h + 1) * half)
            for start, width_ in tiles_of(model, 4):
                cols = slice(start, start + width_)
                part[mine, cols] = dot(dg[mine, :], gate_v[cols, :], 1, 1) + dot(
                    du[mine, :], up_v[cols, :], 1, 1
                )

        scatter_gn = LineScatter(part, shuffled, sent, arrived, t, nt, gn_sem)
        gather_br = LineGather(branch, natural, size, t, nt, br_sem)
        gains[...] = jnp.zeros_like(gains)

        def take_grad(s):
            at = scatter_gn.own(s)
            block_ = slice(s * size, (s + 1) * size)
            there = pl.ds(pl.multiple_of(natural(t, s), size), size)

            def store(cols, value):
                total = cot[block_, cols].astype(F32) + value
                gh[block_, cols] = total
                branch[there, cols] = total.astype(BF)

            def store_gain(cols, value):
                gains[1:2, cols] += value

            back_through_norm(
                lambda c: hid[block_, c], lambda c: part[at, c], gall, 1, store, store_gain
            )
            gather_br.start(s)

        def chunk_of(left, right):
            def chunk(d):
                return dot(left[:, pl.ds(pl.multiple_of(d * shard, shard), shard)], right[...], 0, 0)

            return chunk

        def keep(place):
            def store(at, value):
                part[place + at.start : place + at.stop, :hidden] = value

            return store

        s_gate, s_up = [
            BlockScatter(
                chunk_of(rowsbuf, grad), given, totals.at[w], landed.at[w], keep(w * shard), me, width,
                hs.at[5 + w], hr.at[5 + w], ps.at[5 + w], pr.at[5 + w],
            )
            for w, grad in enumerate((dg, du))
        ]

        def take(s):
            s.take()
            s.send(0)

        with jax.named_scope("wait_ffn"):
            for w in (2, 3, 4):
                gathers[w].place(place_sem.at[w]).wait()
                gathers[w].pair_wait()
        work = [lambda i=i: tile(0, i) for i in range(len(cuts))]
        for late in steps[pieces:]:
            with jax.named_scope("nf_step"):
                for k, s in late:
                    gather_nf.step(k, s)
            if work:
                with jax.named_scope("tile"):
                    work.pop(0)()
        for job in work:
            job()
        scatter_o.finish()
        with jax.named_scope("back_dots"):
            back_dots(0)
        scatter_gn.edge(0)
        scatter_gn.edge(1)
        with jax.named_scope("tile"):
            tile(1, 0)
        with jax.named_scope("gn_round"):
            scatter_gn.relay(scatter_gn.near, 0)
        with jax.named_scope("tile"):
            for i in range(1, len(cuts)):
                tile(1, i)
        with jax.named_scope("gn_round"):
            scatter_gn.relay(scatter_gn.far, 0)
        with jax.named_scope("back_dots"):
            back_dots(1)
        with jax.named_scope("gn_take"):
            take_grad(0)
        with jax.named_scope("gn_fill"):
            s_gate.give()
        fills = [
            lambda: take(s_gate),
            lambda: (s_gate.given(), s_up.give()),
            lambda: take(s_up),
        ]
        for tick in range(1, pieces):
            with jax.named_scope("gn_tick"):
                flow(tick, scatter_gn, gather_br, take_grad)
            if fills:
                with jax.named_scope("gn_fill"):
                    fills.pop(0)()
        for k, s in steps[pieces]:
            gather_br.step(k, s)

        with jax.named_scope("down"):
            scatter_gn.finish()
            scatter_y = LineScatter(part, shuffled, sent, arrived, t, nt, y_sem)
            for start, width_ in tiles_of(model, 4):
                cols = slice(start, start + width_)
                part[:, cols] = dot(act[...], down_v[:, cols])
            for s in range(pieces):
                scatter_y.edge(s)

        def on(s, stage):
            s.add(stage)
            if stage + 1 < stages:
                s.send(stage + 1)

        rest = list(steps[pieces + 1 :])
        fills = [functools.partial(on, s, stage) for stage in range(stages - 1) for s in (s_gate, s_up)]
        for s in range(pieces):
            with jax.named_scope("y_round"):
                scatter_y.relay(scatter_y.near, s)
                scatter_y.relay(scatter_y.far, s)
            if rest:
                with jax.named_scope("br_step"):
                    for k, s_ in rest.pop(0):
                        gather_br.step(k, s_)
            if fills:
                with jax.named_scope("y_fill"):
                    fills.pop(0)()
        with jax.named_scope("y_own"):
            for late in rest:
                for k, s_ in late:
                    gather_br.step(k, s_)
            for fill in fills:
                fill()
            for s in range(pieces):
                at = scatter_y.own(s)
                block_ = slice(s * size, (s + 1) * size)
                y[block_, :] = (hid[block_, :] + part[at, :model]).astype(BF)
        with jax.named_scope("end"):
            copies = []
            for w, (s, out) in enumerate(((s_gate, d_gate), (s_up, d_up))):
                s.add(stages - 1)
                copies.append(
                    pltpu.make_async_copy(
                        part.at[pl.ds(w * shard, shard), pl.ds(0, hidden)], out, out_sem.at[1 + w]
                    )
                )
                copies[-1].start()
            s_up.given()
            for s in (s_gate, s_up):
                s.drain()
            gather_br.finish()
            scatter_y.finish()
            for copy in copies:
                copy.wait()

    pl.run_scoped(
        feed,
        pltpu.VMEM((tokens, hidden), BF),
        pltpu.VMEM((tokens, hidden), BF),
        pltpu.VMEM((nd // 2, shard, hidden), BF),
    )
    for g in gathers:
        g.drain()
    for mask in range(1, nd):
        gain_copy(mask).wait_send()
    cots.finish()
    gather_nf.finish()


def fore(nt, nd, x, cot, gain_a, gain_f, segr, wq, wkt, wvt, wo, gate, up, down):
    width = nd.bit_length() - 1
    rows, model = x.shape
    tokens = nt * rows
    queries = wq.shape[1]
    hidden = gate.shape[1]
    shard = model // nd
    half = nd // 2
    wide = queries + LANES
    span = max(width_ for _, width_ in tiles_of(hidden, 6))
    shape = jax.ShapeDtypeStruct
    outs = [
        (shape((model, wide), BF), hbm()),
        (shape((queries, model), BF), hbm()),
        (shape((tokens, model), BF), hbm()),
        (shape((tokens, model), BF), vmem()),
        (shape((tokens, queries), BF), vmem()),
        (shape((tokens, LANES), BF), vmem()),
        (shape((tokens, queries), BF), vmem()),
        (shape((tokens, LANES), F32), vmem()),
        (shape((nd, 8, shard), F32), vmem()),
        (shape((tokens, LANES), F32), vmem()),
        (shape((tokens, LANES), F32), vmem()),
        (shape((tokens, hidden), BF), vmem()),
        (shape((tokens, model), BF), vmem()),
        (shape((rows, model), F32), vmem()),
        (shape((8, model), F32), vmem()),
        (shape((rows, model), BF), vmem()),
        (shape((shard, hidden), F32), hbm()),
        (shape((shard, hidden), F32), hbm()),
    ]
    return pl.pallas_call(
        functools.partial(fore_kernel, nt, width),
        out_shape=[o for o, _ in outs],
        in_specs=[vmem()] * 8 + [hbm()] * 4,
        out_specs=[s for _, s in outs],
        scratch_shapes=[
            pltpu.VMEM((tokens, model), BF),
            pltpu.VMEM((rows, model), F32),
            pltpu.VMEM((model, hidden), BF),
            pltpu.VMEM((model, hidden), BF),
            pltpu.VMEM((hidden, model), BF),
            pltpu.VMEM((max(tokens, 2 * shard), max(model, 3 * span)), F32),
        ]
        + line_scratch(nt, rows, model)
        + [
            pltpu.VMEM((2, half, shard, hidden), BF),
            pltpu.VMEM((2, 2, half - 1, shard // 2, hidden), BF),
            pltpu.VMEM((shard, wide), BF),
            pltpu.VMEM((8, shard), F32),
            dma(2, nd),
            dma(7),
            dma(3),
            dma(4, nt, PIECES),
            dma(4, nt, PIECES),
            dma(4, nt, PIECES),
            dma(4, nt, PIECES),
            dma(2, 2, nt, PIECES),
            dma(2, 2, nt, PIECES),
            dma(2, 2, nt, PIECES),
            dma(7, 2, half),
            dma(7, 2, half),
            dma(7, half),
            dma(7, half),
        ],
        compiler_params=pltpu.CompilerParams(
            collective_id=0, has_side_effects=True, vmem_limit_bytes=VMEM_BYTES
        ),
        name="fore",
    )(x, cot, gain_a, gain_f, segr, wq, wkt, wvt, wo, gate, up, down)


def attend_back_pairs(first, last, qo, gm, mo, lo, kpad, vpad, bias, cos, sin, dqkv, dkey, dval):
    rows = qo.shape[0]

    @pl.loop(first, last)
    def _(pair):
        lanes = pl.ds(pl.multiple_of(pair * LANES, LANES), LANES)
        for start, block, seen in query_cuts(rows):
            at = slice(start, start + block)
            lane = lane_index((block, LANES))
            query, grad = qo[at, lanes], gm[at, lanes]
            both = grad.astype(F32) * mo[at, lanes].astype(F32)
            logs = lo[at, :]
            dq = jnp.zeros((block, LANES), F32)
            for side in range(2):
                inside = (lane >= HD) if side else (lane < HD)
                delta = jnp.sum(jnp.where(inside, both, 0.0), axis=-1, keepdims=True)
                log = jnp.sum(
                    jnp.where(lane == 2 * pair + side, logs, 0.0), axis=-1, keepdims=True
                )
                key, value = kpad[side, :seen, :], vpad[side, :seen, :]
                probs = jnp.exp(dot(query, key, 1, 1) + bias[at, :seen] - log)
                grad_scores = (probs * (dot(grad, value, 1, 1) - delta)).astype(BF)
                dq = dq + dot(grad_scores, key)
                dkey[side, :seen, :] += dot(grad_scores, query, 0, 0)
                dval[side, :seen, :] += dot(probs.astype(BF), grad, 0, 0)
            dq = dq * HD ** (-0.5)
            dqkv[at, lanes] = (dq * cos[at, :] - swapped(dq) * sin[at, :]).astype(BF)


def back_kernel(
    nt, width,
    branch, cf, act, mo, qo, kvo, lo, cos, sin, segr, x, gh, gparts, gall, na_f, wqkv_f, wo_f,
    gi, gain_out, d_wq, d_kv, d_wo, d_down,
    na, wqkv_v, wo_v, part, sent, arrived,
    bias, kpad, vpad, gm, dqkv, dkey, dval,
    given_d, totals_d, landed_d, given_q, totals_q, landed_q, given_o, totals_o, landed_o,
    gsum, zslots, dslots,
    load_sem, scatter_sem, zsem, dsem, hs, hr, ps, pr,
):
    me, t = lax.axis_index("dp"), lax.axis_index("tensor")
    nd = 1 << width
    rows, model = x.shape
    tokens, queries = qo.shape
    shard = model >> width
    pieces = PIECES
    size = rows // pieces
    loads = [
        pltpu.make_async_copy(wo_f, wo_v, load_sem.at[0]),
        pltpu.make_async_copy(wqkv_f, wqkv_v, load_sem.at[1]),
        pltpu.make_async_copy(na_f, na, load_sem.at[2]),
    ]
    for load in loads:
        load.start()
    bias_into(bias, segr)
    pad_pair(kvo[...].astype(F32), kpad, vpad)
    dkey[...] = jnp.zeros_like(dkey)
    dval[...] = jnp.zeros_like(dval)
    gsum[...] = gparts[...]
    with jax.named_scope("b_enter"):
        enter(t, nt, me, width, pltpu.get_barrier_semaphore(), everyone_along_tensor=True)

    def chunk_of(left, right):
        def chunk(d):
            return dot(left[:, pl.ds(pl.multiple_of(d * shard, shard), shard)], right[...], 0, 0)

        return chunk

    def store_down(at, value):
        d_down[:, at] = value.T

    def store_qkv(at, value):
        d_wq[at, :] = value[:, :queries]
        d_kv[:, at] = value[:, queries:].T

    def store_wo(at, value):
        d_wo[:, at] = value.T

    s_down, s_qkv, s_out = [
        BlockScatter(
            chunk_of(left, right), given, totals, landed, store, me, width,
            hs.at[w], hr.at[w], ps.at[w], pr.at[w],
        )
        for w, (left, right, given, totals, landed, store) in enumerate(
            (
                (cf, act, given_d, totals_d, landed_d, store_down),
                (na, dqkv, given_q, totals_q, landed_q, store_qkv),
                (branch, mo, given_o, totals_o, landed_o, store_wo),
            )
        )
    ]
    stages = s_down.stages

    with jax.named_scope("b_gm"):
        loads[0].wait()
        gm[...] = dot(branch[...], wo_v[...], 1, 1).astype(BF)
    with jax.named_scope("b_give"):
        s_down.give()
    with jax.named_scope("b_att"):
        attend_back_pairs(
            0, queries // LANES, qo, gm, mo, lo, kpad, vpad, bias, cos, sin, dqkv, dkey, dval
        )
        key = dkey[0] + pltpu.roll(dkey[1], HD, 1)
        value = pltpu.roll(dval[0], HD, 1) + dval[1]
        key = key * cos[...] - swapped(key) * sin[...]
        dqkv[:, queries : queries + LANES] = jnp.where(
            lane_index(key.shape) < HD, key, value
        ).astype(BF)

    inward = LineScatter(
        part, lambda j, s: j * rows + s * size, sent, arrived, t, nt, scatter_sem
    )
    with jax.named_scope("b_part"):
        loads[1].wait()
        for start, width_ in tiles_of(model, 4):
            part[:, start : start + width_] = dot(dqkv[...], wqkv_v[start : start + width_, :], 1, 1)
        for s in range(pieces):
            inward.edge(s)
        loads[2].wait()

    def take(s):
        s.take()
        s.send(0)

    def on(s, stage):
        s.add(stage)
        if stage + 1 < stages:
            s.send(stage + 1)

    def take_grad(s):
        at = inward.own(s)
        block = slice(s * size, (s + 1) * size)

        def store(cols, value):
            gi[block, cols] = gh[block, cols] + value

        def store_gain(cols, value):
            gsum[0:1, cols] += value

        back_through_norm(
            lambda c: x[block, c].astype(F32), lambda c: part[at, c], gall, 0, store, store_gain
        )

    fills = [
        lambda: s_qkv.give(),
        lambda: (take(s_qkv), s_out.give()),
        lambda: take(s_out),
    ]
    fills += [functools.partial(on, s, stage) for stage in range(stages) for s in (s_down, s_qkv, s_out)]
    with jax.named_scope("b_take"):
        take(s_down)
    for s in range(pieces):
        with jax.named_scope("b_round"):
            inward.relay(inward.near, s)
            inward.relay(inward.far, s)
        with jax.named_scope("b_fill"):
            if fills:
                fills.pop(0)()
    with jax.named_scope("b_own"):
        for s in range(pieces):
            take_grad(s)
            if fills and s < pieces - 1:
                fills.pop(0)()

    with jax.named_scope("b_gains"):
        zslots[t] = gsum[...]

        def along(step):
            return remote(
                zslots.at[t], zslots.at[t], zsem.at[0, step], zsem.at[1, step],
                {"tensor": lax.rem(t + step, nt)},
            )

        for step in range(1, nt):
            along(step).start()
    with jax.named_scope("b_rest"):
        for fill in fills:
            fill()
    with jax.named_scope("b_gains"):
        for step in range(1, nt):
            slot = zslots.at[lax.rem(t + nt - step, nt)]
            remote(
                slot, slot, zsem.at[0, step], zsem.at[1, step], {"tensor": lax.rem(t + step, nt)}
            ).wait_recv()
        gsum[...] = sum(zslots[i] for i in range(nt))

        def across(mask):
            peer = flip(me, mask, width)
            return remote(
                gsum.at[:, pl.ds(pl.multiple_of(peer * shard, shard), shard)], dslots.at[me],
                dsem.at[0, mask], dsem.at[1, mask], {"dp": peer},
            )

        for mask in range(1, nd):
            across(mask).start()
        dslots[me] = gsum[:, pl.ds(pl.multiple_of(me * shard, shard), shard)]
        for mask in range(1, nd):
            peer = flip(me, mask, width)
            slot = dslots.at[peer]
            remote(slot, slot, dsem.at[0, mask], dsem.at[1, mask], {"dp": peer}).wait_recv()
        gain_out[...] = sum(dslots[i] for i in range(nd))

    for step in range(1, nt):
        along(step).wait_send()
    for mask in range(1, nd):
        across(mask).wait_send()
    for s in (s_down, s_qkv, s_out):
        s.given()
        s.drain()
    inward.finish()


def back(nt, nd, branch, cf, act, mo, qo, kvo, lo, cos, sin, segr, x, gh, gparts, gall, na, wqkv_f, wo_f):
    width = nd.bit_length() - 1
    rows, model = x.shape
    tokens, queries = qo.shape
    hidden = act.shape[1]
    wide = wqkv_f.shape[1]
    shard = model // nd
    half = nd // 2
    shape = jax.ShapeDtypeStruct
    outs = [
        shape((rows, model), F32),
        shape((8, shard), F32),
        shape((shard, queries), F32),
        shape((LANES, shard), F32),
        shape((queries, shard), F32),
        shape((hidden, shard), F32),
    ]

    def cube(size):
        return [
            pltpu.VMEM((half, shard, size), BF),
            pltpu.VMEM((half, shard, size), BF),
            pltpu.VMEM((2, half - 1, shard // 2, size), BF),
        ]

    return pl.pallas_call(
        functools.partial(back_kernel, nt, width),
        out_shape=outs,
        in_specs=[vmem()] * 14 + [hbm()] * 3,
        out_specs=[vmem()] * len(outs),
        scratch_shapes=[
            pltpu.VMEM((tokens, model), BF),
            pltpu.VMEM((model, wide), BF),
            pltpu.VMEM((queries, model), BF),
            pltpu.VMEM((tokens, model), F32),
        ]
        + line_scratch(nt, rows, model)
        + [
            pltpu.VMEM((tokens, tokens), F32),
            pltpu.VMEM((2, tokens, LANES), BF),
            pltpu.VMEM((2, tokens, LANES), BF),
            pltpu.VMEM((tokens, queries), BF),
            pltpu.VMEM((tokens, wide), BF),
            pltpu.VMEM((2, tokens, LANES), F32),
            pltpu.VMEM((2, tokens, LANES), F32),
        ]
        + cube(hidden)
        + cube(wide)
        + cube(queries)
        + [
            pltpu.VMEM((8, model), F32),
            pltpu.VMEM((nt, 8, model), F32),
            pltpu.VMEM((nd, 8, shard), F32),
            dma(3),
            dma(2, 2, nt, PIECES),
            dma(2, nt),
            dma(2, nd),
            dma(3, 2, half),
            dma(3, 2, half),
            dma(3, half),
            dma(3, half),
        ],
        compiler_params=pltpu.CompilerParams(
            collective_id=1, has_side_effects=True, vmem_limit_bytes=VMEM_BYTES
        ),
        name="back",
    )(branch, cf, act, mo, qo, kvo, lo, cos, sin, segr, x, gh, gparts, gall, na, wqkv_f, wo_f)


def narrow_scatter(value, axis, scatter_dimension, tiled):
    low = value.astype(BF) if value.ndim == 2 else value
    return lax.psum_scatter(low, axis, scatter_dimension=scatter_dimension, tiled=tiled).astype(F32)


def rope_tables(segments, head_dim):
    row_count = segments.shape[0]
    row_index = jnp.arange(row_count, dtype=jnp.int32)
    change = jnp.concatenate(
        [jnp.ones((1,), jnp.int32), (segments[1:] != segments[:-1]).astype(jnp.int32)]
    )
    starts = lax.cummax(jnp.where(change > 0, row_index, jnp.zeros_like(row_index)), axis=0)
    position = (row_index - starts).astype(F32)
    half_dim = head_dim // 2
    frequency = jnp.exp(jnp.arange(half_dim, dtype=F32) * (-math.log(10000.0) / half_dim))
    angles = position[:, None] * frequency[None, :]
    return (jnp.cos(angles)[:, None, :], jnp.sin(angles)[:, None, :])


def rotate(tensor, cosine, sine):
    half_dim = tensor.shape[-1] // 2
    first_half = tensor[..., :half_dim]
    second_half = tensor[..., half_dim:]
    return jnp.concatenate(
        [first_half * cosine - second_half * sine, second_half * cosine + first_half * sine],
        axis=-1,
    )


def unrotate(tensor, cosine, sine):
    half_dim = tensor.shape[-1] // 2
    first_half = tensor[..., :half_dim]
    second_half = tensor[..., half_dim:]
    return jnp.concatenate(
        [first_half * cosine + second_half * sine, second_half * cosine - first_half * sine],
        axis=-1,
    )


def visible(segments):
    row_index = jnp.arange(segments.shape[0], dtype=jnp.int32)
    same_seq = segments[:, None] == segments[None, :]
    return same_seq & (row_index[:, None] >= row_index[None, :])


def normalize(values, gain):
    inverse = lax.rsqrt(jnp.mean(values * values, axis=-1, keepdims=True) + EPSILON)
    unit_rows = values * inverse
    return (unit_rows, inverse, (unit_rows * gain.astype(F32)).astype(BF))


def normalize_back(grad_normed, unit_rows, inverse, gain):
    scaled = grad_normed * gain.astype(F32)
    grad_values = inverse * (
        scaled - unit_rows * jnp.mean(scaled * unit_rows, axis=-1, keepdims=True)
    )
    return (grad_values, jnp.sum(grad_normed * unit_rows, axis=0))


def contract(left, right, left_dim, right_dim):
    return lax.dot_general(
        left, right, (((left_dim,), (right_dim,)), ((), ())), preferred_element_type=F32
    )


def block_scores(query_block, key_heads, allowed_block, score_scale):
    scores = (
        jnp.einsum("rkgd,skd->kgrs", query_block, key_heads, preferred_element_type=F32)
        * score_scale
    )
    return jnp.where(allowed_block[None, None], scores, NEGATIVE)


def attend_forward(query_groups, key_heads, value_heads, allowed, score_scale):
    scores = block_scores(query_groups, key_heads, allowed, score_scale)
    row_max = jnp.max(scores, axis=-1, keepdims=True)
    log_total = row_max + jnp.log(jnp.sum(jnp.exp(scores - row_max), axis=-1, keepdims=True))
    probs_low = jnp.exp(scores - log_total).astype(BF)
    mixed_parts = jnp.einsum(
        "kgrs,skd->rkgd", probs_low, value_heads, preferred_element_type=F32
    ).astype(BF)
    return (mixed_parts, log_total)


def attend_backward(
    query_groups, key_heads, value_heads, mixed_heads, grad_mixed, log_totals, allowed, score_scale
):
    scores = block_scores(query_groups, key_heads, allowed, score_scale)
    attn_probs = jnp.exp(scores - log_totals)
    probs_low = attn_probs.astype(BF)
    grad_probs = jnp.einsum(
        "rkgd,skd->kgrs", grad_mixed, value_heads, preferred_element_type=F32
    )
    row_delta = jnp.sum(grad_mixed.astype(F32) * mixed_heads.astype(F32), axis=-1)
    row_delta = jnp.transpose(row_delta, (1, 2, 0))[..., None]
    grad_scores = (attn_probs * (grad_probs - row_delta)).astype(BF)
    query_parts = (
        jnp.einsum("kgrs,skd->rkgd", grad_scores, key_heads, preferred_element_type=F32)
        * score_scale
    )
    grad_key_rot = (
        jnp.einsum("kgrs,rkgd->skd", grad_scores, query_groups, preferred_element_type=F32)
        * score_scale
    )
    grad_value_heads = jnp.einsum(
        "kgrs,rkgd->skd", probs_low, grad_mixed, preferred_element_type=F32
    )
    return (query_parts, grad_key_rot, grad_value_heads)


def plain_device(
    layer_input,
    segment_ids,
    norm_attn,
    w_query,
    w_key,
    w_value,
    w_output,
    norm_ffn,
    w_gate,
    w_up,
    w_down,
    cotangent,
):
    score_scale = HD ** (-0.5)
    query_full, key_full, value_full, output_full, gain_attn = (
        lax.all_gather(w_query, "dp", axis=0, tiled=True),
        lax.all_gather(w_key, "dp", axis=0, tiled=True),
        lax.all_gather(w_value, "dp", axis=0, tiled=True),
        lax.all_gather(w_output, "dp", axis=1, tiled=True),
        lax.all_gather(norm_attn, "dp", axis=0, tiled=True),
    )
    gate_full, up_full, down_full, gain_ffn = (
        lax.all_gather(w_gate, "dp", axis=0, tiled=True),
        lax.all_gather(w_up, "dp", axis=0, tiled=True),
        lax.all_gather(w_down, "dp", axis=1, tiled=True),
        lax.all_gather(norm_ffn, "dp", axis=0, tiled=True),
    )
    heads_local = query_full.shape[1] // HD
    kv_local = key_full.shape[1] // HD
    group = heads_local // kv_local
    residual_in = layer_input.astype(F32)
    unit_attn, inverse_attn, normed_local = normalize(residual_in, gain_attn)
    normed_attn = lax.all_gather(normed_local, "tensor", axis=0, tiled=True)
    row_count = normed_attn.shape[0]
    cosine, sine = rope_tables(segment_ids, HD)
    allowed = visible(segment_ids)
    query_heads = rotate(
        jnp.dot(normed_attn, query_full, preferred_element_type=F32).reshape(
            row_count, heads_local, HD
        ),
        cosine,
        sine,
    ).astype(BF)
    query_groups = query_heads.reshape(row_count, kv_local, group, HD)
    key_heads = rotate(
        jnp.dot(normed_attn, key_full, preferred_element_type=F32).reshape(
            row_count, kv_local, HD
        ),
        cosine,
        sine,
    ).astype(BF)
    value_heads = (
        jnp.dot(normed_attn, value_full, preferred_element_type=F32)
        .astype(BF)
        .reshape(row_count, kv_local, HD)
    )
    mixed_heads, log_totals = attend_forward(
        query_groups, key_heads, value_heads, allowed, score_scale
    )
    mixed_flat = mixed_heads.reshape(row_count, heads_local * HD)
    hidden_res = residual_in + narrow_scatter(
        jnp.dot(mixed_flat, output_full, preferred_element_type=F32),
        "tensor",
        scatter_dimension=0,
        tiled=True,
    )
    unit_ffn, inverse_ffn, normed_ffn_local = normalize(hidden_res, gain_ffn)
    normed_ffn = lax.all_gather(normed_ffn_local, "tensor", axis=0, tiled=True)
    gate_rows = jnp.dot(normed_ffn, gate_full, preferred_element_type=F32)
    up_rows = jnp.dot(normed_ffn, up_full, preferred_element_type=F32)
    sigmoid_gate = jax.nn.sigmoid(gate_rows)
    active = (gate_rows * sigmoid_gate * up_rows).astype(BF)
    layer_output = (
        hidden_res
        + narrow_scatter(
            jnp.dot(active, down_full, preferred_element_type=F32).astype(BF),
            "tensor",
            scatter_dimension=0,
            tiled=True,
        ).astype(F32)
    ).astype(BF)
    query_full, key_full, value_full, output_full, gate_full, up_full, down_full = (
        lax.all_gather(w_query, "dp", axis=0, tiled=True),
        lax.all_gather(w_key, "dp", axis=0, tiled=True),
        lax.all_gather(w_value, "dp", axis=0, tiled=True),
        lax.all_gather(w_output, "dp", axis=1, tiled=True),
        lax.all_gather(w_gate, "dp", axis=0, tiled=True),
        lax.all_gather(w_up, "dp", axis=0, tiled=True),
        lax.all_gather(w_down, "dp", axis=1, tiled=True),
    )
    cotangent_full = lax.all_gather(cotangent, "tensor", axis=0, tiled=True)
    grad_active = contract(cotangent_full, down_full, 1, 1)
    grad_w_down = contract(active, cotangent_full, 0, 0)
    grad_up_rows = (grad_active * gate_rows * sigmoid_gate).astype(BF)
    grad_gate_rows = (
        grad_active * up_rows * sigmoid_gate * (1.0 + gate_rows * (1.0 - sigmoid_gate))
    ).astype(BF)
    grad_w_gate = contract(normed_ffn, grad_gate_rows, 0, 0)
    grad_w_up = contract(normed_ffn, grad_up_rows, 0, 0)
    grad_normed_ffn = narrow_scatter(
        contract(grad_gate_rows, gate_full, 1, 1) + contract(grad_up_rows, up_full, 1, 1),
        "tensor",
        scatter_dimension=0,
        tiled=True,
    )
    grad_hidden, gain_ffn_part = normalize_back(grad_normed_ffn, unit_ffn, inverse_ffn, gain_ffn)
    grad_hidden = cotangent.astype(F32) + grad_hidden
    branch_full = lax.all_gather(grad_hidden.astype(BF), "tensor", axis=0, tiled=True)
    grad_mixed = contract(branch_full, output_full, 1, 1).astype(BF)
    grad_w_output = contract(mixed_flat, branch_full, 0, 0)
    grad_query_rot, grad_key_rot, grad_value_heads = attend_backward(
        query_groups,
        key_heads,
        value_heads,
        mixed_heads,
        grad_mixed.reshape(row_count, kv_local, group, HD),
        log_totals,
        allowed,
        score_scale,
    )
    grad_queries = (
        unrotate(grad_query_rot.reshape(row_count, heads_local, HD), cosine, sine)
        .reshape(row_count, heads_local * HD)
        .astype(BF)
    )
    grad_keys = (
        unrotate(grad_key_rot, cosine, sine).reshape(row_count, kv_local * HD).astype(BF)
    )
    grad_values = grad_value_heads.reshape(row_count, kv_local * HD).astype(BF)
    grad_w_query = contract(normed_attn, grad_queries, 0, 0)
    grad_w_key = contract(normed_attn, grad_keys, 0, 0)
    grad_w_value = contract(normed_attn, grad_values, 0, 0)
    grad_normed_attn = narrow_scatter(
        contract(grad_queries, query_full, 1, 1)
        + contract(grad_keys, key_full, 1, 1)
        + contract(grad_values, value_full, 1, 1),
        "tensor",
        scatter_dimension=0,
        tiled=True,
    )
    grad_residual, gain_attn_part = normalize_back(
        grad_normed_attn, unit_attn, inverse_attn, gain_attn
    )
    grad_input = grad_hidden + grad_residual
    gain_attn_total, gain_ffn_total = lax.psum((gain_attn_part, gain_ffn_part), "tensor")
    owned = (
        narrow_scatter(grad_w_query, "dp", scatter_dimension=0, tiled=True),
        narrow_scatter(grad_w_key, "dp", scatter_dimension=0, tiled=True),
        narrow_scatter(grad_w_value, "dp", scatter_dimension=0, tiled=True),
        narrow_scatter(grad_w_output, "dp", scatter_dimension=1, tiled=True),
        narrow_scatter(gain_attn_total, "dp", scatter_dimension=0, tiled=True),
        narrow_scatter(gain_ffn_total, "dp", scatter_dimension=0, tiled=True),
        narrow_scatter(grad_w_gate, "dp", scatter_dimension=0, tiled=True),
        narrow_scatter(grad_w_up, "dp", scatter_dimension=0, tiled=True),
        narrow_scatter(grad_w_down, "dp", scatter_dimension=1, tiled=True),
    )
    return (
        layer_output,
        grad_input,
        owned[4],
        owned[0],
        owned[1],
        owned[2],
        owned[3],
        owned[5],
        owned[6],
        owned[7],
        owned[8],
    )


def with_kernels(nt, nd, layer_input, segment_ids, norm_attn, w_query, w_key, w_value, w_output, norm_ffn, w_gate, w_up, w_down, cotangent):
    segr = segment_ids[None, :]
    (wqkv_f, wo_f, na, cf, qo, kvo, mo, lo, gall, cos, sin, act, branch, gh, gparts, y, d_gate, d_up) = fore(
        nt, nd, layer_input, cotangent, norm_attn[None, :], norm_ffn[None, :], segr,
        w_query, w_key.T, w_value.T, w_output, w_gate, w_up, w_down,
    )
    gi, gains, d_wq, d_kv, d_wo, d_down = back(
        nt, nd, branch, cf, act, mo, qo, kvo, lo, cos, sin, segr, layer_input, gh, gparts, gall,
        na, wqkv_f, wo_f,
    )
    k = w_key.shape[1]
    return (
        y, gi, gains[0], d_wq, d_kv[:k].T, d_kv[k:].T, d_wo, gains[1], d_gate, d_up, d_down
    )


def fits(nt, nd, shards):
    layer_input, segment_ids, norm_attn, w_query, w_key, w_value, w_output, norm_ffn, w_gate, w_up, w_down, _ = shards
    return (
        nd >= 4
        and nd & (nd - 1) == 0
        and nt >= 2
        and norm_attn.shape[0] % LANES == 0
        and w_output.shape[1] % LANES == 0
        and w_gate.shape[1] % LANES == 0
        and w_query.shape[1] % LANES == 0
        and w_key.shape[1] == HD
        and segment_ids.shape[0] == nt * layer_input.shape[0]
        and segment_ids.shape[0] % LANES == 0
    )


def on_device(nt, nd, *shards):
    if fits(nt, nd, shards):
        return with_kernels(nt, nd, *shards)
    return plain_device(*shards)


def solution(mesh):
    placed = (
        P(("dp", "tensor"), None),
        P("dp"),
        P("dp"),
        P("dp", "tensor"),
        P("dp", "tensor"),
        P("dp", "tensor"),
        P("tensor", "dp"),
        P("dp"),
        P("dp", "tensor"),
        P("dp", "tensor"),
        P("tensor", "dp"),
        P(("dp", "tensor"), None),
    )
    return jax.shard_map(
        functools.partial(on_device, mesh.shape["tensor"], mesh.shape["dp"]),
        mesh=mesh,
        in_specs=placed,
        out_specs=(
            P(("dp", "tensor"), None),
            P(("dp", "tensor"), None),
            P("dp"),
            P("dp", "tensor"),
            P("dp", "tensor"),
            P("dp", "tensor"),
            P("tensor", "dp"),
            P("dp"),
            P("dp", "tensor"),
            P("dp", "tensor"),
            P("tensor", "dp"),
        ),
        check_vma=False,
    )
```

time: 1210 us -> 342 us (0.28)
  waiting for transfers between devices: 955 us -> 0 us
  Pallas kernels: 0 us -> 321 us
  matrix products: 123 us -> 0 us
  blocking collectives: 75 us -> 0 us
  other arithmetic: 19.8 us -> 0 us
  between operations: 16.1 us -> 1.13 us
    reduce_scatter x11 -> x0, waiting for transfers between devices: 631 us -> none  [the longest x1 91.1 us: on_device(): lax.psum_scatter(grad_w_gate, 'dp', scatter_dimension=0, tiled=True)]
    pallas_call x0 -> x2, Pallas kernels: none -> 321 us  [the longest x1 244 us: fore(): pl.pallas_call(functools.partial(fore_kernel, nt, width), out_shape=[o fo...]
    all_gather x9 -> x0, waiting for transfers between devices: 319 us -> none  [the longest x1 47.7 us: on_device(): normed_ffn = lax.all_gather(normed_ffn_local, 'tensor', axis=0, tiled=True)]
    dot_general x27 -> x0, matrix products: 123 us -> none  [the longest x14 71.2 us: contract(): lax.dot_general(left, right, (((left_dim,), (right_dim,)), ((), ())), pre...]
    all_gather x4 -> x0, blocking collectives: 38.6 us -> none  [the longest x1 10.4 us: on_device(): lax.all_gather(norm_attn, 'dp', axis=0, tiled=True)]
    unnamed x1 -> x0, blocking collectives: 24.5 us -> none
  transfers between devices with their start and end apart: 20 -> 0, of which waited for: 20 -> 0; matrix products, arithmetic and copies ran while one was open for 7% -> 0% of each run, Pallas kernels for 0% -> 0%
where the time goes in v2:
time: 342 us; the launch traced here: 336 us
  Pallas kernels  321 us (94%)
  local copies, waits for them, and re-layouts  13.6 us (4%)
    pallas_call x1, Pallas kernels, fore(): pl.pallas_call(functools.partial(fore_kernel, nt, width), out_shape=[o fo...  244 us
    pallas_call x1, Pallas kernels, back(): pl.pallas_call(functools.partial(back_kernel, nt, width), out_shape=outs,...  77 us
    unnamed x21, local copies, waits for them, and re-layouts  8.23 us

profile of v2, /device:TPU:0, one launch (start us, length us, event | category | flops | bytes accessed | tf_op | source)
XLA Modules:
  0.0 335.9 jit_solution(16037334070462570746)
XLA Ops:
  0.6 1.2 broadcast_in_dim.9.gain_a
  1.9 1.2 broadcast_in_dim.10.gain_f
  3.1 244.2 %fore.1 = (bf16[2048,640]{1,0:T(8,128)(2,1)}, bf16[512,2048]{1,0:T(8,128)(2,1)}, bf16[512,2048]{1,0:T(8,128)(2,1)}, bf16[512,2048]{1,0:T(8,128)(2,1)}, bf16[512,...) custom-call(bf16[128,2048]{1,0:T(8,128)(2,1)} %x.3, ...), custom_call_target="tpu_custom_call" | custom-call | tf_op jit(solution)/shard_map/fore/pallas_call | solution.py:990
  247.2 0.0 copy-start.4
  247.3 77.0 %back.1 = (f32[128,2048]{1,0:T(8,128)}, f32[8,256]{1,0:T(8,128)}, f32[256,512]{1,0:T(8,128)}, f32[128,256]{1,0:T(8,128)}, f32[512,256]{1,0:T(8,128)}, /*index=5*/f32[1408,256]{1,0:T(8,128)}) custom-call(bf16[512,2048]{1,0:T(8,128)(2,1)} %get-tuple-element.36.branch, bf16[512,2048]{1,0:T(8,128)(2,1)} %get-tuple-element.37.cf, ...), custom_call_target="tpu_custom_call" | custom-call | tf_op jit(solution)/shard_map/back/pallas_call | solution.py:1267
  324.3 0.0 copy-start.3
  324.3 1.4 fusion
  325.7 1.5 slice_bitcast_fusion
  327.2 0.0 copy-done.4
  327.2 0.0 copy-start.6
  327.2 0.8 copy.30
  328.0 0.0 copy-done.3
  328.0 0.0 copy-start.5
  328.0 1.0 copy.31
  329.0 0.0 copy-done.6
  329.0 0.0 copy-start.1
  329.0 0.8 copy.32
  329.8 0.0 copy-done.5
  329.8 0.8 copy.33
  330.6 0.0 copy-done.1
  330.6 0.0 copy-start
  330.6 1.1 copy.34
  331.7 0.8 copy-done
  332.5 0.0 copy-start.2
  332.5 1.1 copy.35
  333.6 0.8 copy-done.2
  334.3 1.1 copy.36
Async XLA Ops:
  247.2 80.0 %copy-start.4 = (bf16[128,2048]{1,0:T(8,128)(2,1)S(1)}, bf16[128,2048]{1,0:T(8,128)(2,1)}, u32[]{:S(2)}) copy-start(bf16[128,2048]{1,0:T(8,128)(2,1)} %get-tuple-element.74) | copy-start | bytes 1572868
  324.3 3.7 %copy-start.3 = (f32[128,2048]{1,0:T(8,128)S(1)}, f32[128,2048]{1,0:T(8,128)}, u32[]{:S(2)}) copy-start(f32[128,2048]{1,0:T(8,128)} %get-tuple-element.75) | copy-start | bytes 3145732
  327.2 1.8 copy-start.6
  328.0 1.8 copy-start.5
  329.0 1.6 copy-start.1
  330.6 1.9 copy-start
  332.5 1.9 copy-start.2

commit v3 on v2

--- a/solution.py
+++ b/solution.py
@@ -14,7 +14,7 @@
 LANES = 128
 BF = jnp.bfloat16
 F32 = jnp.float32
-VMEM_BYTES = 66_000_000
+VMEM_BYTES = 67_000_000
 
 
 def spans(bits):
@@ -177,9 +177,12 @@
     def goal(self, way, i):
         return (1 - way) * (self.nt - 1 - i) + way * i
 
+    def slot(self, way, j):
+        return j + 1 - way
+
     def move(self, way, j, s):
         return remote(
-            self.sent.at[j, self.sub(s), :], self.arrived.at[way, j, self.sub(s), :],
+            self.sent.at[j, self.sub(s), :], self.arrived.at[self.slot(way, j), self.sub(s), :],
             self.sems.at[0, way, j, s], self.sems.at[1, way, j, s],
             {"tensor": lax.rem(self.t + self.nt + 1 - 2 * way, self.nt)},
         )
@@ -212,7 +215,7 @@
             def _(i):
                 j = self.goal(way, i)
                 self.move(way, j, s).wait_recv()
-                total = self.mine(j, s) + self.arrived[way, j, self.sub(s), :].astype(F32)
+                total = self.mine(j, s) + self.arrived[self.slot(way, j), self.sub(s), :].astype(F32)
                 self.sent[j, self.sub(s), :] = total.astype(BF)
                 self.move(way, j, s).start()
 
@@ -223,7 +226,7 @@
             @pl.when(self.depth(way) > 0)
             def _():
                 self.move(way, t, s).wait_recv()
-                self.part[rows, : self.model] += self.arrived[way, t, self.sub(s), :].astype(F32)
+                self.part[rows, : self.model] += self.arrived[self.slot(way, t), self.sub(s), :].astype(F32)
 
         return rows
 
@@ -498,6 +501,35 @@
         store(c, inverse * (grads(c) * gains[d, which : which + 1, :] - unit * mean))
 
 
+def attend_back_pairs(first, last, qo, gm, mo, lo, kpad, vpad, bias, cos, sin, dqkv, dkey, dval):
+    rows = qo.shape[0]
+
+    @pl.loop(first, last)
+    def _(pair):
+        lanes = pl.ds(pl.multiple_of(pair * LANES, LANES), LANES)
+        for start, block, seen in query_cuts(rows):
+            at = slice(start, start + block)
+            lane = lane_index((block, LANES))
+            query, grad = qo[at, lanes], gm[at, lanes]
+            both = grad.astype(F32) * mo[at, lanes].astype(F32)
+            logs = lo[at, :]
+            dq = jnp.zeros((block, LANES), F32)
+            for side in range(2):
+                inside = (lane >= HD) if side else (lane < HD)
+                delta = jnp.sum(jnp.where(inside, both, 0.0), axis=-1, keepdims=True)
+                log = jnp.sum(
+                    jnp.where(lane == 2 * pair + side, logs, 0.0), axis=-1, keepdims=True
+                )
+                key, value = kpad[side, :seen, :], vpad[side, :seen, :]
+                probs = jnp.exp(dot(query, key, 1, 1) + bias[at, :seen] - log)
+                grad_scores = (probs * (dot(grad, value, 1, 1) - delta)).astype(BF)
+                dq = dq + dot(grad_scores, key)
+                dkey[side, :seen, :] += dot(grad_scores, query, 0, 0)
+                dval[side, :seen, :] += dot(probs.astype(BF), grad, 0, 0)
+            dq = dq * HD ** (-0.5)
+            dqkv[at, lanes] = (dq * cos[at, :] - swapped(dq) * sin[at, :]).astype(BF)
+
+
 PIECES = 4
 
 
@@ -514,7 +546,7 @@
 
 
 def line_scratch(nt, rows, model):
-    return [pltpu.VMEM((nt, rows, model), BF), pltpu.VMEM((2, nt, rows, model), BF)]
+    return [pltpu.VMEM((nt, rows, model), BF), pltpu.VMEM((nt + 1, rows, model), BF)]
 
 
 def ticks(pieces, nt):
@@ -524,12 +556,14 @@
     ]
 
 
-def fore_kernel(
+def layer_kernel(
     nt, width,
     x, cot, gain_a, gain_f, segr, wq, wkt, wvt, wo, gate, up, down,
-    wqkv_f, wo_f, na_o, cf, qo, kvo, mo, lo, gall, cos, sin, act, branch, gh, gains, y, d_gate, d_up,
-    rowsbuf, hid, gate_v, up_v, down_v, part, sent, arrived, totals, landed, own_qkv, gain,
-    gain_sem, place_sem, out_sem, x_sem, cot_sem, nf_sem, br_sem, o_sem, gn_sem, y_sem, hs, hr, ps, pr,
+    y, gi, gain_out, d_wq, d_kv, d_wo, d_down, d_gate, d_up, wqkv_f, wo_f, na_f,
+    rowsbuf, cf, branch, act, hid, gate_v, up_v, down_v, part, sent, arrived, totals, landed, stage_v,
+    own_qkv, gain, gall, qo, kvo, mo, lo, cos, sin, gsum, zslots, dslots,
+    gain_sem, place_sem, out_sem, x_sem, cot_sem, nf_sem, br_sem, o_sem, gn_sem, y_sem, gi_sem,
+    hs, hr, ps, pr, zsem, dsem, ready, calm,
 ):
     me, t = lax.axis_index("dp"), lax.axis_index("tensor")
     nd = 1 << width
@@ -664,7 +698,7 @@
             if fills:
                 with jax.named_scope("x_fill"):
                     fills.pop(0)()
-        keep = pltpu.make_async_copy(na, na_o, out_sem.at[0])
+        keep = pltpu.make_async_copy(na, na_f, out_sem.at[0])
         keep.start()
         with jax.named_scope("wait_qkv"):
             load.wait()
@@ -680,9 +714,6 @@
             kvo[...] = keyed.astype(BF)
             pad_pair(keyed, kpad, vpad)
         pairs = queries // LANES
-        with jax.named_scope("g1"):
-            for stage in range(1, stages):
-                forward(g_gate, stage)
         with jax.named_scope("att"):
             attend_pairs(0, pairs, qo, kpad, vpad, bias, mo, lo)
         load_out.wait()
@@ -724,6 +755,8 @@
         for s in range(pieces):
             cots.step(1, s)
     with jax.named_scope("u0"):
+        for stage in range(1, stages):
+            forward(g_gate, stage)
         forward(g_up, 0)
     later = [
         lambda: ([cots.step(2, s) for s in range(pieces)], forward(g_down, 0)),
@@ -756,6 +789,49 @@
     for fill in later:
         fill()
 
+    def chunk_of(left, right):
+        def chunk(d):
+            return dot(left[:, pl.ds(pl.multiple_of(d * shard, shard), shard)], right[...], 0, 0)
+
+        return chunk
+
+    def cube(w, totals_, landed_, store):
+        return BlockScatter(
+            None, None, totals_, landed_, store, me, width, hs.at[w], hr.at[w], ps.at[w], pr.at[w]
+        )
+
+    def store_stage(at, value):
+        stage_v[at, :] = value
+
+    def store_down(at, value):
+        d_down[:, at] = value.T
+
+    def store_qkv(at, value):
+        d_wq[at, :] = value[:, :queries]
+        d_kv[:, at] = value[:, queries:].T
+
+    def store_wo(at, value):
+        d_wo[:, at] = value.T
+
+    for_qkv, for_wo = pl.ds(0, wide), pl.ds(wide, queries)
+    s_gate = cube(5, totals.at[0], landed.at[0], store_stage)
+    s_up = cube(6, totals.at[1], landed.at[1], store_stage)
+    s_down = cube(7, totals.at[0], landed.at[0], store_down)
+    s_qkv = cube(8, totals.at[1, :, :, for_qkv], landed.at[1, :, :, :, for_qkv], store_qkv)
+    s_out = cube(9, totals.at[1, :, :, for_wo], landed.at[1, :, :, :, for_wo], store_wo)
+
+    def take(s):
+        s.take()
+        s.send(0)
+
+    def on(s, stage):
+        s.add(stage)
+        if stage + 1 < stages:
+            s.send(stage + 1)
+
+    gsum[...] = jnp.zeros_like(gsum)
+    gather_br = LineGather(branch, natural, size, t, nt, br_sem)
+
     def feed(dg, du, given):
         cuts = tiles_of(hidden, 6)
         span = max(width_ for _, width_ in cuts)
@@ -794,8 +870,6 @@
                 )
 
         scatter_gn = LineScatter(part, shuffled, sent, arrived, t, nt, gn_sem)
-        gather_br = LineGather(branch, natural, size, t, nt, br_sem)
-        gains[...] = jnp.zeros_like(gains)
 
         def take_grad(s):
             at = scatter_gn.own(s)
@@ -804,40 +878,19 @@
 
             def store(cols, value):
                 total = cot[block_, cols].astype(F32) + value
-                gh[block_, cols] = total
+                gi[block_, cols] = total
                 branch[there, cols] = total.astype(BF)
 
             def store_gain(cols, value):
-                gains[1:2, cols] += value
+                gsum[1:2, cols] += value
 
             back_through_norm(
                 lambda c: hid[block_, c], lambda c: part[at, c], gall, 1, store, store_gain
             )
             gather_br.start(s)
 
-        def chunk_of(left, right):
-            def chunk(d):
-                return dot(left[:, pl.ds(pl.multiple_of(d * shard, shard), shard)], right[...], 0, 0)
-
-            return chunk
-
-        def keep(place):
-            def store(at, value):
-                part[place + at.start : place + at.stop, :hidden] = value
-
-            return store
-
-        s_gate, s_up = [
-            BlockScatter(
-                chunk_of(rowsbuf, grad), given, totals.at[w], landed.at[w], keep(w * shard), me, width,
-                hs.at[5 + w], hr.at[5 + w], ps.at[5 + w], pr.at[5 + w],
-            )
-            for w, grad in enumerate((dg, du))
-        ]
-
-        def take(s):
-            s.take()
-            s.send(0)
+        s_gate.chunk, s_up.chunk = chunk_of(rowsbuf, dg), chunk_of(rowsbuf, du)
+        s_gate.sent = s_up.sent = given
 
         with jax.named_scope("wait_ffn"):
             for w in (2, 3, 4):
@@ -886,77 +939,257 @@
                     fills.pop(0)()
         for k, s in steps[pieces]:
             gather_br.step(k, s)
-
+        scatter_gn.finish()
+        s_up.given()
+
+    pl.run_scoped(
+        feed,
+        pltpu.VMEM((tokens, hidden), BF),
+        pltpu.VMEM((tokens, hidden), BF),
+        pltpu.VMEM((nd // 2, shard, hidden), BF),
+    )
+
+    wo_v = down_v.at[pl.ds(0, queries), :]
+    na_v = down_v.at[pl.ds(queries, tokens), :]
+    wqkv_v = gate_v.at[:, pl.ds(0, wide)]
+    gm = up_v.at[pl.ds(0, tokens), pl.ds(0, queries)]
+    dqkv = up_v.at[pl.ds(tokens, tokens), pl.ds(0, wide)]
+
+    def rear(bias, kpad, vpad, dkey, dval, given):
+        scatter_y = LineScatter(part, shuffled, sent, arrived, t, nt, y_sem)
+        inward = LineScatter(part, natural, sent, arrived, t, nt, gi_sem)
         with jax.named_scope("down"):
-            scatter_gn.finish()
-            scatter_y = LineScatter(part, shuffled, sent, arrived, t, nt, y_sem)
             for start, width_ in tiles_of(model, 4):
                 cols = slice(start, start + width_)
                 part[:, cols] = dot(act[...], down_v[:, cols])
             for s in range(pieces):
                 scatter_y.edge(s)
-
-        def on(s, stage):
-            s.add(stage)
-            if stage + 1 < stages:
-                s.send(stage + 1)
-
-        rest = list(steps[pieces + 1 :])
-        fills = [functools.partial(on, s, stage) for stage in range(stages - 1) for s in (s_gate, s_up)]
-        for s in range(pieces):
-            with jax.named_scope("y_round"):
+        for g in (g_gate, g_up, g_down):
+            g.drain()
+        loads = [
+            pltpu.make_async_copy(wo_f, wo_v, place_sem.at[0]),
+            pltpu.make_async_copy(wqkv_f, wqkv_v, place_sem.at[1]),
+            pltpu.make_async_copy(na_f, na_v, place_sem.at[2]),
+        ]
+        for load in loads:
+            load.start()
+        bias_into(bias, segr)
+        pad_pair(kvo[...].astype(F32), kpad, vpad)
+        dkey[...] = jnp.zeros_like(dkey)
+        dval[...] = jnp.zeros_like(dval)
+        s_down.chunk, s_down.sent = chunk_of(cf, act), given
+        s_qkv.chunk, s_qkv.sent = chunk_of(na_v, dqkv), given.at[:, :, for_qkv]
+        s_out.chunk, s_out.sent = chunk_of(branch, mo), given.at[:, :, for_wo]
+
+        def pass_y(s):
+            with jax.named_scope("y_relay"):
                 scatter_y.relay(scatter_y.near, s)
                 scatter_y.relay(scatter_y.far, s)
+
+        def att(first, last):
+            with jax.named_scope("b_att"):
+                attend_back_pairs(
+                    first, last, qo, gm, mo, lo, kpad, vpad, bias, cos, sin, dqkv, dkey, dval
+                )
+
+        def free(s, out, slot):
+            s.add(stages - 1)
+            copy = pltpu.make_async_copy(stage_v, out, out_sem.at[1 + slot])
+            copy.start()
+            s.drain()
+            for bit in range(width):
+                pl.semaphore_signal(
+                    ready.at[slot], inc=1, device_id={"dp": flip(me, 1 << bit, width)},
+                    device_id_type=pl.DeviceIdType.MESH,
+                )
+            return copy
+
+        pairs = queries // LANES
+        rest = list(steps[pieces + 1 :])
+        jobs = [functools.partial(on, s, stage) for stage in range(stages - 1) for s in (s_gate, s_up)]
+        for s in range(pieces - 2):
+            pass_y(s)
             if rest:
                 with jax.named_scope("br_step"):
                     for k, s_ in rest.pop(0):
                         gather_br.step(k, s_)
-            if fills:
+            if jobs:
                 with jax.named_scope("y_fill"):
-                    fills.pop(0)()
-        with jax.named_scope("y_own"):
-            for late in rest:
+                    jobs.pop(0)()
+        for late in rest:
+            with jax.named_scope("br_step"):
                 for k, s_ in late:
                     gather_br.step(k, s_)
-            for fill in fills:
-                fill()
+        for job in jobs:
+            job()
+        with jax.named_scope("b_gm"):
+            loads[0].wait()
+            gm[...] = dot(branch[...], wo_v[...], 1, 1).astype(BF)
+        att(0, pairs // 2)
+        pass_y(pieces - 2)
+        with jax.named_scope("free0"):
+            copy_gate = free(s_gate, d_gate, 0)
+        att(pairs // 2, pairs)
+        pass_y(pieces - 1)
+        with jax.named_scope("b_give"):
+            pl.semaphore_wait(ready.at[0], width)
+            s_down.give()
+        key = dkey[0] + pltpu.roll(dkey[1], HD, 1)
+        value = pltpu.roll(dval[0], HD, 1) + dval[1]
+        key = key * cos[...] - swapped(key) * sin[...]
+        dqkv[:, queries : queries + LANES] = jnp.where(
+            lane_index(key.shape) < HD, key, value
+        ).astype(BF)
+        with jax.named_scope("y_own"):
             for s in range(pieces):
                 at = scatter_y.own(s)
                 block_ = slice(s * size, (s + 1) * size)
                 y[block_, :] = (hid[block_, :] + part[at, :model]).astype(BF)
+            scatter_y.finish()
+
+        @pl.when(t > 0)
+        def _():
+            pl.semaphore_signal(
+                calm.at[0], inc=1, device_id={"tensor": t - 1}, device_id_type=pl.DeviceIdType.MESH
+            )
+
+        @pl.when(t < nt - 1)
+        def _():
+            pl.semaphore_signal(
+                calm.at[0], inc=1, device_id={"tensor": t + 1}, device_id_type=pl.DeviceIdType.MESH
+            )
+
+        with jax.named_scope("b_part"):
+            loads[1].wait()
+            for start, width_ in tiles_of(model, 4):
+                part[:, start : start + width_] = dot(
+                    dqkv[...], wqkv_v[start : start + width_, :], 1, 1
+                )
+        with jax.named_scope("calm"):
+            pl.semaphore_wait(calm.at[0], lax.min(t, 1) + lax.min(nt - 1 - t, 1))
+            for s in range(pieces):
+                inward.edge(s)
+            loads[2].wait()
+
+        def take_grad(s):
+            at = inward.own(s)
+            block = slice(s * size, (s + 1) * size)
+
+            def store(cols, value):
+                gi[block, cols] += value
+
+            def store_gain(cols, value):
+                gsum[0:1, cols] += value
+
+            back_through_norm(
+                lambda c: x[block, c].astype(F32), lambda c: part[at, c], gall, 0, store, store_gain
+            )
+
+        copies = []
+
+        def free_up():
+            s_down.given()
+            copy_gate.wait()
+            copies.append(free(s_up, d_up, 1))
+
+        def give_small():
+            pl.semaphore_wait(ready.at[1], width)
+            s_qkv.give()
+
+        fills = [
+            give_small,
+            lambda: (take(s_qkv), s_out.give()),
+            lambda: take(s_out),
+        ]
+        fills += [
+            functools.partial(on, s, stage)
+            for stage in range(stages)
+            for s in (s_down, s_qkv, s_out)
+        ]
+        with jax.named_scope("b_take"):
+            take(s_down)
+        with jax.named_scope("free1"):
+            free_up()
+        for s in range(pieces):
+            with jax.named_scope("b_relay"):
+                inward.relay(inward.near, s)
+                inward.relay(inward.far, s)
+            with jax.named_scope("b_fill"):
+                fills.pop(0)()
+        with jax.named_scope("b_own"):
+            for s in range(pieces):
+                take_grad(s)
+                if s < pieces - 1 and fills:
+                    fills.pop(0)()
+        with jax.named_scope("b_gains"):
+            zslots[t] = gsum[...]
+
+            def along(step):
+                return remote(
+                    zslots.at[t], zslots.at[t], zsem.at[0, step], zsem.at[1, step],
+                    {"tensor": lax.rem(t + step, nt)},
+                )
+
+            for step in range(1, nt):
+                along(step).start()
+        with jax.named_scope("b_rest"):
+            for fill in fills:
+                fill()
+        with jax.named_scope("b_gains"):
+            for step in range(1, nt):
+                slot = zslots.at[lax.rem(t + nt - step, nt)]
+                remote(
+                    slot, slot, zsem.at[0, step], zsem.at[1, step], {"tensor": lax.rem(t + step, nt)}
+                ).wait_recv()
+            gsum[...] = sum(zslots[i] for i in range(nt))
+
+            def across(mask):
+                peer = flip(me, mask, width)
+                return remote(
+                    gsum.at[:, pl.ds(pl.multiple_of(peer * shard, shard), shard)], dslots.at[me],
+                    dsem.at[0, mask], dsem.at[1, mask], {"dp": peer},
+                )
+
+            for mask in range(1, nd):
+                across(mask).start()
+            dslots[me] = gsum[:, pl.ds(pl.multiple_of(me * shard, shard), shard)]
+            for mask in range(1, nd):
+                peer = flip(me, mask, width)
+                slot = dslots.at[peer]
+                remote(slot, slot, dsem.at[0, mask], dsem.at[1, mask], {"dp": peer}).wait_recv()
+            gain_out[...] = sum(dslots[i] for i in range(nd))
+            for step in range(1, nt):
+                along(step).wait_send()
+            for mask in range(1, nd):
+                across(mask).wait_send()
         with jax.named_scope("end"):
-            copies = []
-            for w, (s, out) in enumerate(((s_gate, d_gate), (s_up, d_up))):
-                s.add(stages - 1)
-                copies.append(
-                    pltpu.make_async_copy(
-                        part.at[pl.ds(w * shard, shard), pl.ds(0, hidden)], out, out_sem.at[1 + w]
-                    )
-                )
-                copies[-1].start()
-            s_up.given()
-            for s in (s_gate, s_up):
+            for s in (s_qkv, s_out):
+                s.given()
+            for s in (s_down, s_qkv, s_out):
                 s.drain()
-            gather_br.finish()
-            scatter_y.finish()
+            inward.finish()
             for copy in copies:
                 copy.wait()
 
     pl.run_scoped(
-        feed,
-        pltpu.VMEM((tokens, hidden), BF),
-        pltpu.VMEM((tokens, hidden), BF),
+        rear,
+        pltpu.VMEM((tokens, tokens), F32),
+        pltpu.VMEM((2, tokens, LANES), BF),
+        pltpu.VMEM((2, tokens, LANES), BF),
+        pltpu.VMEM((2, tokens, LANES), F32),
+        pltpu.VMEM((2, tokens, LANES), F32),
         pltpu.VMEM((nd // 2, shard, hidden), BF),
     )
-    for g in gathers:
+    for g in (g_qkv, g_out):
         g.drain()
     for mask in range(1, nd):
         gain_copy(mask).wait_send()
     cots.finish()
     gather_nf.finish()
-
-
-def fore(nt, nd, x, cot, gain_a, gain_f, segr, wq, wkt, wvt, wo, gate, up, down):
+    gather_br.finish()
+
+
+def layer(nt, nd, x, cot, gain_a, gain_f, segr, wq, wkt, wvt, wo, gate, up, down):
     width = nd.bit_length() - 1
     rows, model = x.shape
     tokens = nt * rows
@@ -968,32 +1201,29 @@
     span = max(width_ for _, width_ in tiles_of(hidden, 6))
     shape = jax.ShapeDtypeStruct
     outs = [
+        (shape((rows, model), BF), vmem()),
+        (shape((rows, model), F32), vmem()),
+        (shape((8, shard), F32), vmem()),
+        (shape((shard, queries), F32), vmem()),
+        (shape((LANES, shard), F32), vmem()),
+        (shape((queries, shard), F32), vmem()),
+        (shape((hidden, shard), F32), vmem()),
+        (shape((shard, hidden), F32), hbm()),
+        (shape((shard, hidden), F32), hbm()),
         (shape((model, wide), BF), hbm()),
         (shape((queries, model), BF), hbm()),
         (shape((tokens, model), BF), hbm()),
-        (shape((tokens, model), BF), vmem()),
-        (shape((tokens, queries), BF), vmem()),
-        (shape((tokens, LANES), BF), vmem()),
-        (shape((tokens, queries), BF), vmem()),
-        (shape((tokens, LANES), F32), vmem()),
-        (shape((nd, 8, shard), F32), vmem()),
-        (shape((tokens, LANES), F32), vmem()),
-        (shape((tokens, LANES), F32), vmem()),
-        (shape((tokens, hidden), BF), vmem()),
-        (shape((tokens, model), BF), vmem()),
-        (shape((rows, model), F32), vmem()),
-        (shape((8, model), F32), vmem()),
-        (shape((rows, model), BF), vmem()),
-        (shape((shard, hidden), F32), hbm()),
-        (shape((shard, hidden), F32), hbm()),
     ]
     return pl.pallas_call(
-        functools.partial(fore_kernel, nt, width),
+        functools.partial(layer_kernel, nt, width),
         out_shape=[o for o, _ in outs],
         in_specs=[vmem()] * 8 + [hbm()] * 4,
         out_specs=[s for _, s in outs],
         scratch_shapes=[
             pltpu.VMEM((tokens, model), BF),
+            pltpu.VMEM((tokens, model), BF),
+            pltpu.VMEM((tokens, model), BF),
+            pltpu.VMEM((tokens, hidden), BF),
             pltpu.VMEM((rows, model), F32),
             pltpu.VMEM((model, hidden), BF),
             pltpu.VMEM((model, hidden), BF),
@@ -1004,8 +1234,19 @@
         + [
             pltpu.VMEM((2, half, shard, hidden), BF),
             pltpu.VMEM((2, 2, half - 1, shard // 2, hidden), BF),
+            pltpu.VMEM((shard, hidden), F32),
             pltpu.VMEM((shard, wide), BF),
             pltpu.VMEM((8, shard), F32),
+            pltpu.VMEM((nd, 8, shard), F32),
+            pltpu.VMEM((tokens, queries), BF),
+            pltpu.VMEM((tokens, LANES), BF),
+            pltpu.VMEM((tokens, queries), BF),
+            pltpu.VMEM((tokens, LANES), F32),
+            pltpu.VMEM((tokens, LANES), F32),
+            pltpu.VMEM((tokens, LANES), F32),
+            pltpu.VMEM((8, model), F32),
+            pltpu.VMEM((nt, 8, model), F32),
+            pltpu.VMEM((nd, 8, shard), F32),
             dma(2, nd),
             dma(7),
             dma(3),
@@ -1016,296 +1257,21 @@
             dma(2, 2, nt, PIECES),
             dma(2, 2, nt, PIECES),
             dma(2, 2, nt, PIECES),
-            dma(7, 2, half),
-            dma(7, 2, half),
-            dma(7, half),
-            dma(7, half),
+            dma(2, 2, nt, PIECES),
+            dma(10, 2, half),
+            dma(10, 2, half),
+            dma(10, half),
+            dma(10, half),
+            dma(2, nt),
+            dma(2, nd),
+            pltpu.SemaphoreType.REGULAR((2,)),
+            pltpu.SemaphoreType.REGULAR((1,)),
         ],
         compiler_params=pltpu.CompilerParams(
             collective_id=0, has_side_effects=True, vmem_limit_bytes=VMEM_BYTES
         ),
-        name="fore",
+        name="layer",
     )(x, cot, gain_a, gain_f, segr, wq, wkt, wvt, wo, gate, up, down)
-
-
-def attend_back_pairs(first, last, qo, gm, mo, lo, kpad, vpad, bias, cos, sin, dqkv, dkey, dval):
-    rows = qo.shape[0]
-
-    @pl.loop(first, last)
-    def _(pair):
-        lanes = pl.ds(pl.multiple_of(pair * LANES, LANES), LANES)
-        for start, block, seen in query_cuts(rows):
-            at = slice(start, start + block)
-            lane = lane_index((block, LANES))
-            query, grad = qo[at, lanes], gm[at, lanes]
-            both = grad.astype(F32) * mo[at, lanes].astype(F32)
-            logs = lo[at, :]
-            dq = jnp.zeros((block, LANES), F32)
-            for side in range(2):
-                inside = (lane >= HD) if side else (lane < HD)
-                delta = jnp.sum(jnp.where(inside, both, 0.0), axis=-1, keepdims=True)
-                log = jnp.sum(
-                    jnp.where(lane == 2 * pair + side, logs, 0.0), axis=-1, keepdims=True
-                )
-                key, value = kpad[side, :seen, :], vpad[side, :seen, :]
-                probs = jnp.exp(dot(query, key, 1, 1) + bias[at, :seen] - log)
-                grad_scores = (probs * (dot(grad, value, 1, 1) - delta)).astype(BF)
-                dq = dq + dot(grad_scores, key)
-                dkey[side, :seen, :] += dot(grad_scores, query, 0, 0)
-                dval[side, :seen, :] += dot(probs.astype(BF), grad, 0, 0)
-            dq = dq * HD ** (-0.5)
-            dqkv[at, lanes] = (dq * cos[at, :] - swapped(dq) * sin[at, :]).astype(BF)
-
-
-def back_kernel(
-    nt, width,
-    branch, cf, act, mo, qo, kvo, lo, cos, sin, segr, x, gh, gparts, gall, na_f, wqkv_f, wo_f,
-    gi, gain_out, d_wq, d_kv, d_wo, d_down,
-    na, wqkv_v, wo_v, part, sent, arrived,
-    bias, kpad, vpad, gm, dqkv, dkey, dval,
-    given_d, totals_d, landed_d, given_q, totals_q, landed_q, given_o, totals_o, landed_o,
-    gsum, zslots, dslots,
-    load_sem, scatter_sem, zsem, dsem, hs, hr, ps, pr,
-):
-    me, t = lax.axis_index("dp"), lax.axis_index("tensor")
-    nd = 1 << width
-    rows, model = x.shape
-    tokens, queries = qo.shape
-    shard = model >> width
-    pieces = PIECES
-    size = rows // pieces
-    loads = [
-        pltpu.make_async_copy(wo_f, wo_v, load_sem.at[0]),
-        pltpu.make_async_copy(wqkv_f, wqkv_v, load_sem.at[1]),
-        pltpu.make_async_copy(na_f, na, load_sem.at[2]),
-    ]
-    for load in loads:
-        load.start()
-    bias_into(bias, segr)
-    pad_pair(kvo[...].astype(F32), kpad, vpad)
-    dkey[...] = jnp.zeros_like(dkey)
-    dval[...] = jnp.zeros_like(dval)
-    gsum[...] = gparts[...]
-    with jax.named_scope("b_enter"):
-        enter(t, nt, me, width, pltpu.get_barrier_semaphore(), everyone_along_tensor=True)
-
-    def chunk_of(left, right):
-        def chunk(d):
-            return dot(left[:, pl.ds(pl.multiple_of(d * shard, shard), shard)], right[...], 0, 0)
-
-        return chunk
-
-    def store_down(at, value):
-        d_down[:, at] = value.T
-
-    def store_qkv(at, value):
-        d_wq[at, :] = value[:, :queries]
-        d_kv[:, at] = value[:, queries:].T
-
-    def store_wo(at, value):
-        d_wo[:, at] = value.T
-
-    s_down, s_qkv, s_out = [
-        BlockScatter(
-            chunk_of(left, right), given, totals, landed, store, me, width,
-            hs.at[w], hr.at[w], ps.at[w], pr.at[w],
-        )
-        for w, (left, right, given, totals, landed, store) in enumerate(
-            (
-                (cf, act, given_d, totals_d, landed_d, store_down),
-                (na, dqkv, given_q, totals_q, landed_q, store_qkv),
-                (branch, mo, given_o, totals_o, landed_o, store_wo),
-            )
-        )
-    ]
-    stages = s_down.stages
-
-    with jax.named_scope("b_gm"):
-        loads[0].wait()
-        gm[...] = dot(branch[...], wo_v[...], 1, 1).astype(BF)
-    with jax.named_scope("b_give"):
-        s_down.give()
-    with jax.named_scope("b_att"):
-        attend_back_pairs(
-            0, queries // LANES, qo, gm, mo, lo, kpad, vpad, bias, cos, sin, dqkv, dkey, dval
-        )
-        key = dkey[0] + pltpu.roll(dkey[1], HD, 1)
-        value = pltpu.roll(dval[0], HD, 1) + dval[1]
-        key = key * cos[...] - swapped(key) * sin[...]
-        dqkv[:, queries : queries + LANES] = jnp.where(
-            lane_index(key.shape) < HD, key, value
-        ).astype(BF)
-
-    inward = LineScatter(
-        part, lambda j, s: j * rows + s * size, sent, arrived, t, nt, scatter_sem
-    )
-    with jax.named_scope("b_part"):
-        loads[1].wait()
-        for start, width_ in tiles_of(model, 4):
-            part[:, start : start + width_] = dot(dqkv[...], wqkv_v[start : start + width_, :], 1, 1)
-        for s in range(pieces):
-            inward.edge(s)
-        loads[2].wait()
-
-    def take(s):
-        s.take()
-        s.send(0)
-
-    def on(s, stage):
-        s.add(stage)
-        if stage + 1 < stages:
-            s.send(stage + 1)
-
-    def take_grad(s):
-        at = inward.own(s)
-        block = slice(s * size, (s + 1) * size)
-
-        def store(cols, value):
-            gi[block, cols] = gh[block, cols] + value
-
-        def store_gain(cols, value):
-            gsum[0:1, cols] += value
-
-        back_through_norm(
-            lambda c: x[block, c].astype(F32), lambda c: part[at, c], gall, 0, store, store_gain
-        )
-
-    fills = [
-        lambda: s_qkv.give(),
-        lambda: (take(s_qkv), s_out.give()),
-        lambda: take(s_out),
-    ]
-    fills += [functools.partial(on, s, stage) for stage in range(stages) for s in (s_down, s_qkv, s_out)]
-    with jax.named_scope("b_take"):
-        take(s_down)
-    for s in range(pieces):
-        with jax.named_scope("b_round"):
-            inward.relay(inward.near, s)
-            inward.relay(inward.far, s)
-        with jax.named_scope("b_fill"):
-            if fills:
-                fills.pop(0)()
-    with jax.named_scope("b_own"):
-        for s in range(pieces):
-            take_grad(s)
-            if fills and s < pieces - 1:
-                fills.pop(0)()
-
-    with jax.named_scope("b_gains"):
-        zslots[t] = gsum[...]
-
-        def along(step):
-            return remote(
-                zslots.at[t], zslots.at[t], zsem.at[0, step], zsem.at[1, step],
-                {"tensor": lax.rem(t + step, nt)},
-            )
-
-        for step in range(1, nt):
-            along(step).start()
-    with jax.named_scope("b_rest"):
-        for fill in fills:
-            fill()
-    with jax.named_scope("b_gains"):
-        for step in range(1, nt):
-            slot = zslots.at[lax.rem(t + nt - step, nt)]
-            remote(
-                slot, slot, zsem.at[0, step], zsem.at[1, step], {"tensor": lax.rem(t + step, nt)}
-            ).wait_recv()
-        gsum[...] = sum(zslots[i] for i in range(nt))
-
-        def across(mask):
-            peer = flip(me, mask, width)
-            return remote(
-                gsum.at[:, pl.ds(pl.multiple_of(peer * shard, shard), shard)], dslots.at[me],
-                dsem.at[0, mask], dsem.at[1, mask], {"dp": peer},
-            )
-
-        for mask in range(1, nd):
-            across(mask).start()
-        dslots[me] = gsum[:, pl.ds(pl.multiple_of(me * shard, shard), shard)]
-        for mask in range(1, nd):
-            peer = flip(me, mask, width)
-            slot = dslots.at[peer]
-            remote(slot, slot, dsem.at[0, mask], dsem.at[1, mask], {"dp": peer}).wait_recv()
-        gain_out[...] = sum(dslots[i] for i in range(nd))
-
-    for step in range(1, nt):
-        along(step).wait_send()
-    for mask in range(1, nd):
-        across(mask).wait_send()
-    for s in (s_down, s_qkv, s_out):
-        s.given()
-        s.drain()
-    inward.finish()
-
-
-def back(nt, nd, branch, cf, act, mo, qo, kvo, lo, cos, sin, segr, x, gh, gparts, gall, na, wqkv_f, wo_f):
-    width = nd.bit_length() - 1
-    rows, model = x.shape
-    tokens, queries = qo.shape
-    hidden = act.shape[1]
-    wide = wqkv_f.shape[1]
-    shard = model // nd
-    half = nd // 2
-    shape = jax.ShapeDtypeStruct
-    outs = [
-        shape((rows, model), F32),
-        shape((8, shard), F32),
-        shape((shard, queries), F32),
-        shape((LANES, shard), F32),
-        shape((queries, shard), F32),
-        shape((hidden, shard), F32),
-    ]
-
-    def cube(size):
-        return [
-            pltpu.VMEM((half, shard, size), BF),
-            pltpu.VMEM((half, shard, size), BF),
-            pltpu.VMEM((2, half - 1, shard // 2, size), BF),
-        ]
-
-    return pl.pallas_call(
-        functools.partial(back_kernel, nt, width),
-        out_shape=outs,
-        in_specs=[vmem()] * 14 + [hbm()] * 3,
-        out_specs=[vmem()] * len(outs),
-        scratch_shapes=[
-            pltpu.VMEM((tokens, model), BF),
-            pltpu.VMEM((model, wide), BF),
-            pltpu.VMEM((queries, model), BF),
-            pltpu.VMEM((tokens, model), F32),
-        ]
-        + line_scratch(nt, rows, model)
-        + [
-            pltpu.VMEM((tokens, tokens), F32),
-            pltpu.VMEM((2, tokens, LANES), BF),
-            pltpu.VMEM((2, tokens, LANES), BF),
-            pltpu.VMEM((tokens, queries), BF),
-            pltpu.VMEM((tokens, wide), BF),
-            pltpu.VMEM((2, tokens, LANES), F32),
-            pltpu.VMEM((2, tokens, LANES), F32),
-        ]
-        + cube(hidden)
-        + cube(wide)
-        + cube(queries)
-        + [
-            pltpu.VMEM((8, model), F32),
-            pltpu.VMEM((nt, 8, model), F32),
-            pltpu.VMEM((nd, 8, shard), F32),
-            dma(3),
-            dma(2, 2, nt, PIECES),
-            dma(2, nt),
-            dma(2, nd),
-            dma(3, 2, half),
-            dma(3, 2, half),
-            dma(3, half),
-            dma(3, half),
-        ],
-        compiler_params=pltpu.CompilerParams(
-            collective_id=1, has_side_effects=True, vmem_limit_bytes=VMEM_BYTES
-        ),
-        name="back",
-    )(branch, cf, act, mo, qo, kvo, lo, cos, sin, segr, x, gh, gparts, gall, na, wqkv_f, wo_f)
 
 
 def narrow_scatter(value, axis, scatter_dimension, tiled):
@@ -1591,14 +1557,9 @@
 
 
 def with_kernels(nt, nd, layer_input, segment_ids, norm_attn, w_query, w_key, w_value, w_output, norm_ffn, w_gate, w_up, w_down, cotangent):
-    segr = segment_ids[None, :]
-    (wqkv_f, wo_f, na, cf, qo, kvo, mo, lo, gall, cos, sin, act, branch, gh, gparts, y, d_gate, d_up) = fore(
-        nt, nd, layer_input, cotangent, norm_attn[None, :], norm_ffn[None, :], segr,
+    y, gi, gains, d_wq, d_kv, d_wo, d_down, d_gate, d_up, *_ = layer(
+        nt, nd, layer_input, cotangent, norm_attn[None, :], norm_ffn[None, :], segment_ids[None, :],
         w_query, w_key.T, w_value.T, w_output, w_gate, w_up, w_down,
-    )
-    gi, gains, d_wq, d_kv, d_wo, d_down = back(
-        nt, nd, branch, cf, act, mo, qo, kvo, lo, cos, sin, segr, layer_input, gh, gparts, gall,
-        na, wqkv_f, wo_f,
     )
     k = w_key.shape[1]
     return (

time: 342 us -> 317 us (0.927)
  Pallas kernels: 321 us -> 295 us
    pallas_call x2 -> x1, Pallas kernels: 321 us -> 295 us  [layer(): pl.pallas_call(functools.partial(layer_kernel, nt, width), out_shape=[o f...]
    unnamed x21 -> x19, local copies, waits for them, and re-layouts: 8.23 us -> 9.37 us
where the time goes in v3:
time: 317 us; the launch traced here: 311 us
  Pallas kernels  295 us (93%)
  local copies, waits for them, and re-layouts  14.7 us (5%)
    pallas_call x1, Pallas kernels, layer(): pl.pallas_call(functools.partial(layer_kernel, nt, width), out_shape=[o f...  295 us
    unnamed x19, local copies, waits for them, and re-layouts  9.37 us

profile of v3, /device:TPU:0, one launch (start us, length us, event | category | flops | bytes accessed | tf_op | source)
XLA Modules:
  0.0 310.9 jit_solution(3196157183559193852)
XLA Ops:
  0.6 1.2 broadcast_in_dim.9.gain_a
  1.9 1.2 broadcast_in_dim.10.gain_f
  3.1 295.0 %layer.1 = (bf16[128,2048]{1,0:T(8,128)(2,1)}, f32[128,2048]{1,0:T(8,128)}, f32[8,256]{1,0:T(8,128)}, f32[256,512]{1,0:T(8,128)}, f32[128,256]{1,0:T(8,128)}, /*...) custom-call(bf16[128,2048]{1,0:T(8,128)(2,1)} %x.1, ...), custom_call_target="tpu_custom_call" | custom-call | tf_op jit(solution)/shard_map/layer/pallas_call | solution.py:1217
  298.1 0.0 copy-start.3
  298.1 1.4 fusion
  299.5 1.5 slice_bitcast_fusion
  301.0 0.0 copy-start.5
  301.0 1.9 copy.30
  303.0 0.0 copy-done.3
  303.0 0.0 copy-start.4
  303.0 1.0 copy.31
  304.0 0.0 copy-done.5
  304.0 0.0 copy-start.2
  304.0 0.8 copy.32
  304.8 0.0 copy-done.4
  304.8 0.8 copy.33
  305.6 0.0 copy-done.2
  305.6 0.0 copy-start.1
  305.6 1.1 copy.34
  306.7 0.8 copy-done.1
  307.4 0.0 copy-start
  307.4 1.1 copy.35
  308.5 0.8 copy-done
  309.3 1.1 copy.36
Async XLA Ops:
  298.1 4.9 %copy-start.3 = (f32[128,2048]{1,0:T(8,128)S(1)}, f32[128,2048]{1,0:T(8,128)}, u32[]{:S(2)}) copy-start(f32[128,2048]{1,0:T(8,128)} %get-tuple-element.45) | copy-start | bytes 3145732
  301.0 2.9 copy-start.5
  303.0 1.8 copy-start.4
  304.0 1.6 copy-start.2
  305.6 1.9 copy-start.1
  307.4 1.9 copy-start
